TPU v7x, 256 devices: a whole 4x4x8 slice. The times are simulated.
256 devices in a mesh: img: 8 (over y, core), tile: 32 (over z, x).
Axes of the slice: x: 4, y: 4, z: 8, core: 2. Of those that a mesh axis runs over, the one named last changes fastest.
Arguments:
- means: float32 [3, 524288], P(None, ('img', 'tile')), may hold values from -3 to 3
- log_scales: float32 [3, 524288], P(None, ('img', 'tile')), may hold values from -6 to -3
- quat_w: float32 [1, 524288], P(None, ('img', 'tile')), may hold values from 1 to 2
- quat_v: float32 [3, 524288], P(None, ('img', 'tile')), may hold values from -1 to 1
- opacity: float32 [1, 524288], P(None, ('img', 'tile')), may hold values from -6 to 6
- sh_coeffs: float32 [48, 524288], P(None, ('img', 'tile')), may hold values from -3 to 3
- cameras: float32 [8, 10], replicated, may hold values from -300 to 300
- requests: int32 [8, 32, 8, 32, 16], P('img', 'tile'), may hold values from 0 to 2047, as said below
- lists: int32 [8, 256, 256], P('img', 'tile'), may hold values from 0 to 4095, as said below
- counts: int32 [8, 256], P('img', 'tile'), may hold values from 1 to 256
- image_cot: float32 [8, 3, 256, 256], P('img', None, 'tile'), may hold values from -6 to 6
Outputs:
- rendered: float32 [8, 3, 256, 256], P('img', None, 'tile')
- param_grad: float32 [59, 524288], P(None, ('img', 'tile'))
- camera_grad: float32 [8, 10], replicated
Inputs may be any that keep to these rules, and one draw needn't show every extreme that they name: Entries may repeat within a device's requests. `lists`: each entry names a request slot of the device that renders the tile; slot (a * 32 + b) * 16 + c is requests[i, t, a, b, c]; only the first counts entries of a list are live.
All inputs are finite; a program needn't handle non-finite values.
Results may differ from a plain program's by a relative error of at most 0.0003.
Values sent between devices are 32-bit elements; how exact they have to be, the bound alone decides.
No kernel may reach another device: no remote copies, remote signals or barrier semaphores. Data moves between devices by JAX's collectives and lax.ppermute only.
A program may use at most 64 MiB of HBM per device.

v0:
```python
import jax
import jax.numpy as jnp
from jax import lax
from jax.sharding import Mesh
from jax.sharding import PartitionSpec as P

TILE_SIDE = 16
TW = 16
TILE = ("tile_0", "tile_1")
IMG_TILE = ("img_0", "img_1", "tile_0", "tile_1")
IMG = ("img_0", "img_1")


sh_first = 0.28209479177387814
sh_second = 0.4886025119029199
sh_third = (
    1.0925484305920792,
    -1.0925484305920792,
    0.31539156525252005,
    -1.0925484305920792,
    0.5462742152960396,
)
sh_fourth = (
    -0.5900435899266435,
    2.890611442640554,
    -0.4570457994644658,
    0.3731763325901154,
    -0.4570457994644658,
    1.445305721320277,
    -0.5900435899266435,
)
dilation = 0.3


def in_blocks(array, dim, count):
    shape = array.shape
    blocks = array.reshape(*shape[:dim], count, shape[dim] // count, *shape[dim + 1 :])
    return jnp.moveaxis(blocks, dim, 0)


def joined_along(blocks, dim):
    shape = list(blocks.shape[1:])
    shape[dim] *= blocks.shape[0]
    return jnp.moveaxis(blocks, 0, dim).reshape(shape)


def one_exchange(array, axis, axes, splits, concats):
    sizes = [lax.axis_size(a) for a in axes]
    blocks = in_blocks(array, splits[0], sizes[0])
    blocks = jnp.moveaxis(in_blocks(blocks, splits[1] + 1, sizes[1]), 0, 1)
    inside = blocks.shape[2:]
    blocks = blocks.reshape(-1, *inside)
    blocks = lax.all_to_all(blocks, axis, split_axis=0, concat_axis=0, tiled=True)
    blocks = joined_along(blocks.reshape(*sizes, *inside), concats[0] + 1)
    return joined_along(blocks, concats[1])


def over_axes(array, axes):
    for axis in axes:
        array = lax.psum(array, axis)
    return array


def harmonic_values(camera):
    polar_angle = camera[8]
    azimuth = camera[9]
    view_x = jnp.sin(polar_angle) * jnp.cos(azimuth)
    view_y = jnp.sin(polar_angle) * jnp.sin(azimuth)
    view_z = jnp.cos(polar_angle)
    square_x = view_x * view_x
    square_y = view_y * view_y
    square_z = view_z * view_z
    return jnp.stack(
        [
            sh_first + 0.0 * view_x,
            -sh_second * view_y,
            sh_second * view_z,
            -sh_second * view_x,
            sh_third[0] * view_x * view_y,
            sh_third[1] * view_y * view_z,
            sh_third[2] * (2.0 * square_z - square_x - square_y),
            sh_third[3] * view_x * view_z,
            sh_third[4] * (square_x - square_y),
            sh_fourth[0] * view_y * (3.0 * square_x - square_y),
            sh_fourth[1] * view_x * view_y * view_z,
            sh_fourth[2] * view_y * (4.0 * square_z - square_x - square_y),
            sh_fourth[3] * view_z * (2.0 * square_z - 3.0 * square_x - 3.0 * square_y),
            sh_fourth[4] * view_x * (4.0 * square_z - square_x - square_y),
            sh_fourth[5] * view_z * (square_x - square_y),
            sh_fourth[6] * view_x * (square_x - 3.0 * square_y),
        ]
    )


def project(params, camera):
    trailing = params.shape[1:]
    mean_x, mean_y, mean_z = (params[0], params[1], params[2])
    screen_x = camera[0] * mean_x + camera[1] * mean_y + camera[2] * mean_z + camera[6]
    screen_y = camera[3] * mean_x + camera[4] * mean_y + camera[5] * mean_z + camera[7]
    quat_norm = jnp.sqrt(
        params[6] * params[6]
        + params[7] * params[7]
        + params[8] * params[8]
        + params[9] * params[9]
    )
    unit_w = params[6] / quat_norm
    unit_x = params[7] / quat_norm
    unit_y = params[8] / quat_norm
    unit_z = params[9] / quat_norm
    rotation = (
        (
            1.0 - 2.0 * (unit_y * unit_y + unit_z * unit_z),
            2.0 * (unit_x * unit_y - unit_w * unit_z),
            2.0 * (unit_x * unit_z + unit_w * unit_y),
        ),
        (
            2.0 * (unit_x * unit_y + unit_w * unit_z),
            1.0 - 2.0 * (unit_x * unit_x + unit_z * unit_z),
            2.0 * (unit_y * unit_z - unit_w * unit_x),
        ),
        (
            2.0 * (unit_x * unit_z - unit_w * unit_y),
            2.0 * (unit_y * unit_z + unit_w * unit_x),
            1.0 - 2.0 * (unit_x * unit_x + unit_y * unit_y),
        ),
    )
    stretch = (jnp.exp(params[3]), jnp.exp(params[4]), jnp.exp(params[5]))

    def image_row(first_coef, second_coef, third_coef):
        return [
            (
                first_coef * rotation[0][col_idx]
                + second_coef * rotation[1][col_idx]
                + third_coef * rotation[2][col_idx]
            )
            * stretch[col_idx]
            for col_idx in range(3)
        ]

    upper_row = image_row(camera[0], camera[1], camera[2])
    lower_row = image_row(camera[3], camera[4], camera[5])
    cov_xx = (
        upper_row[0] * upper_row[0]
        + upper_row[1] * upper_row[1]
        + upper_row[2] * upper_row[2]
        + dilation
    )
    cov_xy = upper_row[0] * lower_row[0] + upper_row[1] * lower_row[1] + upper_row[2] * lower_row[2]
    cov_yy = (
        lower_row[0] * lower_row[0]
        + lower_row[1] * lower_row[1]
        + lower_row[2] * lower_row[2]
        + dilation
    )
    determinant = cov_xx * cov_yy - cov_xy * cov_xy
    base_opacity = jax.nn.sigmoid(params[10])
    harmonics = harmonic_values(camera).reshape((1, 16) + (1,) * len(trailing))
    coeffs = params[11:59].reshape((3, 16) + trailing)
    colours = 0.5 + jnp.sum(coeffs * harmonics, axis=1)
    return jnp.stack(
        [
            screen_x,
            screen_y,
            cov_yy / determinant,
            -cov_xy / determinant,
            cov_xx / determinant,
            base_opacity,
            colours[0],
            colours[1],
            colours[2],
        ],
        axis=0,
    )


def render_tile(features, live_count, tile_number, height):
    entries = features.shape[1]
    pixel = jnp.arange(TILE_SIDE * TILE_SIDE, dtype=jnp.int32)
    tile_col = tile_number % TW
    tile_row = tile_number // TW
    pixel_x = (
        (TILE_SIDE * tile_col + pixel % TILE_SIDE).astype(jnp.float32) + 0.5 - 0.5 * TILE_SIDE * TW
    )
    pixel_y = (TILE_SIDE * tile_row + pixel // TILE_SIDE).astype(jnp.float32) + 0.5 - 0.5 * height
    delta_x = pixel_x[:, None] - features[0][None, :]
    delta_y = pixel_y[:, None] - features[1][None, :]
    power = (
        -0.5 * (features[2][None, :] * delta_x * delta_x + features[4][None, :] * delta_y * delta_y)
        - features[3][None, :] * delta_x * delta_y
    )
    live = jnp.arange(entries, dtype=jnp.int32) < live_count
    alpha = jnp.where(live[None, :], features[5][None, :] * jnp.exp(power), jnp.float32(0.0))
    log_keep = jnp.log1p(-alpha)
    positions = jnp.arange(entries, dtype=jnp.int32)
    strict_upper = (positions[:, None] < positions[None, :]).astype(jnp.float32)
    log_before = jnp.dot(log_keep, strict_upper, precision=lax.Precision.HIGHEST)
    weights = alpha * jnp.exp(log_before)
    return jnp.einsum("ce,pe->cp", features[6:9], weights, precision=lax.Precision.HIGHEST)


def local(
    means,
    log_scales,
    quat_w,
    quat_v,
    opacity,
    sh_coeffs,
    cameras,
    requests,
    lists,
    counts,
    image_cot,
):
    tile_count = lax.axis_size(TILE)
    my_tile = lax.axis_index(TILE)
    owned = jnp.concatenate([means, log_scales, quat_w, quat_v, opacity, sh_coeffs], axis=0)
    wanted = requests.reshape(requests.shape[2:])
    asked = one_exchange(wanted, IMG_TILE, (IMG, TILE), (0, 1), (0, 1))
    picked = owned[:, asked]
    tiles_here = lists.shape[1]
    height = TILE_SIDE * tiles_here * tile_count / TW
    numbers = my_tile * tiles_here + jnp.arange(tiles_here, dtype=jnp.int32)
    slot_lists = lists[0]
    live_counts = counts[0]
    cotangent = image_cot[0]

    def render_packed(packed):
        return render_tile(packed[0], packed[1], packed[2], height)

    def render_all(slot_features):
        tile_features = slot_features[:, slot_lists].transpose(1, 0, 2)
        images = lax.map(jax.checkpoint(render_packed), (tile_features, live_counts, numbers))
        return images.transpose(1, 0, 2)

    def project_sources(picked_rows, all_cameras):
        return jax.vmap(project, in_axes=(1, 0), out_axes=1)(picked_rows, all_cameras)

    projected, pull_owner = jax.vjp(project_sources, picked, cameras)
    arrived = one_exchange(projected, IMG_TILE, (IMG, TILE), (1, 2), (1, 2))
    slot_features = arrived.reshape(arrived.shape[0], -1)
    rendered, pull_render = jax.vjp(render_all, slot_features)
    slot_grads = pull_render(cotangent)[0]
    returned = one_exchange(
        slot_grads.reshape(arrived.shape), IMG_TILE, (IMG, TILE), (1, 2), (1, 2)
    )
    picked_grads, camera_terms = pull_owner(returned)
    param_grad = (
        jnp.zeros_like(owned).at[:, asked.reshape(-1)].add(picked_grads.reshape(owned.shape[0], -1))
    )
    camera_grad = over_axes(camera_terms, IMG_TILE)
    return (rendered[None], param_grad, camera_grad)


def solution(mesh):
    finer = Mesh(mesh.devices.reshape(4, 2, 8, 4), ("img_0", "img_1", "tile_0", "tile_1"))
    return jax.shard_map(
        local,
        mesh=finer,
        in_specs=(
            P(None, IMG_TILE),
            P(None, IMG_TILE),
            P(None, IMG_TILE),
            P(None, IMG_TILE),
            P(None, IMG_TILE),
            P(None, IMG_TILE),
            P(),
            P(IMG, TILE, None, None, None),
            P(IMG, TILE, None),
            P(IMG, TILE),
            P(IMG, None, TILE, None),
        ),
        out_specs=(P(IMG, None, TILE, None), P(None, IMG_TILE), P()),
        check_vma=False,
    )
```

profile of v0, /device:TPU:1, one launch (start us, length us, event | category | flops | bytes accessed | tf_op | source)
XLA Modules:
  0.0 381.3 jit_solution(5063203595928172959)
XLA Ops:
  0.7 1.6 copy.430
  2.3 15.6 %all-to-all-start = ((s32[256,1,1,16]{3,2,1,0:T(1,128)}), s32[256,1,1,16]{3,2,1,0:T(1,128)S(1)}, u32[]{:S(2)}, u32[]{:S(2)}) async-start(s32[256,1,1,16]{3,2,1,0:T(1,128)} %bitcast.17), calls=%async_computation | async-start | bytes 262144 | tf_op jit(solution)/shard_map/all_to_all | solution.py:53
  18.0 1.9 slice_reduce_fusion.15
  27.4 2.1 copy.372
  34.9 3.8 %concatenate.3 = f32[59,2048]{0,1:T(8,128)S(1)} concatenate(f32[3,2048]{0,1:T(8,128)S(1)} %copy.370, f32[3,2048]{0,1:T(8,128)S(1)} %copy.371, f32[1,2048]{0,1:T(8,128)} %copy.372, f32[3,2048]{0,1:T(8,128)} %copy.373, f32[1,2048]{0,1:T(8,128)} %copy.374, f32[48,2048]{0,1:T(8,128)} %copy.375), dimensions={0} | concatenate | bytes 966656 | tf_op jit(solution)/shard_map/concatenate | solution.py:216
  39.6 10.8 %gather_fusion = f32[4096,59]{1,0:T(8,128)S(1)} fusion(f32[59,2048]{0,1:T(8,128)S(1)} %concatenate.3, s32[4096]{0:T(1024)S(1)} %broadcast_clamp_fusion), kind=kCustom, calls=%fused_computation | custom fusion | bytes 1949696 | tf_op jit(solution)/shard_map/gather | solution.py:219
  50.3 4.4 %copy.378 = f32[8,32,16,59]{1,2,0,3:T(8,128)} copy(f32[8,32,16,59]{3,2,1,0:T(8,128)S(1)} %bitcast.690) | data formatting | bytes 1933312 | tf_op jit(solution)/shard_map/gather | solution.py:219
  54.8 2.2 slice_bitcast_fusion
  60.2 2.1 divide_dynamic-update-slice_fusion.2
  66.2 1.6 reshape.1202
  67.8 13.7 %all-to-all-start.1 = ((f32[256,1,144]{2,1,0:T(1,128)}), f32[256,1,144]{2,1,0:T(1,128)S(1)}, u32[]{:S(2)}, u32[]{:S(2)}) async-start(f32[256,1,144]{2,1,0:T(1,128)} %reshape.1202), calls=%async_computation.1 | async-start | bytes 524288 | tf_op jit(solution)/shard_map/all_to_all | solution.py:53
  82.2 1.6 bitcast_divide_fusion.3
  83.8 1.6 bitcast_divide_fusion.6
  85.5 10.8 %all-to-all-done.1 = f32[256,1,144]{2,1,0:T(1,128)S(1)} async-done(((f32[256,1,144]{2,1,0:T(1,128)}), f32[256,1,144]{2,1,0:T(1,128)S(1)}, u32[]{:S(2)}, u32[]{:S(2)}) %all-to-all-start.1) | async-done | bytes 147488 | tf_op jit(solution)/shard_map/all_to_all | solution.py:53
  98.7 1.9 copy.413
  100.6 6.4 %gather_fusion.1 = f32[2048,9]{1,0:T(8,128)S(1)} fusion(f32[9,4096]{0,1:T(8,128)S(1)} %bitcast.716, s32[2048]{0:T(1024)} %broadcast_clamp_fusion.1), kind=kCustom, calls=%fused_computation.1 | custom fusion | bytes 155648 | tf_op jit(solution)/shard_map/jvp()/gather | solution.py:231
  107.4 68.9 %while.32 = (s32[]{:T(128)}, f32[8,9,256]{2,1,0:T(8,128)S(1)}, f32[8,9,256]{2,1,0:T(8,128)S(1)}, s32[8]{0:T(128)}, s32[8]{0:T(128)}, /*index=5*/f32[8,3,256]{2,1...) while((s32[]{:T(128)}, f32[8,9,256]{2,1,0:T(8,128)S(1)}, ...), condition=%wide.region_10.11_spmd, body=%wide.region_3.10_spmd.sunk | while | flops 413418752 | bytes 1426828 | solution.py:232
  176.9 12.1 %scatter_custom_fusion = f32[9,4096]{0,1:T(8,128)S(1)} fusion(s32[2048]{0:T(1024)} %bitcast.734, f32[2048,9]{1,0:T(8,128)S(1)} %bitcast.722, f32[]{:T(128)} %constant.357.clone.1), kind=kCustom, calls=%fused_computation.147 | custom fusion | flops 18432 | bytes 147968 | tf_op jit(solution)/shard_map/transpose(jvp())/scatter-add | solution.py:231
  189.0 2.0 copy.419
  191.0 3.6 reduce.56
  194.6 1.6 reshape.1204
  196.2 6.4 %all-to-all-start.2 = ((f32[256,1,144]{2,1,0:T(1,128)}), f32[256,1,144]{2,1,0:T(1,128)S(1)}, u32[]{:S(2)}, u32[]{:S(2)}) async-start(f32[256,1,144]{2,1,0:T(1,128)} %reshape.1204), calls=%async_computation.2 | async-start | bytes 524288 | tf_op jit(solution)/shard_map/all_to_all | solution.py:53
  202.6 80.2 %while.33 = (s32[]{:T(128)}, f32[8,3,256]{2,0,1:T(8,128)}, f32[8,9,256]{2,1,0:T(8,128)}, s32[8]{0:T(128)}, s32[8]{0:T(128)}, /*index=5*/s32[]{:T(128)}, s32[]{:T...) while((s32[]{:T(128)}, f32[8,3,256]{2,0,1:T(8,128)}, ...), condition=%wide.region_2.3_spmd.clone, body=%wide.region_1.2_spmd.clone.sunk | while | flops 205656864 | bytes 567804 | solution.py:232
  288.7 3.5 multiply_reduce_fusion.1
  294.8 1.5 fusion.105
  301.9 9.5 %psum.28 = f32[8,10]{0,1:T(8,128)} all-reduce(f32[8,10]{0,1:T(8,128)} %pad_add_fusion.1), channel_id=1, replica_groups=mesh['img_0'=4,'img_1'=2,'tile_0'=8,'tile_1'=4] {'img_0'}, use_global_device_ids=true, to_apply=%region_41.42 | all-reduce | flops 80 | bytes 640 | tf_op jit(solution)/shard_map/psum | solution.py:60
  311.5 5.2 %psum.29 = f32[8,10]{0,1:T(8,128)} all-reduce(f32[8,10]{0,1:T(8,128)} %psum.28), channel_id=1, replica_groups=mesh['img_0'=4,'img_1'=2,'tile_0'=8,'tile_1'=4] {'img_1'}, use_global_device_ids=true, to_apply=%region_42.43 | all-reduce | flops 80 | bytes 640 | tf_op jit(solution)/shard_map/psum | solution.py:60
  316.7 15.9 %psum.30 = f32[8,10]{0,1:T(8,128)} all-reduce(f32[8,10]{0,1:T(8,128)} %psum.29), channel_id=1, replica_groups=mesh['img_0'=4,'img_1'=2,'tile_0'=8,'tile_1'=4] {'tile_0'}, use_global_device_ids=true, to_apply=%region_43.44 | all-reduce | flops 80 | bytes 640 | tf_op jit(solution)/shard_map/psum | solution.py:60
  332.6 9.5 %psum.31 = f32[8,10]{0,1:T(8,128)} all-reduce(f32[8,10]{0,1:T(8,128)} %psum.30), channel_id=1, replica_groups=mesh['img_0'=4,'img_1'=2,'tile_0'=8,'tile_1'=4] {'tile_1'}, use_global_device_ids=true, to_apply=%region_44.45 | all-reduce | flops 80 | bytes 640 | tf_op jit(solution)/shard_map/psum | solution.py:60
  350.6 2.6 fusion.92
  353.1 4.2 %copy.425 = f32[59,8,32,16]{0,3,2,1:T(8,128)S(1)} copy(f32[59,8,32,16]{2,3,1,0:T(8,128)} %fusion.92) | data formatting | bytes 1933312 | tf_op jit(solution)/shard_map/transpose(jvp(vmap()))/add_any | solution.py:97
  357.4 22.7 %scatter_custom_fusion.1 = f32[59,2048]{0,1:T(8,128)S(1)} fusion(s32[4096]{0:T(1024)} %bitcast.763, f32[4096,59]{1,0:T(8,128)S(1)} %bitcast.717, f32[]{:T(128)} %constant.357.clone.1), kind=kCustom, calls=%fused_computation.150 | custom fusion | flops 241664 | bytes 483840 | tf_op jit(solution)/shard_map/scatter-add | solution.py:248
  (375 shorter events, 153.2 us)
Async XLA Ops:
  0.6 28.8 %copy-start.25 = (f32[3,2048]{1,0:T(4,128)S(1)}, f32[3,2048]{1,0:T(4,128)}, u32[]{:S(2)}) copy-start(f32[3,2048]{1,0:T(4,128)} %param.18) | copy-start | bytes 73732
  0.6 30.2 %copy-start.29 = (f32[1,2048]{1,0:T(1,128)S(1)}, f32[1,2048]{1,0:T(1,128)}, u32[]{:S(2)}) copy-start(f32[1,2048]{1,0:T(1,128)} %param.19) | copy-start | bytes 24580
  0.7 31.6 %copy-start.15 = (f32[48,2048]{1,0:T(8,128)S(1)}, f32[48,2048]{1,0:T(8,128)}, u32[]{:S(2)}) copy-start(f32[48,2048]{1,0:T(8,128)} %param.20) | copy-start | bytes 1179652
  0.7 32.9 %copy-start.28 = (f32[1,3,8,256]{3,2,1,0:T(8,128)S(1)}, f32[1,3,8,256]{3,2,1,0:T(8,128)}, u32[]{:S(2)}) copy-start(f32[1,3,8,256]{3,2,1,0:T(8,128)} %param.25) | copy-start | bytes 73732
  2.3 36.5 %all-to-all-start = ((s32[256,1,1,16]{3,2,1,0:T(1,128)}), s32[256,1,1,16]{3,2,1,0:T(1,128)S(1)}, u32[]{:S(2)}, u32[]{:S(2)}) async-start(s32[256,1,1,16]{3,2,1,0:T(1,128)} %bitcast.17), calls=%async_computation | async-start | bytes 262144 | tf_op jit(solution)/shard_map/all_to_all | solution.py:53
  19.8 14.3 %copy-start.22 = (f32[8]{0:T(128)}, f32[8]{0:T(128)S(1)}, u32[]{:S(2)}) copy-start(f32[8]{0:T(128)S(1)} %get-tuple-element.530) | copy-start | bytes 100
  19.8 38.0 %copy-start.24 = (f32[8]{0:T(128)}, f32[8]{0:T(128)S(1)}, u32[]{:S(2)}) copy-start(f32[8]{0:T(128)S(1)} %get-tuple-element.533) | copy-start | bytes 100
  19.8 40.3 %copy-start.20 = (f32[8]{0:T(128)}, f32[8]{0:T(128)S(1)}, u32[]{:S(2)}) copy-start(f32[8]{0:T(128)S(1)} %get-tuple-element.534) | copy-start | bytes 100
  21.7 17.1 %copy-start.26 = (s32[1,2,8,128]{3,1,2,0:T(2,128)}, s32[1,2,8,128]{3,1,2,0:T(2,128)S(1)}, u32[]{:S(2)}) copy-start(s32[1,2,8,128]{3,1,2,0:T(2,128)S(1)} %copy.508) | copy-start | bytes 24580
  57.0 2.0 copy-start.23
  57.4 2.8 copy-start.36
  57.4 2.8 copy-start.37
  57.4 2.8 copy-start.38
  57.4 2.8 copy-start.39
  57.4 2.8 copy-start.40
  57.4 2.8 copy-start.41
  63.3 18.2 %copy-start.7 = (s32[256,1,1,16]{3,2,1,0:T(1,128)S(1)}, s32[256,1,1,16]{3,2,1,0:T(1,128)}, u32[]{:S(2)}) copy-start(s32[256,1,1,16]{3,2,1,0:T(1,128)} %copy-done.6) | copy-start | bytes 49156
  67.8 28.5 %all-to-all-start.1 = ((f32[256,1,144]{2,1,0:T(1,128)}), f32[256,1,144]{2,1,0:T(1,128)S(1)}, u32[]{:S(2)}, u32[]{:S(2)}) async-start(f32[256,1,144]{2,1,0:T(1,128)} %reshape.1202), calls=%async_computation.1 | async-start | bytes 524288 | tf_op jit(solution)/shard_map/all_to_all | solution.py:53
  196.2 86.6 %all-to-all-start.2 = ((f32[256,1,144]{2,1,0:T(1,128)}), f32[256,1,144]{2,1,0:T(1,128)S(1)}, u32[]{:S(2)}, u32[]{:S(2)}) async-start(f32[256,1,144]{2,1,0:T(1,128)} %reshape.1204), calls=%async_computation.2 | async-start | bytes 524288 | tf_op jit(solution)/shard_map/all_to_all | solution.py:53
  285.3 2.3 copy-start.27
  286.4 2.3 copy-start
  292.2 51.3 %copy-start.3 = (f32[1,8,32,16]{2,3,1,0:T(8,128)S(1)}, f32[1,8,32,16]{2,3,1,0:T(8,128)}, u32[]{:S(2)}) copy-start(f32[1,8,32,16]{2,3,1,0:T(8,128)} %copy-done.2) | copy-start | bytes 49156
  292.2 53.9 %copy-start.5 = (f32[1,8,32,16]{2,3,1,0:T(8,128)S(1)}, f32[1,8,32,16]{2,3,1,0:T(8,128)}, u32[]{:S(2)}) copy-start(f32[1,8,32,16]{2,3,1,0:T(8,128)} %copy-done.4) | copy-start | bytes 49156
  297.6 50.7 %copy-start.21 = (f32[8]{0:T(128)S(1)}, f32[8]{0:T(128)}, u32[]{:S(2)}) copy-start(f32[8]{0:T(128)} %copy-done.20) | copy-start | bytes 100
  343.5 6.0 %copy-start.10 = (f32[1,8,32,16]{2,3,1,0:T(8,128)S(1)}, f32[1,8,32,16]{2,3,1,0:T(8,128)}, u32[]{:S(2)}) copy-start(f32[1,8,32,16]{2,3,1,0:T(8,128)} %get-tuple-element.620) | copy-start | bytes 49156
  343.5 6.0 %copy-start.11 = (f32[1,8,32,16]{2,3,1,0:T(8,128)S(1)}, f32[1,8,32,16]{2,3,1,0:T(8,128)}, u32[]{:S(2)}) copy-start(f32[1,8,32,16]{2,3,1,0:T(8,128)} %get-tuple-element.622) | copy-start | bytes 49156
  343.5 6.0 %copy-start.12 = (f32[1,8,32,16]{2,3,1,0:T(8,128)S(1)}, f32[1,8,32,16]{2,3,1,0:T(8,128)}, u32[]{:S(2)}) copy-start(f32[1,8,32,16]{2,3,1,0:T(8,128)} %get-tuple-element.627) | copy-start | bytes 49156
  343.5 6.0 %copy-start.13 = (f32[1,8,32,16]{2,3,1,0:T(8,128)S(1)}, f32[1,8,32,16]{2,3,1,0:T(8,128)}, u32[]{:S(2)}) copy-start(f32[1,8,32,16]{2,3,1,0:T(8,128)} %get-tuple-element.629) | copy-start | bytes 49156
  343.5 6.0 %copy-start.16 = (f32[1,8,32,16]{2,3,1,0:T(8,128)S(1)}, f32[1,8,32,16]{2,3,1,0:T(8,128)}, u32[]{:S(2)}) copy-start(f32[1,8,32,16]{2,3,1,0:T(8,128)} %get-tuple-element.621) | copy-start | bytes 49156
  343.5 6.0 %copy-start.17 = (f32[1,8,32,16]{2,3,1,0:T(8,128)S(1)}, f32[1,8,32,16]{2,3,1,0:T(8,128)}, u32[]{:S(2)}) copy-start(f32[1,8,32,16]{2,3,1,0:T(8,128)} %get-tuple-element.623) | copy-start | bytes 49156
  343.5 6.0 %copy-start.18 = (f32[1,8,32,16]{2,3,1,0:T(8,128)S(1)}, f32[1,8,32,16]{2,3,1,0:T(8,128)}, u32[]{:S(2)}) copy-start(f32[1,8,32,16]{2,3,1,0:T(8,128)} %get-tuple-element.628) | copy-start | bytes 49156
  343.5 6.0 %copy-start.19 = (f32[1,8,32,16]{2,3,1,0:T(8,128)S(1)}, f32[1,8,32,16]{2,3,1,0:T(8,128)}, u32[]{:S(2)}) copy-start(f32[1,8,32,16]{2,3,1,0:T(8,128)} %get-tuple-element.630) | copy-start | bytes 49156
  (14 other events, 13.1 us)
where the time goes:
time: 389 us; the launch traced here: 381 us
  local copies, waits for them, and re-layouts  131 us (34%)
  other arithmetic  87.5 us (22%)
  loops' own time  43.8 us (11%)
  blocking collectives  40.2 us (10%)
  starting transfers between devices  35.8 us (9%)
  matrix products  30.7 us (8%)
  waiting for transfers between devices  10.8 us (3%)
    another operation x2, loops' own time, render_all(): lax.map(jax.checkpoint(render_packed), (tile_features, live_counts, numbe...  43.8 us
    psum x4, blocking collectives, over_axes(): array = lax.psum(array, axis)  40.2 us
    dynamic_slice x32, local copies, waits for them, and re-layouts, render_all(): lax.map(jax.checkpoint(render_packed), (tile_features, live_counts, numbe...  39.6 us
    all_to_all x3, starting transfers between devices, one_exchange(): lax.all_to_all(blocks, axis, split_axis=0, concat_axis=0, tiled=True)  35.8 us
    scatter-add x1, other arithmetic, local(): jnp.zeros_like(owned).at[:, asked.reshape(-1)]  22.7 us
    unnamed x107, local copies, waits for them, and re-layouts  22.2 us
    dot_general x24, matrix products, render_tile(): jnp.dot(log_keep, strict_upper, precision=lax.Precision.HIGHEST)  15.9 us
    gather x2, local copies, waits for them, and re-layouts, local(): picked = owned[:, asked]  15.2 us
  transfers between devices with their start and end apart: 3, of which 1 were waited for; matrix products, arithmetic and copies ran while one was open for 22% of the time, Pallas kernels for 0%

commit v1 on v0

v1 whole, which is shorter than its diff:
```python
import jax
import jax.numpy as jnp
from jax import lax
from jax.experimental import pallas as pl
from jax.experimental.pallas import tpu as pltpu
from jax.sharding import PartitionSpec as P

TILE_SIDE = 16
TW = 16
ALL = ("img", "tile")
N_IMG = 8
N_TILE = 32
CAP = 16
OWNED = 2048
LIST = 256
TILES_HERE = 8
PIX = 256
LANES = 128
N_FEAT = 24
N_USED = 9
N_GRAD = 9
FEAT_ROWS = 3
GRAD_ROWS = 2

sh_first = 0.28209479177387814
sh_second = 0.4886025119029199
sh_third = (
    1.0925484305920792,
    -1.0925484305920792,
    0.31539156525252005,
    -1.0925484305920792,
    0.5462742152960396,
)
sh_fourth = (
    -0.5900435899266435,
    2.890611442640554,
    -0.4570457994644658,
    0.3731763325901154,
    -0.4570457994644658,
    1.445305721320277,
    -0.5900435899266435,
)
dilation = 0.3
LOG2E = 1.4426950408889634
f32 = jnp.float32
bf16 = jnp.bfloat16


def harmonics_of(polar, azimuth):
    sin_p, cos_p = jnp.sin(polar), jnp.cos(polar)
    x = sin_p * jnp.cos(azimuth)
    y = sin_p * jnp.sin(azimuth)
    z = cos_p
    xx, yy, zz = x * x, y * y, z * z
    return jnp.stack(
        [
            sh_first + 0.0 * x,
            -sh_second * y,
            sh_second * z,
            -sh_second * x,
            sh_third[0] * x * y,
            sh_third[1] * y * z,
            sh_third[2] * (2.0 * zz - xx - yy),
            sh_third[3] * x * z,
            sh_third[4] * (xx - yy),
            sh_fourth[0] * y * (3.0 * xx - yy),
            sh_fourth[1] * x * y * z,
            sh_fourth[2] * y * (4.0 * zz - xx - yy),
            sh_fourth[3] * z * (2.0 * zz - 3.0 * xx - 3.0 * yy),
            sh_fourth[4] * x * (4.0 * zz - xx - yy),
            sh_fourth[5] * z * (xx - yy),
            sh_fourth[6] * x * (xx - 3.0 * yy),
        ],
        axis=-1,
    )


def camera_table(cameras):
    polar, azimuth = cameras[:, 8], cameras[:, 9]
    one = jnp.ones_like(polar)
    zero = jnp.zeros_like(polar)
    values, d_polar = jax.jvp(harmonics_of, (polar, azimuth), (one, zero))
    d_azimuth = jax.jvp(harmonics_of, (polar, azimuth), (zero, one))[1]
    return jnp.concatenate([cameras, values, d_polar, d_azimuth], axis=1)


def shape_matrix(log_scales, quat):
    w, x, y, z = quat
    norm = jnp.sqrt(w * w + x * x + y * y + z * z)
    w, x, y, z = w / norm, x / norm, y / norm, z / norm
    rotation = (
        (1.0 - 2.0 * (y * y + z * z), 2.0 * (x * y - w * z), 2.0 * (x * z + w * y)),
        (2.0 * (x * y + w * z), 1.0 - 2.0 * (x * x + z * z), 2.0 * (y * z - w * x)),
        (2.0 * (x * z - w * y), 2.0 * (y * z + w * x), 1.0 - 2.0 * (x * x + y * y)),
    )
    stretch = [jnp.exp(v) for v in log_scales]
    return [[rotation[r][c] * stretch[c] for c in range(3)] for r in range(3)]


def swap_groups(vregs):
    vregs = list(vregs)
    group = lax.broadcasted_iota(jnp.int32, (8, LANES), 1) // CAP
    for bit in (1, 2, 4):
        low = (group & bit) == 0
        for i in range(8):
            if i & bit:
                continue
            a, b = vregs[i], vregs[i + bit]
            vregs[i] = jnp.where(low, a, pltpu.roll(b, CAP * bit, 1))
            vregs[i + bit] = jnp.where(low, pltpu.roll(a, LANES - CAP * bit, 1), b)
    return vregs


def lane_take(table, lanes):
    return jnp.take_along_axis(table, lanes, axis=1, mode="promise_in_bounds")


def halves(value):
    high = value.astype(bf16)
    return high, (value - high.astype(f32)).astype(bf16)


def dot(a, b):
    return lax.dot_general(a, b, (((1,), (0,)), ((), ())), preferred_element_type=f32)


def dot_t(a, b):
    return lax.dot_general(a, b, (((1,), (1,)), ((), ())), preferred_element_type=f32)


PROJECT_CHUNK = 256


def project_kernel(means, log_scales, quat_w, quat_v, opacity, sh, cam, out):
    column = [jnp.broadcast_to(cam[:, m : m + 1], (N_IMG, PROJECT_CHUNK)) for m in range(8)]

    def chunk(h, carry):
        at = pl.ds(pl.multiple_of(h * PROJECT_CHUNK, PROJECT_CHUNK), PROJECT_CHUNK)
        mean = [means[c : c + 1, at] for c in range(3)]
        quat = [quat_w[0:1, at]] + [quat_v[c : c + 1, at] for c in range(3)]
        m = shape_matrix([log_scales[c : c + 1, at] for c in range(3)], quat)
        for row in range(2):
            a = column[3 * row : 3 * row + 3]
            out[row, :, at] = a[0] * mean[0] + a[1] * mean[1] + a[2] * mean[2] + column[6 + row]
        p = [
            [
                sum(column[3 * row + r] * m[r][c] for r in range(3))
                for c in range(3)
            ]
            for row in range(2)
        ]
        s00 = p[0][0] * p[0][0] + p[0][1] * p[0][1] + p[0][2] * p[0][2] + dilation
        s01 = p[0][0] * p[1][0] + p[0][1] * p[1][1] + p[0][2] * p[1][2]
        s11 = p[1][0] * p[1][0] + p[1][1] * p[1][1] + p[1][2] * p[1][2] + dilation
        det = s00 * s11 - s01 * s01
        out[2, :, at] = s11 / det
        out[3, :, at] = -s01 / det
        out[4, :, at] = s00 / det
        base = 1.0 / (1.0 + jnp.exp(-opacity[0:1, at]))
        out[5, :, at] = jnp.broadcast_to(base, (N_IMG, PROJECT_CHUNK))
        for c in range(3):
            out[9 + c, :, at] = jnp.broadcast_to(mean[c], (N_IMG, PROJECT_CHUNK))
            for row in range(2):
                out[12 + 3 * row + c, :, at] = (
                    m[c][0] * p[row][0] + m[c][1] * p[row][1] + m[c][2] * p[row][2]
                )
        for base_row, first, start in ((6, 10, 0.5), (18, 26, 0.0), (21, 42, 0.0)):
            total = [jnp.full((N_IMG, PROJECT_CHUNK), start, f32) for _ in range(3)]
            for b in range(16):
                y = jnp.broadcast_to(cam[:, first + b : first + b + 1], (N_IMG, PROJECT_CHUNK))
                for k in range(3):
                    total[k] = total[k] + y * sh[16 * k + b : 16 * k + b + 1, at]
            for k in range(3):
                out[base_row + k, :, at] = total[k]
        return carry

    lax.fori_loop(0, OWNED // PROJECT_CHUNK, chunk, 0)


def asked_lanes(asked):
    group = lax.broadcasted_iota(jnp.int32, (8, LANES), 1) // CAP
    result = []
    for q in range(4):
        total = asked[pl.ds(8 * q, 8, stride=N_TILE), :]
        for k in range(1, 8):
            piece = asked[pl.ds(8 * q + k, 8, stride=N_TILE), :]
            total = jnp.where(group == k, pltpu.roll(piece, CAP * k, 1), total)
        result.append(total)
    return result


def pick_kernel(feats, asked, out):
    index = asked_lanes(asked)
    low = [v & (LANES - 1) for v in index]
    high = [v >> 7 for v in index]
    for g in range(FEAT_ROWS):
        picked = [[None] * 8 for _ in range(4)]
        for f in range(8):
            for q in range(4):
                value = jnp.zeros((8, LANES), f32)
                for h in range(OWNED // LANES):
                    table = feats[8 * g + f, :, h * LANES : (h + 1) * LANES]
                    value = jnp.where(high[q] == h, lane_take(table, low[q]), value)
                picked[q][f] = value
        for q in range(4):
            rows = swap_groups(picked[q])
            for k in range(8):
                out[pl.ds(FEAT_ROWS * (8 * q + k) + g, 8, stride=FEAT_ROWS * N_TILE), :] = rows[k]


def render_kernel(
    meta,
    rows,
    lists,
    cot,
    image,
    out,
    tab,
    feat,
    grads,
    slot,
    upper,
    lower,
    al_s,
    lk_s,
    lb_s,
    s_s,
    w_s,
    sw_s,
    g_s,
):
    tile_base = meta[TILES_HERE] * TILES_HERE
    for g in range(FEAT_ROWS):
        for q in range(4):
            pieces = [
                rows[pl.ds(FEAT_ROWS * (8 * q + k) + g, 8, stride=FEAT_ROWS * N_TILE), :]
                for k in range(8)
            ]
            pieces = swap_groups(pieces)
            for f in range(8):
                tab[8 * g + f, 8 * q : 8 * q + 8, :] = pieces[f]
    entry_lane = [lists[:, h * LANES : (h + 1) * LANES] & (LANES - 1) for h in range(2)]
    entry_chunk = []
    for h in range(2):
        s = lists[:, h * LANES : (h + 1) * LANES]
        entry_chunk.append(((s >> 7) & 3) * 8 + (s >> 9))

    def gather(ch, carry):
        new = []
        for f in range(N_USED):
            table = jnp.broadcast_to(tab[f, pl.ds(ch, 1), :], (8, LANES))
            for h in range(2):
                new.append(
                    jnp.where(entry_chunk[h] == ch, lane_take(table, entry_lane[h]), carry[2 * f + h])
                )
        return tuple(new)

    zero = jnp.zeros((8, LANES), f32)
    found = lax.fori_loop(0, 32, gather, tuple([zero] * (2 * N_USED)))
    for f in range(N_USED):
        for h in range(2):
            feat[f, :, h * LANES : (h + 1) * LANES] = found[2 * f + h]
    ri = lax.broadcasted_iota(jnp.int32, (LIST, LIST), 0)
    ci = lax.broadcasted_iota(jnp.int32, (LIST, LIST), 1)
    up = (ri < ci).astype(f32).astype(bf16)
    lo = (ri > ci).astype(f32).astype(bf16)
    for part in range(2):
        upper[part * LIST : (part + 1) * LIST, :] = up
        lower[part * LIST : (part + 1) * LIST, :] = lo
    slot[...] = jnp.zeros_like(slot)
    lane = lax.broadcasted_iota(jnp.int32, (1, LIST), 1)
    px = lax.broadcasted_iota(jnp.int32, (TILE_SIDE, LIST), 0).astype(f32) - 7.5
    pix = lax.broadcasted_iota(jnp.int32, (8, PIX), 1)
    which = lax.broadcasted_iota(jnp.int32, (8, PIX), 0)
    pxr = (pix % TILE_SIDE).astype(f32) - 7.5
    pyr = (pix // TILE_SIDE).astype(f32) - 7.5
    basis = jnp.where(
        which == 0,
        1.0,
        jnp.where(
            which == 1,
            pxr,
            jnp.where(
                which == 2,
                pyr,
                jnp.where(which == 3, pxr * pxr, jnp.where(which == 4, pxr * pyr, pyr * pyr)),
            ),
        ),
    ).astype(bf16)
    basis = jnp.concatenate([basis, basis], axis=1)
    ch_iota = lax.broadcasted_iota(jnp.int32, (32, LIST), 0)
    lane_iota = lax.broadcasted_iota(jnp.int32, (LANES, LIST), 0)

    def tile(j, carry):
        number = tile_base + j
        centre_x = (TILE_SIDE * (number % TW)).astype(f32) + (0.5 * TILE_SIDE - 0.5 * TILE_SIDE * TW)
        centre_y = (TILE_SIDE * (number // TW)).astype(f32) + (0.5 * TILE_SIDE - 0.5 * TILE_SIDE * TW)
        at = pl.ds(j, 1)
        ux = feat[0, at, :] - centre_x
        uy = feat[1, at, :] - centre_y
        ca, cb, cc = feat[2, at, :], feat[3, at, :], feat[4, at, :]
        op = jnp.where(lane < meta[j], feat[5, at, :], 0.0)
        op8 = jnp.broadcast_to(op, (TILE_SIDE, LIST))
        uy8 = jnp.broadcast_to(uy, (TILE_SIDE, LIST))
        cc8 = jnp.broadcast_to(cc * (-0.5 * LOG2E), (TILE_SIDE, LIST))
        dx = px - ux
        na = (ca * (-0.5 * LOG2E)) * dx * dx
        nb = (cb * (-LOG2E)) * dx
        colours = jnp.concatenate([feat[6 + k, at, :] for k in range(3)], axis=0)
        cots = jnp.concatenate([cot[k, at, :] for k in range(3)], axis=0)
        col_h, col_l = halves(colours)
        cot_h, cot_l = halves(cots)
        col_h, col_l, cot_h, cot_l = [v.astype(f32) for v in (col_h, col_l, cot_h, cot_l)]
        pad = jnp.zeros((4, LIST), f32)
        cot_k = jnp.concatenate([cot_h, cot_h, cot_l, cot_l, pad], axis=0)
        col_k = jnp.concatenate([col_h, col_l, col_h, col_l, pad], axis=0).astype(bf16)
        s_s[...] = dot(jnp.transpose(cot_k).astype(bf16), col_k)
        for py in range(TILE_SIDE):
            r = slice(TILE_SIDE * py, TILE_SIDE * (py + 1))
            dy = (py - 7.5) - uy8
            alpha = op8 * jnp.exp2(na + cc8 * dy * dy + nb * dy)
            al_s[r, :] = alpha
            hi, low = halves(jnp.log2(1.0 - alpha))
            lk_s[r, 0:LIST] = hi
            lk_s[r, LIST : 2 * LIST] = low
        lb_s[...] = dot(lk_s[...], upper[...])
        for py in range(TILE_SIDE):
            r = slice(TILE_SIDE * py, TILE_SIDE * (py + 1))
            w = al_s[r, :] * jnp.exp2(lb_s[r, :])
            hi, low = halves(w)
            w_s[r, :] = hi
            w_s[PIX + TILE_SIDE * py : PIX + TILE_SIDE * (py + 1), :] = low
            sw = s_s[r, :] * w
            s_s[r, :] = sw
            hi, low = halves(sw)
            sw_s[r, 0:LIST] = hi
            sw_s[r, LIST : 2 * LIST] = low
        lb_s[...] = dot(sw_s[...], lower[...])
        for py in range(TILE_SIDE):
            r = slice(TILE_SIDE * py, TILE_SIDE * (py + 1))
            alpha = al_s[r, :]
            g = s_s[r, :] - lb_s[r, :] * (alpha / (1.0 - alpha))
            hi, low = halves(g)
            g_s[r, :] = hi
            g_s[PIX + TILE_SIDE * py : PIX + TILE_SIDE * (py + 1), :] = low
        pad2 = jnp.zeros((2, LIST), f32)
        col_rows = jnp.concatenate([col_h, col_l, pad2], axis=0).astype(bf16)
        shown = dot_t(col_rows, w_s[0:PIX, :]) + dot_t(col_rows, w_s[PIX : 2 * PIX, :])
        for k in range(3):
            image[k, at, :] = shown[k : k + 1, :] + shown[3 + k : 4 + k, :]
        cot_rows = jnp.concatenate([cot_h, cot_l, pad2], axis=0).astype(bf16)
        gcol = dot(jnp.concatenate([cot_rows, cot_rows], axis=1), w_s[...])
        mom = dot(basis, g_s[...])
        m0, mx, my = mom[0:1, :], mom[1:2, :], mom[2:3, :]
        mxx, mxy, myy = mom[3:4, :], mom[4:5, :], mom[5:6, :]
        grad = [
            m0,
            mx - ux * m0,
            my - uy * m0,
            mxx - 2.0 * ux * mx + ux * ux * m0,
            mxy - ux * my - uy * mx + ux * uy * m0,
            myy - 2.0 * uy * my + uy * uy * m0,
        ] + [gcol[k : k + 1, :] + gcol[3 + k : 4 + k, :] for k in range(3)]
        s = lists[at, :]
        chunk = ((s >> 7) & 3) * 8 + (s >> 9)
        chunk_hit = ch_iota == chunk
        lane_hit = (lane_iota == (s & (LANES - 1))).astype(f32).astype(bf16)
        for f in range(N_GRAD):
            hi, low = halves(jnp.where(chunk_hit, grad[f], 0.0))
            grads[32 * f : 32 * (f + 1), 0:LIST] = hi
            grads[32 * f : 32 * (f + 1), LIST : 2 * LIST] = low
        slot[...] += dot_t(grads[...], jnp.concatenate([lane_hit, lane_hit], axis=1))
        return carry

    lax.fori_loop(0, TILES_HERE, tile, 0)

    terms = [jnp.zeros((8, LANES), f32) for _ in range(10)]
    for q in range(4):
        r = slice(8 * q, 8 * q + 8)
        ca, cb, cc = tab[2, r, :], tab[3, r, :], tab[4, r, :]
        gr = [slot[32 * f + 8 * q : 32 * f + 8 * q + 8, :] for f in range(N_GRAD)]
        du = (ca * gr[1] + cb * gr[2], cb * gr[1] + cc * gr[2])
        h00, h01, h11 = conic_pull(ca, cb, cc, gr[3], gr[4], gr[5])
        for c in range(3):
            mean, n0, n1 = tab[9 + c, r, :], tab[12 + c, r, :], tab[15 + c, r, :]
            terms[c] += du[0] * mean + 2.0 * (h00 * n0 + h01 * n1)
            terms[3 + c] += du[1] * mean + 2.0 * (h01 * n0 + h11 * n1)
            terms[8] += gr[6 + c] * tab[18 + c, r, :]
            terms[9] += gr[6 + c] * tab[21 + c, r, :]
        terms[6] += du[0]
        terms[7] += du[1]
    lanes = lax.broadcasted_iota(jnp.int32, (8, LANES), 1)
    share = jnp.zeros((8, LANES), f32)
    for m in range(10):
        total = jnp.sum(jnp.sum(terms[m], axis=0, keepdims=True), axis=1, keepdims=True)
        share = jnp.where(lanes == CAP + m, jnp.broadcast_to(total, (8, LANES)), share)
    for q in range(4):
        pieces = swap_groups([slot[32 * f + 8 * q : 32 * f + 8 * q + 8, :] for f in range(8)])
        last = slot[32 * 8 + 8 * q : 32 * 8 + 8 * q + 8, :]
        for k in range(8):
            first_row = GRAD_ROWS * (8 * q + k)
            stride = GRAD_ROWS * N_TILE
            out[pl.ds(first_row, 8, stride=stride), :] = pieces[k]
            moved = last if k == 0 else pltpu.roll(last, LANES - CAP * k, 1)
            out[pl.ds(first_row + 1, 8, stride=stride), :] = jnp.where(lanes < CAP, moved, share)


def conic_pull(ca, cb, cc, qxx, qxy, qyy):
    t00, t01 = ca * qxx + cb * qxy, ca * qxy + cb * qyy
    t10, t11 = cb * qxx + cc * qxy, cb * qxy + cc * qyy
    return 0.5 * (t00 * ca + t01 * cb), 0.5 * (t00 * cb + t01 * cc), 0.5 * (t10 * cb + t11 * cc)


PULL_CHUNK = 128


def pull_kernel(
    returned, asked, feats, log_scales, quat_w, quat_v, cam, out, cam_out, row_s, idx_s, lhs_s, sum_s, y_s, gc_s
):
    index = asked_lanes(asked)
    for q in range(4):
        idx_s[:, q * LANES : (q + 1) * LANES] = index[q]
    stride = GRAD_ROWS * N_TILE
    group = lax.broadcasted_iota(jnp.int32, (8, LANES), 1) // CAP
    camera = jnp.zeros((8, LANES), f32)
    for q in range(4):
        pieces = [returned[pl.ds(GRAD_ROWS * (8 * q + k), 8, stride=stride), :] for k in range(8)]
        pieces = swap_groups(pieces)
        for f in range(8):
            row_s[f, :, q * LANES : (q + 1) * LANES] = pieces[f]
        last = None
        for k in range(8):
            piece = returned[pl.ds(GRAD_ROWS * (8 * q + k) + 1, 8, stride=stride), :]
            camera = camera + piece
            last = piece if k == 0 else jnp.where(group == k, pltpu.roll(piece, CAP * k, 1), last)
        row_s[8, :, q * LANES : (q + 1) * LANES] = last
    cam_out[...] = pltpu.roll(camera, LANES - CAP, 1)[:, 0:10]

    slots = N_TILE * CAP
    high_iota = lax.broadcasted_iota(jnp.int32, (16, slots), 0)
    lane_iota = lax.broadcasted_iota(jnp.int32, (LANES, slots), 0)

    def image(i, carry):
        at = pl.ds(i, 1)
        s = idx_s[at, :]
        high_hit = high_iota == (s >> 7)
        lane_hit = (lane_iota == (s & (LANES - 1))).astype(f32).astype(bf16)
        for f in range(N_GRAD):
            hi, low = halves(jnp.where(high_hit, row_s[f, at, :], 0.0))
            lhs_s[16 * f : 16 * (f + 1), 0:slots] = hi
            lhs_s[16 * f : 16 * (f + 1), slots : 2 * slots] = low
        sum_s[pl.ds(pl.multiple_of(i * (16 * N_GRAD), 16), 16 * N_GRAD), :] = dot_t(
            lhs_s[...], jnp.concatenate([lane_hit, lane_hit], axis=1)
        )
        return carry

    lax.fori_loop(0, N_IMG, image, 0)

    column = [jnp.broadcast_to(cam[:, m : m + 1], (N_IMG, PULL_CHUNK)) for m in range(6)]

    def chunk(h, carry):
        at = pl.ds(pl.multiple_of(h * PULL_CHUNK, PULL_CHUNK), PULL_CHUNK)
        gr = [sum_s[pl.ds(16 * f + h, 8, stride=16 * N_GRAD), :] for f in range(N_GRAD)]
        ca, cb, cc = feats[2, :, at], feats[3, :, at], feats[4, :, at]
        du = (ca * gr[1] + cb * gr[2], cb * gr[1] + cc * gr[2])
        h00, h01, h11 = conic_pull(ca, cb, cc, gr[3], gr[4], gr[5])
        a0, a1 = column[0:3], column[3:6]

        def over_images(v):
            return jnp.sum(v, axis=0, keepdims=True)

        for c in range(3):
            out[c : c + 1, at] = over_images(a0[c] * du[0] + a1[c] * du[1])
        t0 = [h00 * a0[c] + h01 * a1[c] for c in range(3)]
        t1 = [h01 * a0[c] + h11 * a1[c] for c in range(3)]
        v = [[None] * 3 for _ in range(3)]
        for c in range(3):
            for d in range(c, 3):
                v[c][d] = v[d][c] = over_images(t0[c] * a0[d] + t1[c] * a1[d])
        ls = [log_scales[c : c + 1, at] for c in range(3)]
        quat = [quat_w[0:1, at]] + [quat_v[c : c + 1, at] for c in range(3)]
        m, pull = jax.vjp(shape_matrix, ls, quat)
        dm = [[2.0 * sum(v[r][d] * m[d][c] for d in range(3)) for c in range(3)] for r in range(3)]
        dls, dquat = pull(dm)
        for c in range(3):
            out[3 + c : 4 + c, at] = dls[c]
        for c in range(4):
            out[6 + c : 7 + c, at] = dquat[c]
        base = feats[5, 0:1, at]
        out[10:11, at] = over_images(gr[0]) * (1.0 - base)
        for k in range(3):
            gc_s[8 * k : 8 * k + 8, at] = gr[6 + k]
        return carry

    lax.fori_loop(0, OWNED // PULL_CHUNK, chunk, 0)

    y_h, y_l = halves(jnp.transpose(cam[:, 10:26]))
    y_all = jnp.concatenate([y_h.astype(f32), y_h.astype(f32), y_l.astype(f32), y_l.astype(f32)], axis=1).astype(bf16)
    for k in range(3):
        g_h, g_l = halves(gc_s[8 * k : 8 * k + 8, :])
        g_all = jnp.concatenate([g_h.astype(f32), g_l.astype(f32), g_h.astype(f32), g_l.astype(f32)], axis=0).astype(bf16)
        out[11 + 16 * k : 27 + 16 * k, :] = dot(y_all, g_all)


def whole(memory=pltpu.VMEM):
    return pl.BlockSpec(memory_space=memory)


def call(kernel, name, out_shape, scratch, n_in, smem=0):
    return pl.pallas_call(
        kernel,
        name=name,
        out_shape=out_shape,
        in_specs=[whole(pltpu.SMEM)] * smem + [whole()] * (n_in - smem),
        out_specs=jax.tree.map(lambda _: whole(), out_shape),
        scratch_shapes=scratch,
        compiler_params=pltpu.CompilerParams(vmem_limit_bytes=32 << 20),
    )


def exchange(array):
    return lax.all_to_all(array, ALL, split_axis=0, concat_axis=0, tiled=True)


def exchange_rows(array, rows):
    shape = array.shape
    return exchange(array.reshape(-1, 1, rows * LANES)).reshape(shape)


def local(
    means, log_scales, quat_w, quat_v, opacity, sh_coeffs, cameras, requests, lists, counts, image_cot
):
    devices = N_IMG * N_TILE
    wanted = jnp.pad(requests.reshape(devices, CAP), ((0, 0), (0, LANES - CAP)))
    asked = exchange_rows(wanted, 1)
    cam = camera_table(cameras)
    feats = call(
        project_kernel, "project", jax.ShapeDtypeStruct((N_FEAT, N_IMG, OWNED), f32), [], 7
    )(means, log_scales, quat_w, quat_v, opacity, sh_coeffs, cam)
    packed = call(
        pick_kernel, "pick", jax.ShapeDtypeStruct((FEAT_ROWS * devices, LANES), f32), [], 2
    )(feats, asked)
    rows = exchange_rows(packed, FEAT_ROWS)
    meta = jnp.concatenate([counts[0], lax.axis_index("tile").astype(jnp.int32)[None]])
    rendered, slot_grads = call(
        render_kernel,
        "render",
        (
            jax.ShapeDtypeStruct((3, TILES_HERE, PIX), f32),
            jax.ShapeDtypeStruct((GRAD_ROWS * devices, LANES), f32),
        ),
        [
            pltpu.VMEM((N_FEAT, 32, LANES), f32),
            pltpu.VMEM((N_USED, 8, LIST), f32),
            pltpu.VMEM((32 * N_GRAD, 2 * LIST), bf16),
            pltpu.VMEM((32 * N_GRAD, LANES), f32),
            pltpu.VMEM((2 * LIST, LIST), bf16),
            pltpu.VMEM((2 * LIST, LIST), bf16),
            pltpu.VMEM((PIX, LIST), f32),
            pltpu.VMEM((PIX, 2 * LIST), bf16),
            pltpu.VMEM((PIX, LIST), f32),
            pltpu.VMEM((PIX, LIST), f32),
            pltpu.VMEM((2 * PIX, LIST), bf16),
            pltpu.VMEM((PIX, 2 * LIST), bf16),
            pltpu.VMEM((2 * PIX, LIST), bf16),
        ],
        4,
        smem=1,
    )(meta, rows, lists[0], image_cot[0])
    returned = exchange_rows(slot_grads, GRAD_ROWS)
    param_grad, camera_grad = call(
        pull_kernel,
        "pull",
        (
            jax.ShapeDtypeStruct((59, OWNED), f32),
            jax.ShapeDtypeStruct((N_IMG, 10), f32),
        ),
        [
            pltpu.VMEM((N_GRAD, N_IMG, N_TILE * CAP), f32),
            pltpu.VMEM((N_IMG, N_TILE * CAP), jnp.int32),
            pltpu.VMEM((16 * N_GRAD, 2 * N_TILE * CAP), bf16),
            pltpu.VMEM((N_IMG * 16 * N_GRAD, LANES), f32),
            pltpu.VMEM((16, LANES), f32),
            pltpu.VMEM((24, OWNED), f32),
        ],
        7,
    )(returned, asked, feats, log_scales, quat_w, quat_v, cam)
    return (rendered[None], param_grad, camera_grad)


def solution(mesh):
    own = P(None, ALL)
    return jax.shard_map(
        local,
        mesh=mesh,
        in_specs=(
            own,
            own,
            own,
            own,
            own,
            own,
            P(),
            P("img", "tile", None, None, None),
            P("img", "tile", None),
            P("img", "tile"),
            P("img", None, "tile", None),
        ),
        out_specs=(P("img", None, "tile", None), own, P()),
        check_vma=False,
    )
```

time: 389 us -> 101 us (0.26); the launches traced: 381 us -> 101 us
  local copies, waits for them, and re-layouts: 131 us -> 6.15 us
  other arithmetic: 87.5 us -> 2.71 us
  loops' own time: 43.8 us -> 0 us
  matrix products: 30.7 us -> 0 us
  Pallas kernels: 0 us -> 23.2 us
  blocking collectives: 40.2 us -> 21.2 us
  starting transfers between devices: 35.8 us -> 25.4 us
  waiting for transfers between devices: 10.8 us -> 21.1 us
    another operation x2 -> x0, loops' own time: 43.8 us -> none  [render_all(): lax.map(jax.checkpoint(render_packed), (tile_features, live_counts, numbe...]
    psum x4 -> x0, blocking collectives: 40.2 us -> none  [over_axes(): array = lax.psum(array, axis)]
    dynamic_slice x32 -> x0, local copies, waits for them, and re-layouts: 39.6 us -> none  [render_all(): lax.map(jax.checkpoint(render_packed), (tile_features, live_counts, numbe...]
    scatter-add x2 -> x0, other arithmetic: 34.8 us -> none  [the longest x1 22.7 us: local(): jnp.zeros_like(owned).at[:, asked.reshape(-1)]]
    dot_general x48 -> x0, matrix products: 30.7 us -> none  [the longest x24 15.9 us: render_tile(): jnp.dot(log_keep, strict_upper, precision=lax.Precision.HIGHEST)]
    pallas_call x0 -> x4, Pallas kernels: none -> 23.2 us  [the longest x1 12.7 us: local(): call(render_kernel, 'render', (jax.ShapeDtypeStruct((3, TILES_HERE, PIX),...]
    gather x4 -> x0, local copies, waits for them, and re-layouts: 22 us -> none  [the longest x2 15.2 us: local(): picked = owned[:, asked]]
    all_to_all x0 -> x1, blocking collectives: none -> 21.2 us  [exchange(): return lax.all_to_all(array, ALL, split_axis=0, concat_axis=0, tiled=True)]
  transfers between devices with their start and end apart: 3 -> 2, of which waited for: 1 -> 2; matrix products, arithmetic and copies ran while one was open for 22% -> 3% of each run, Pallas kernels for 0% -> 1%
where the time goes in v1:
time: 101 us
  starting transfers between devices  25.4 us (25%)
  Pallas kernels  23.2 us (23%)
  blocking collectives  21.2 us (21%)
  waiting for transfers between devices  21.1 us (21%)
  local copies, waits for them, and re-layouts  6.15 us (6%)
  other arithmetic  2.71 us (3%)
    all_to_all x2, starting transfers between devices, exchange(): return lax.all_to_all(array, ALL, split_axis=0, concat_axis=0, tiled=True)  25.4 us
    all_to_all x1, blocking collectives, exchange(): return lax.all_to_all(array, ALL, split_axis=0, concat_axis=0, tiled=True)  21.2 us
    all_to_all x2, waiting for transfers between devices, exchange(): return lax.all_to_all(array, ALL, split_axis=0, concat_axis=0, tiled=True)  21.1 us
    pallas_call x1, Pallas kernels, local(): call(render_kernel, 'render', (jax.ShapeDtypeStruct((3, TILES_HERE, PIX),...  12.7 us
    pallas_call x1, Pallas kernels, local(): call(pull_kernel, 'pull', (jax.ShapeDtypeStruct((59, OWNED), f32), jax.Sh...  4.83 us
    unnamed x25, local copies, waits for them, and re-layouts  4.67 us
    pallas_call x1, Pallas kernels, local(): call(pick_kernel, 'pick', jax.ShapeDtypeStruct((FEAT_ROWS * devices, LANE...  4.29 us
  transfers between devices with their start and end apart: 2, of which 2 were waited for; matrix products, arithmetic and copies ran while one was open for 3% of the time, Pallas kernels for 1%

profile of v1, /device:TPU:1, one launch (start us, length us, event | category | flops | bytes accessed | tf_op | source)
XLA Modules:
  0.0 100.6 jit_solution(8946668452972759569)
XLA Ops:
  0.6 0.0 copy-start
  0.6 1.0 copy.15
  1.6 0.7 pad.4
  2.3 15.6 %all-to-all-start = ((s32[256,1,128]{2,1,0:T(1,128)}), s32[256,1,128]{2,1,0:T(1,128)S(1)}, u32[]{:S(2)}, u32[]{:S(2)}) async-start(s32[256,1,128]{2,1,0:T(1,128)} %bitcast.3), calls=%async_computation | async-start | bytes 262144 | tf_op jit(solution)/shard_map/all_to_all | solution.py:522
  18.0 0.9 multiply_add_fusion
  18.8 0.9 multiply_add_fusion.2
  19.8 0.8 multiply_add_fusion.13
  20.6 0.8 concatenate.7.cam
  21.4 0.0 copy-done
  21.4 0.0 copy-start.1
  21.4 0.7 copy-done.1
  22.2 0.8 copy-done.3
  22.9 0.8 copy-done.5
  23.7 0.7 copy-done.6
  24.4 0.7 copy-done.9
  25.1 1.4 %project.1.feats = f32[24,8,2048]{2,1,0:T(8,128)S(1)} custom-call(f32[3,2048]{1,0:T(4,128)S(1)} %copy-done.5, f32[3,2048]{1,0:T(4,128)S(1)} %copy-done.1, f32[1,2048]{1,0:T(1,128)S(1)} %copy-done.6, f32[3,2048]{1,0:T(4,128)S(1)} %copy-done.3, f32[1,2048]{1,0:T(1,128)S(1)} %copy-done.9, f32[48,2048]{1,0:T(8,128)S(1)} %copy-done, f32[8,58]{1,0:T(8,128)S(1)} %concatenate.7.cam), custom_call_target="tpu_custom_call" | custom-call | tf_op jit(solution)/shard_map/project/pallas_call | solution.py:537
  26.5 0.0 copy-start.11
  26.5 0.0 copy-start.8
  26.5 0.0 copy-start.10
  26.6 4.0 %all-to-all-done = s32[256,1,128]{2,1,0:T(1,128)S(1)} async-done(((s32[256,1,128]{2,1,0:T(1,128)}), s32[256,1,128]{2,1,0:T(1,128)S(1)}, u32[]{:S(2)}, u32[]{:S(2)}) %all-to-all-start) | async-done | bytes 131104 | tf_op jit(solution)/shard_map/all_to_all | solution.py:522
  30.6 4.3 %pick.1 = f32[768,128]{1,0:T(8,128)} custom-call(f32[24,8,2048]{2,1,0:T(8,128)S(1)} %project.1.feats, s32[256,128]{1,0:T(8,128)S(1)} %bitcast.13), custom_call_target="tpu_custom_call" | custom-call | tf_op jit(solution)/shard_map/pick/pallas_call | solution.py:540
  34.9 9.7 %all-to-all-start.1 = ((f32[256,1,384]{2,1,0:T(1,128)}), f32[256,1,384]{2,1,0:T(1,128)S(1)}, u32[]{:S(2)}, u32[]{:S(2)}) async-start(f32[256,1,384]{2,1,0:T(1,128)} %bitcast.5), calls=%async_computation.1 | async-start | bytes 786432 | tf_op jit(solution)/shard_map/all_to_all | solution.py:522
  44.6 0.0 copy-done.11
  44.6 0.1 pad_add_fusion.meta
  44.7 17.1 %all-to-all-done.1 = f32[256,1,384]{2,1,0:T(1,128)S(1)} async-done(((f32[256,1,384]{2,1,0:T(1,128)}), f32[256,1,384]{2,1,0:T(1,128)S(1)}, u32[]{:S(2)}, u32[]{:S(2)}) %all-to-all-start.1) | async-done | bytes 393248 | tf_op jit(solution)/shard_map/all_to_all | solution.py:522
  61.8 0.0 copy-done.8
  61.8 0.0 copy-done.10
  61.8 12.7 %render.1 = (f32[3,8,256]{2,1,0:T(8,128)}, f32[512,128]{1,0:T(8,128)S(1)}) custom-call(s32[9]{0:T(128)S(1)} %pad_add_fusion.meta, f32[768,128]{1,0:T(8,128)S(1)} %bitcast.12, s32[8,256]{1,0:T(8,128)S(1)} %bitcast.18, f32[3,8,256]{2,1,0:T(8,128)S(1)} %bitcast.17), custom_call_target="tpu_custom_call" | custom-call | tf_op jit(solution)/shard_map/render/pallas_call | solution.py:545
  74.5 21.2 %all_to_all.15 = f32[256,1,256]{2,1,0:T(1,128)S(1)} all-to-all(f32[256,1,256]{2,1,0:T(1,128)S(1)} %bitcast.16), channel_id=1, replica_groups=mesh['img'=8,'tile'=32] {'img','tile'}, dimensions={0} | all-to-all | bytes 524288 | tf_op jit(solution)/shard_map/all_to_all | solution.py:522
  95.7 0.0 copy-done.2
  95.7 0.0 copy-done.4
  95.8 4.8 %pull.1 = (f32[59,2048]{1,0:T(8,128)}, f32[8,10]{1,0:T(8,128)}) custom-call(f32[512,128]{1,0:T(8,128)S(1)} %bitcast.15, s32[256,128]{1,0:T(8,128)S(1)} %bitcast.14, f32[24,8,2048]{2,1,0:T(8,128)S(1)} %project.1.feats, f32[3,2048]{1,0:T(4,128)S(1)} %copy-done.2, f32[1,2048]{1,0:T(1,128)S(1)} %copy-done.7, f32[3,2048]{1,0:T(4,128)S(1)} %copy-done.4, ...), custom_call_target="tpu_custom_call" | custom-call | tf_op jit(solution)/shard_map/pull/pallas_call | solution.py:571
  (8 shorter events, 0.0 us)
Async XLA Ops:
  0.6 20.8 %copy-start = (f32[48,2048]{1,0:T(8,128)S(1)}, f32[48,2048]{1,0:T(8,128)}, u32[]{:S(2)}) copy-start(f32[48,2048]{1,0:T(8,128)} %sh.1) | copy-start | bytes 1179652
  2.3 28.3 %all-to-all-start = ((s32[256,1,128]{2,1,0:T(1,128)}), s32[256,1,128]{2,1,0:T(1,128)S(1)}, u32[]{:S(2)}, u32[]{:S(2)}) async-start(s32[256,1,128]{2,1,0:T(1,128)} %bitcast.3), calls=%async_computation | async-start | bytes 262144 | tf_op jit(solution)/shard_map/all_to_all | solution.py:522
  21.4 0.8 copy-start.1
  22.2 0.8 copy-start.3
  22.9 0.8 copy-start.5
  23.7 0.7 copy-start.6
  24.4 0.7 copy-start.9
  26.5 18.1 %copy-start.11 = (s32[1,8]{1,0:T(1,128)S(1)}, s32[1,8]{1,0:T(1,128)}, u32[]{:S(2)}) copy-start(s32[1,8]{1,0:T(1,128)} %param.20) | copy-start | bytes 100
  26.5 35.3 %copy-start.8 = (f32[1,3,8,256]{3,2,1,0:T(8,128)S(1)}, f32[1,3,8,256]{3,2,1,0:T(8,128)}, u32[]{:S(2)}) copy-start(f32[1,3,8,256]{3,2,1,0:T(8,128)} %param.21) | copy-start | bytes 73732
  26.5 35.3 %copy-start.10 = (s32[1,8,256]{2,1,0:T(8,128)S(1)}, s32[1,8,256]{2,1,0:T(8,128)}, u32[]{:S(2)}) copy-start(s32[1,8,256]{2,1,0:T(8,128)} %param.19) | copy-start | bytes 24580
  30.6 65.2 %copy-start.2 = (f32[3,2048]{1,0:T(4,128)S(1)}, f32[3,2048]{1,0:T(4,128)}, u32[]{:S(2)}) copy-start(f32[3,2048]{1,0:T(4,128)} %log_scales.3) | copy-start | bytes 73732
  30.6 65.2 %copy-start.4 = (f32[3,2048]{1,0:T(4,128)S(1)}, f32[3,2048]{1,0:T(4,128)}, u32[]{:S(2)}) copy-start(f32[3,2048]{1,0:T(4,128)} %quat_v.3) | copy-start | bytes 73732
  30.6 65.2 %copy-start.7 = (f32[1,2048]{1,0:T(1,128)S(1)}, f32[1,2048]{1,0:T(1,128)}, u32[]{:S(2)}) copy-start(f32[1,2048]{1,0:T(1,128)} %quat_w.3) | copy-start | bytes 24580
  34.9 26.9 %all-to-all-start.1 = ((f32[256,1,384]{2,1,0:T(1,128)}), f32[256,1,384]{2,1,0:T(1,128)S(1)}, u32[]{:S(2)}, u32[]{:S(2)}) async-start(f32[256,1,384]{2,1,0:T(1,128)} %bitcast.5), calls=%async_computation.1 | async-start | bytes 786432 | tf_op jit(solution)/shard_map/all_to_all | solution.py:522

commit v2 on v1

v2 whole, which is shorter than its diff:
```python
import jax
import jax.numpy as jnp
from jax import lax
from jax.experimental import pallas as pl
from jax.experimental.pallas import tpu as pltpu
from jax.sharding import PartitionSpec as P

TILE_SIDE = 16
TW = 16
ALL = ("img", "tile")
ORDER = ("tile", "img")
N_IMG = 8
N_TILE = 32
CAP = 16
OWNED = 2048
LIST = 256
TILES_HERE = 8
PIX = 256
LANES = 128
N_FEAT = 24
N_USED = 9
N_GRAD = 9
FEAT_ROWS = 3
GRAD_ROWS = 2

sh_first = 0.28209479177387814
sh_second = 0.4886025119029199
sh_third = (
    1.0925484305920792,
    -1.0925484305920792,
    0.31539156525252005,
    -1.0925484305920792,
    0.5462742152960396,
)
sh_fourth = (
    -0.5900435899266435,
    2.890611442640554,
    -0.4570457994644658,
    0.3731763325901154,
    -0.4570457994644658,
    1.445305721320277,
    -0.5900435899266435,
)
dilation = 0.3
LOG2E = 1.4426950408889634
f32 = jnp.float32
bf16 = jnp.bfloat16


def harmonics_of(polar, azimuth):
    sin_p, cos_p = jnp.sin(polar), jnp.cos(polar)
    x = sin_p * jnp.cos(azimuth)
    y = sin_p * jnp.sin(azimuth)
    z = cos_p
    xx, yy, zz = x * x, y * y, z * z
    return [
        sh_first + 0.0 * x,
        -sh_second * y,
        sh_second * z,
        -sh_second * x,
        sh_third[0] * x * y,
        sh_third[1] * y * z,
        sh_third[2] * (2.0 * zz - xx - yy),
        sh_third[3] * x * z,
        sh_third[4] * (xx - yy),
        sh_fourth[0] * y * (3.0 * xx - yy),
        sh_fourth[1] * x * y * z,
        sh_fourth[2] * y * (4.0 * zz - xx - yy),
        sh_fourth[3] * z * (2.0 * zz - 3.0 * xx - 3.0 * yy),
        sh_fourth[4] * x * (4.0 * zz - xx - yy),
        sh_fourth[5] * z * (xx - yy),
        sh_fourth[6] * x * (xx - 3.0 * yy),
    ]


def shape_matrix(log_scales, quat):
    w, x, y, z = quat
    norm = jnp.sqrt(w * w + x * x + y * y + z * z)
    w, x, y, z = w / norm, x / norm, y / norm, z / norm
    rotation = (
        (1.0 - 2.0 * (y * y + z * z), 2.0 * (x * y - w * z), 2.0 * (x * z + w * y)),
        (2.0 * (x * y + w * z), 1.0 - 2.0 * (x * x + z * z), 2.0 * (y * z - w * x)),
        (2.0 * (x * z - w * y), 2.0 * (y * z + w * x), 1.0 - 2.0 * (x * x + y * y)),
    )
    stretch = [jnp.exp(v) for v in log_scales]
    return [[rotation[r][c] * stretch[c] for c in range(3)] for r in range(3)]


def swap_groups(vregs):
    vregs = list(vregs)
    group = lax.broadcasted_iota(jnp.int32, (8, LANES), 1) // CAP
    for bit in (1, 2, 4):
        low = (group & bit) == 0
        for i in range(8):
            if i & bit:
                continue
            a, b = vregs[i], vregs[i + bit]
            vregs[i] = jnp.where(low, a, pltpu.roll(b, CAP * bit, 1))
            vregs[i + bit] = jnp.where(low, pltpu.roll(a, LANES - CAP * bit, 1), b)
    return vregs


def lane_take(table, lanes):
    return jnp.take_along_axis(table, lanes, axis=1, mode="promise_in_bounds")


def halves(value):
    high = value.astype(bf16)
    return high, (value - high.astype(f32)).astype(bf16)


def dot(a, b):
    return lax.dot_general(a, b, (((1,), (0,)), ((), ())), preferred_element_type=f32)


def dot_t(a, b):
    return lax.dot_general(a, b, (((1,), (1,)), ((), ())), preferred_element_type=f32)


PROJECT_CHUNK = 256


def ask_kernel(wanted, out):
    padded = jnp.concatenate([wanted[...], jnp.zeros((LANES, LANES - N_TILE), jnp.int32)], axis=1)
    turned = jnp.transpose(padded)
    for b in range(N_TILE):
        out[8 * b : 8 * b + 8, :] = jnp.broadcast_to(turned[b : b + 1, :], (8, LANES))


def asked_lanes(asked, my_img):
    group = lax.broadcasted_iota(jnp.int32, (8, LANES), 1) // CAP
    base = LANES - CAP * my_img
    result = []
    for q in range(4):
        total = None
        for k in range(8):
            piece = pltpu.roll(asked[8 * (8 * q + k) : 8 * (8 * q + k) + 8, :], (base + CAP * k) & (LANES - 1), 1)
            total = piece if k == 0 else jnp.where(group == k, piece, total)
        result.append(total)
    return result


def project(means, log_scales, quat_w, quat_v, opacity, sh, cam, out, harm):
    column = [jnp.broadcast_to(cam[:, m : m + 1], (N_IMG, PROJECT_CHUNK)) for m in range(8)]

    def chunk(h, carry):
        at = pl.ds(pl.multiple_of(h * PROJECT_CHUNK, PROJECT_CHUNK), PROJECT_CHUNK)
        mean = [means[c : c + 1, at] for c in range(3)]
        quat = [quat_w[0:1, at]] + [quat_v[c : c + 1, at] for c in range(3)]
        m = shape_matrix([log_scales[c : c + 1, at] for c in range(3)], quat)
        for row in range(2):
            a = column[3 * row : 3 * row + 3]
            out[row, :, at] = a[0] * mean[0] + a[1] * mean[1] + a[2] * mean[2] + column[6 + row]
        p = [
            [
                sum(column[3 * row + r] * m[r][c] for r in range(3))
                for c in range(3)
            ]
            for row in range(2)
        ]
        s00 = p[0][0] * p[0][0] + p[0][1] * p[0][1] + p[0][2] * p[0][2] + dilation
        s01 = p[0][0] * p[1][0] + p[0][1] * p[1][1] + p[0][2] * p[1][2]
        s11 = p[1][0] * p[1][0] + p[1][1] * p[1][1] + p[1][2] * p[1][2] + dilation
        det = s00 * s11 - s01 * s01
        out[2, :, at] = s11 / det
        out[3, :, at] = -s01 / det
        out[4, :, at] = s00 / det
        base = 1.0 / (1.0 + jnp.exp(-opacity[0:1, at]))
        out[5, :, at] = jnp.broadcast_to(base, (N_IMG, PROJECT_CHUNK))
        for c in range(3):
            out[9 + c, :, at] = jnp.broadcast_to(mean[c], (N_IMG, PROJECT_CHUNK))
            for row in range(2):
                out[12 + 3 * row + c, :, at] = (
                    m[c][0] * p[row][0] + m[c][1] * p[row][1] + m[c][2] * p[row][2]
                )
        for base_row, first, start in ((6, 0, 0.5), (18, 16, 0.0), (21, 32, 0.0)):
            total = [jnp.full((N_IMG, PROJECT_CHUNK), start, f32) for _ in range(3)]
            for b in range(16):
                y = jnp.concatenate([harm[first + b]] * (PROJECT_CHUNK // LANES), axis=1)
                for k in range(3):
                    total[k] = total[k] + y * sh[16 * k + b : 16 * k + b + 1, at]
            for k in range(3):
                out[base_row + k, :, at] = total[k]
        return carry

    lax.fori_loop(0, OWNED // PROJECT_CHUNK, chunk, 0)


def pick_kernel(
    meta, asked, means, log_scales, quat_w, quat_v, opacity, sh, cam, out, conic, table, feats, harm
):
    polar = jnp.broadcast_to(cam[:, 8:9], (N_IMG, LANES))
    azimuth = jnp.broadcast_to(cam[:, 9:10], (N_IMG, LANES))
    one, zero = jnp.ones_like(polar), jnp.zeros_like(polar)
    values, d_polar = jax.jvp(harmonics_of, (polar, azimuth), (one, zero))
    d_azimuth = jax.jvp(harmonics_of, (polar, azimuth), (zero, one))[1]
    lanes = lax.broadcasted_iota(jnp.int32, (N_IMG, LANES), 1)
    packed = jnp.zeros((N_IMG, LANES), f32)
    for b in range(16):
        harm[b] = values[b]
        harm[16 + b] = d_polar[b]
        harm[32 + b] = d_azimuth[b]
        packed = jnp.where(lanes == b, values[b], packed)
    table[...] = packed
    project(means, log_scales, quat_w, quat_v, opacity, sh, cam, feats, harm)
    for f in range(4):
        conic[f] = feats[2 + f]
    index = asked_lanes(asked, meta[TILES_HERE + 1])
    low = [v & (LANES - 1) for v in index]
    high = [v >> 7 for v in index]
    for g in range(FEAT_ROWS):
        for q in range(4):
            picked = []
            for f in range(8):
                value = None
                for h in range(OWNED // LANES):
                    found = lane_take(feats[8 * g + f, :, h * LANES : (h + 1) * LANES], low[q])
                    value = found if h == 0 else jnp.where(high[q] == h, found, value)
                picked.append(value)
            rows = swap_groups(picked)
            for k in range(8):
                out[pl.ds(FEAT_ROWS * 8 * (8 * q + k) + g, 8, stride=FEAT_ROWS), :] = rows[k]


def render_kernel(
    meta,
    rows,
    lists,
    cot,
    image,
    out,
    tab,
    feat,
    grads,
    slot,
    upper,
    lower,
    al_s,
    lk_s,
    lb_s,
    s_s,
    w_s,
    sw_s,
):
    tile_base = meta[TILES_HERE] * TILES_HERE
    for g in range(FEAT_ROWS):
        for q in range(4):
            pieces = [
                rows[pl.ds(FEAT_ROWS * 8 * (8 * q + k) + g, 8, stride=FEAT_ROWS), :] for k in range(8)
            ]
            pieces = swap_groups(pieces)
            for f in range(8):
                tab[8 * g + f, 8 * q : 8 * q + 8, :] = pieces[f]
    entry_lane = [lists[:, h * LANES : (h + 1) * LANES] & (LANES - 1) for h in range(2)]
    entry_chunk = []
    for h in range(2):
        s = lists[:, h * LANES : (h + 1) * LANES]
        entry_chunk.append(((s >> 7) & 3) * 8 + (s >> 9))

    def gather(ch, carry):
        new = list(carry)
        for h in range(2):
            hit = entry_chunk[h] == ch
            for f in range(N_USED):
                row = jnp.broadcast_to(tab[f, pl.ds(ch, 1), :], (8, LANES))
                new[2 * f + h] = jnp.where(hit, lane_take(row, entry_lane[h]), carry[2 * f + h])
        return tuple(new)

    zero = jnp.zeros((8, LANES), f32)
    found = lax.fori_loop(0, 32, gather, tuple([zero] * (2 * N_USED)), unroll=8)
    for f in range(N_USED):
        for h in range(2):
            feat[f, :, h * LANES : (h + 1) * LANES] = found[2 * f + h]
    ri = lax.broadcasted_iota(jnp.int32, (LIST, LIST), 0)
    ci = lax.broadcasted_iota(jnp.int32, (LIST, LIST), 1)
    up = (ri < ci).astype(f32).astype(bf16)
    lo = (ri > ci).astype(f32).astype(bf16)
    for part in range(2):
        upper[part * LIST : (part + 1) * LIST, :] = up
        lower[part * LIST : (part + 1) * LIST, :] = lo
    slot[...] = jnp.zeros_like(slot)
    lane = lax.broadcasted_iota(jnp.int32, (1, LIST), 1)
    px = lax.broadcasted_iota(jnp.int32, (8, LIST), 0).astype(f32) - 7.5
    ch_iota = lax.broadcasted_iota(jnp.int32, (32, LIST), 0)
    lane_iota = lax.broadcasted_iota(jnp.int32, (LANES, LIST), 0)

    def row8(v):
        return jnp.broadcast_to(v, (8, LIST))

    def pair(pair_index, carry):
        tiles = [2 * pair_index, 2 * pair_index + 1]
        state = []
        for p in range(2):
            j = tiles[p]
            number = tile_base + j
            centre_x = (TILE_SIDE * (number % TW)).astype(f32) + (0.5 * TILE_SIDE - 0.5 * TILE_SIDE * TW)
            centre_y = (TILE_SIDE * (number // TW)).astype(f32) + (0.5 * TILE_SIDE - 0.5 * TILE_SIDE * TW)
            at = pl.ds(j, 1)
            ux = feat[0, at, :] - centre_x
            uy = row8(feat[1, at, :] - centre_y)
            ca, cb, cc = feat[2, at, :], feat[3, at, :], feat[4, at, :]
            op = row8(jnp.where(lane < meta[j], feat[5, at, :], 0.0))
            cc = row8(cc * (-0.5 * LOG2E))
            ux, na, nb = row8(ux), row8(ca * (-0.5 * LOG2E)), row8(cb * (-LOG2E))
            dx = [px - ux, px + (8.0 - ux)]
            na = [na * d * d for d in dx]
            nb = [nb * d for d in dx]
            colours = jnp.concatenate([feat[6 + k, at, :] for k in range(3)], axis=0)
            cots = jnp.concatenate([cot[k, at, :] for k in range(3)], axis=0)
            col_h, col_l, cot_h, cot_l = [v.astype(f32) for v in halves(colours) + halves(cots)]
            pad = jnp.zeros((4, LIST), f32)
            cot_k = jnp.concatenate([cot_h, cot_h, cot_l, cot_l, pad], axis=0)
            col_k = jnp.concatenate([col_h, col_l, col_h, col_l, pad], axis=0).astype(bf16)
            s_s[p] = dot(jnp.transpose(cot_k).astype(bf16), col_k)
            for py in range(TILE_SIDE):
                r = slice(TILE_SIDE * py, TILE_SIDE * (py + 1))
                dy = (py - 7.5) - uy
                cy = cc * dy * dy
                alpha = jnp.concatenate(
                    [op * jnp.exp2((na[h] + cy) + nb[h] * dy) for h in range(2)], axis=0
                )
                al_s[p, r, :] = alpha
                hi, low = halves(jnp.log2(1.0 - alpha))
                lk_s[p, r, 0:LIST] = hi
                lk_s[p, r, LIST : 2 * LIST] = low
            lb_s[p] = dot(lk_s[p], upper[...])
            state.append((at, uy, dx, col_h, col_l, cot_h, cot_l))
        for p in range(2):
            for py in range(TILE_SIDE):
                r = slice(TILE_SIDE * py, TILE_SIDE * (py + 1))
                w = al_s[p, r, :] * jnp.exp2(lb_s[p, r, :])
                hi, low = halves(w)
                w_s[p, r, :] = hi
                w_s[p, PIX + TILE_SIDE * py : PIX + TILE_SIDE * (py + 1), :] = low
                sw = s_s[p, r, :] * w
                s_s[p, r, :] = sw
                hi, low = halves(sw)
                sw_s[p, r, 0:LIST] = hi
                sw_s[p, r, LIST : 2 * LIST] = low
            lb_s[p] = dot(sw_s[p], lower[...])
        for p in range(2):
            at, uy, dx, col_h, col_l, cot_h, cot_l = state[p]
            pad2 = jnp.zeros((2, LIST), f32)
            col_rows = jnp.concatenate([col_h, col_l, pad2], axis=0).astype(bf16)
            shown = dot_t(col_rows, w_s[p, 0:PIX, :]) + dot_t(col_rows, w_s[p, PIX : 2 * PIX, :])
            for k in range(3):
                image[k, at, :] = shown[k : k + 1, :] + shown[3 + k : 4 + k, :]
            cot_rows = jnp.concatenate([cot_h, cot_l, pad2], axis=0).astype(bf16)
            gcol = dot(jnp.concatenate([cot_rows, cot_rows], axis=1), w_s[p])
            acc = [[None, None] for _ in range(3)]
            for py in range(TILE_SIDE):
                dy = (py - 7.5) - uy
                for h in range(2):
                    r = slice(TILE_SIDE * py + 8 * h, TILE_SIDE * py + 8 * h + 8)
                    alpha = al_s[p, r, :]
                    g = s_s[p, r, :] - lb_s[p, r, :] * (alpha / (1.0 - alpha))
                    gy = g * dy
                    for n, v in enumerate((g, gy, gy * dy)):
                        acc[n][h] = v if py == 0 else acc[n][h] + v

            def down(a, b):
                return jnp.sum(a + b, axis=0, keepdims=True)

            xg = [dx[h] * acc[0][h] for h in range(2)]
            grad = [
                down(acc[0][0], acc[0][1]),
                down(xg[0], xg[1]),
                down(acc[1][0], acc[1][1]),
                down(dx[0] * xg[0], dx[1] * xg[1]),
                down(dx[0] * acc[1][0], dx[1] * acc[1][1]),
                down(acc[2][0], acc[2][1]),
            ] + [gcol[k : k + 1, :] + gcol[3 + k : 4 + k, :] for k in range(3)]
            s = lists[at, :]
            chunk_hit = ch_iota == (((s >> 7) & 3) * 8 + (s >> 9))
            for f in range(N_GRAD):
                hi, low = halves(jnp.where(chunk_hit, grad[f], 0.0))
                grads[p, 32 * f : 32 * (f + 1), 0:LIST] = hi
                grads[p, 32 * f : 32 * (f + 1), LIST : 2 * LIST] = low
            lane_hit = (lane_iota == (s & (LANES - 1))).astype(f32).astype(bf16)
            slot[...] += dot_t(grads[p], jnp.concatenate([lane_hit, lane_hit], axis=1))
        return carry

    lax.fori_loop(0, TILES_HERE // 2, pair, 0)

    terms = [jnp.zeros((8, LANES), f32) for _ in range(10)]
    for q in range(4):
        r = slice(8 * q, 8 * q + 8)
        ca, cb, cc = tab[2, r, :], tab[3, r, :], tab[4, r, :]
        gr = [slot[32 * f + 8 * q : 32 * f + 8 * q + 8, :] for f in range(N_GRAD)]
        du = (ca * gr[1] + cb * gr[2], cb * gr[1] + cc * gr[2])
        h00, h01, h11 = conic_pull(ca, cb, cc, gr[3], gr[4], gr[5])
        for c in range(3):
            mean, n0, n1 = tab[9 + c, r, :], tab[12 + c, r, :], tab[15 + c, r, :]
            terms[c] += du[0] * mean + 2.0 * (h00 * n0 + h01 * n1)
            terms[3 + c] += du[1] * mean + 2.0 * (h01 * n0 + h11 * n1)
            terms[8] += gr[6 + c] * tab[18 + c, r, :]
            terms[9] += gr[6 + c] * tab[21 + c, r, :]
        terms[6] += du[0]
        terms[7] += du[1]
    lanes = lax.broadcasted_iota(jnp.int32, (8, LANES), 1)
    share = jnp.zeros((8, LANES), f32)
    for m in range(10):
        total = jnp.sum(jnp.sum(terms[m], axis=0, keepdims=True), axis=1, keepdims=True)
        share = jnp.where(lanes == CAP + m, jnp.broadcast_to(total, (8, LANES)), share)
    for q in range(4):
        pieces = swap_groups([slot[32 * f + 8 * q : 32 * f + 8 * q + 8, :] for f in range(8)])
        last = slot[32 * 8 + 8 * q : 32 * 8 + 8 * q + 8, :]
        for k in range(8):
            first_row = GRAD_ROWS * 8 * (8 * q + k)
            out[pl.ds(first_row, 8, stride=GRAD_ROWS), :] = pieces[k]
            moved = last if k == 0 else pltpu.roll(last, LANES - CAP * k, 1)
            out[pl.ds(first_row + 1, 8, stride=GRAD_ROWS), :] = jnp.where(lanes < CAP, moved, share)


def conic_pull(ca, cb, cc, qxx, qxy, qyy):
    t00, t01 = ca * qxx + cb * qxy, ca * qxy + cb * qyy
    t10, t11 = cb * qxx + cc * qxy, cb * qxy + cc * qyy
    return 0.5 * (t00 * ca + t01 * cb), 0.5 * (t00 * cb + t01 * cc), 0.5 * (t10 * cb + t11 * cc)


PULL_CHUNK = 128


def pull_kernel(
    meta, returned, asked, conic, table, log_scales, quat_w, quat_v, cam, out, cam_out, row_s, idx_s, lhs_s, sum_s, gc_s
):
    index = asked_lanes(asked, meta[TILES_HERE + 1])
    for q in range(4):
        idx_s[:, q * LANES : (q + 1) * LANES] = index[q]
    group = lax.broadcasted_iota(jnp.int32, (8, LANES), 1) // CAP
    camera = jnp.zeros((8, LANES), f32)
    for q in range(4):
        pieces = [returned[pl.ds(GRAD_ROWS * 8 * (8 * q + k), 8, stride=GRAD_ROWS), :] for k in range(8)]
        pieces = swap_groups(pieces)
        for f in range(8):
            row_s[f, :, q * LANES : (q + 1) * LANES] = pieces[f]
        last = None
        for k in range(8):
            piece = returned[pl.ds(GRAD_ROWS * 8 * (8 * q + k) + 1, 8, stride=GRAD_ROWS), :]
            camera = camera + piece
            last = piece if k == 0 else jnp.where(group == k, pltpu.roll(piece, CAP * k, 1), last)
        row_s[8, :, q * LANES : (q + 1) * LANES] = last
    cam_out[...] = pltpu.roll(camera, LANES - CAP, 1)[:, 0:10]

    slots = N_TILE * CAP
    high_iota = lax.broadcasted_iota(jnp.int32, (16, slots), 0)
    lane_iota = lax.broadcasted_iota(jnp.int32, (LANES, slots), 0)

    def image(i, carry):
        at = pl.ds(i, 1)
        s = idx_s[at, :]
        high_hit = high_iota == (s >> 7)
        lane_hit = (lane_iota == (s & (LANES - 1))).astype(f32).astype(bf16)
        for f in range(N_GRAD):
            hi, low = halves(jnp.where(high_hit, row_s[f, at, :], 0.0))
            lhs_s[16 * f : 16 * (f + 1), 0:slots] = hi
            lhs_s[16 * f : 16 * (f + 1), slots : 2 * slots] = low
        sum_s[pl.ds(pl.multiple_of(i * (16 * N_GRAD), 16), 16 * N_GRAD), :] = dot_t(
            lhs_s[...], jnp.concatenate([lane_hit, lane_hit], axis=1)
        )
        return carry

    lax.fori_loop(0, N_IMG, image, 0)

    column = [jnp.broadcast_to(cam[:, m : m + 1], (N_IMG, PULL_CHUNK)) for m in range(6)]

    def chunk(h, carry):
        at = pl.ds(pl.multiple_of(h * PULL_CHUNK, PULL_CHUNK), PULL_CHUNK)
        gr = [sum_s[pl.ds(16 * f + h, 8, stride=16 * N_GRAD), :] for f in range(N_GRAD)]
        ca, cb, cc = conic[0, :, at], conic[1, :, at], conic[2, :, at]
        du = (ca * gr[1] + cb * gr[2], cb * gr[1] + cc * gr[2])
        h00, h01, h11 = conic_pull(ca, cb, cc, gr[3], gr[4], gr[5])
        a0, a1 = column[0:3], column[3:6]

        def over_images(v):
            return jnp.sum(v, axis=0, keepdims=True)

        for c in range(3):
            out[c : c + 1, at] = over_images(a0[c] * du[0] + a1[c] * du[1])
        t0 = [h00 * a0[c] + h01 * a1[c] for c in range(3)]
        t1 = [h01 * a0[c] + h11 * a1[c] for c in range(3)]
        v = [[None] * 3 for _ in range(3)]
        for c in range(3):
            for d in range(c, 3):
                v[c][d] = v[d][c] = over_images(t0[c] * a0[d] + t1[c] * a1[d])
        ls = [log_scales[c : c + 1, at] for c in range(3)]
        quat = [quat_w[0:1, at]] + [quat_v[c : c + 1, at] for c in range(3)]
        m, pull = jax.vjp(shape_matrix, ls, quat)
        dm = [[2.0 * sum(v[r][d] * m[d][c] for d in range(3)) for c in range(3)] for r in range(3)]
        dls, dquat = pull(dm)
        for c in range(3):
            out[3 + c : 4 + c, at] = dls[c]
        for c in range(4):
            out[6 + c : 7 + c, at] = dquat[c]
        base = conic[3, 0:1, at]
        out[10:11, at] = over_images(gr[0]) * (1.0 - base)
        for k in range(3):
            gc_s[8 * k : 8 * k + 8, at] = gr[6 + k]
        return carry

    lax.fori_loop(0, OWNED // PULL_CHUNK, chunk, 0)

    y_h, y_l = halves(jnp.transpose(table[...])[0:16, :])
    y_all = jnp.concatenate([y_h.astype(f32), y_h.astype(f32), y_l.astype(f32), y_l.astype(f32)], axis=1).astype(bf16)
    for k in range(3):
        g_h, g_l = halves(gc_s[8 * k : 8 * k + 8, :])
        g_all = jnp.concatenate([g_h.astype(f32), g_l.astype(f32), g_h.astype(f32), g_l.astype(f32)], axis=0).astype(bf16)
        out[11 + 16 * k : 27 + 16 * k, :] = dot(y_all, g_all)


def whole(memory=pltpu.VMEM):
    return pl.BlockSpec(memory_space=memory)


def call(kernel, name, out_shape, scratch, n_in, smem=0):
    return pl.pallas_call(
        kernel,
        name=name,
        out_shape=out_shape,
        in_specs=[whole(pltpu.SMEM)] * smem + [whole()] * (n_in - smem),
        out_specs=jax.tree.map(lambda _: whole(), out_shape),
        scratch_shapes=scratch,
        compiler_params=pltpu.CompilerParams(vmem_limit_bytes=32 << 20),
    )


def exchange(array):
    return lax.all_to_all(array, ORDER, split_axis=0, concat_axis=0, tiled=True)


def exchange_rows(array, rows):
    shape = array.shape
    return exchange(array.reshape(-1, 1, rows * LANES)).reshape(shape)


def local(
    means, log_scales, quat_w, quat_v, opacity, sh_coeffs, cameras, requests, lists, counts, image_cot
):
    devices = N_IMG * N_TILE
    meta = jnp.concatenate(
        [counts[0], jnp.stack([lax.axis_index("tile"), lax.axis_index("img")]).astype(jnp.int32)]
    )
    by_owner = jnp.transpose(requests.reshape(N_IMG, N_TILE, CAP), (0, 2, 1)).reshape(N_IMG * CAP, N_TILE)
    wanted = call(ask_kernel, "ask", jax.ShapeDtypeStruct((devices, LANES), jnp.int32), [], 1)(by_owner)
    wanted, meta = lax.optimization_barrier((wanted, meta))
    asked = exchange_rows(wanted, 1)
    packed, conic, table = call(
        pick_kernel,
        "pick",
        (
            jax.ShapeDtypeStruct((FEAT_ROWS * devices, LANES), f32),
            jax.ShapeDtypeStruct((4, N_IMG, OWNED), f32),
            jax.ShapeDtypeStruct((N_IMG, LANES), f32),
        ),
        [pltpu.VMEM((N_FEAT, N_IMG, OWNED), f32), pltpu.VMEM((48, N_IMG, LANES), f32)],
        9,
        smem=1,
    )(meta, asked, means, log_scales, quat_w, quat_v, opacity, sh_coeffs, cameras)
    rows = exchange_rows(packed, FEAT_ROWS)
    rendered, slot_grads = call(
        render_kernel,
        "render",
        (
            jax.ShapeDtypeStruct((3, TILES_HERE, PIX), f32),
            jax.ShapeDtypeStruct((GRAD_ROWS * devices, LANES), f32),
        ),
        [
            pltpu.VMEM((N_FEAT, 32, LANES), f32),
            pltpu.VMEM((N_USED, 8, LIST), f32),
            pltpu.VMEM((2, 32 * N_GRAD, 2 * LIST), bf16),
            pltpu.VMEM((32 * N_GRAD, LANES), f32),
            pltpu.VMEM((2 * LIST, LIST), bf16),
            pltpu.VMEM((2 * LIST, LIST), bf16),
            pltpu.VMEM((2, PIX, LIST), f32),
            pltpu.VMEM((2, PIX, 2 * LIST), bf16),
            pltpu.VMEM((2, PIX, LIST), f32),
            pltpu.VMEM((2, PIX, LIST), f32),
            pltpu.VMEM((2, 2 * PIX, LIST), bf16),
            pltpu.VMEM((2, PIX, 2 * LIST), bf16),
        ],
        4,
        smem=1,
    )(meta, rows, lists[0], image_cot[0])
    returned = exchange_rows(slot_grads, GRAD_ROWS)
    param_grad, camera_grad = call(
        pull_kernel,
        "pull",
        (
            jax.ShapeDtypeStruct((59, OWNED), f32),
            jax.ShapeDtypeStruct((N_IMG, 10), f32),
        ),
        [
            pltpu.VMEM((N_GRAD, N_IMG, N_TILE * CAP), f32),
            pltpu.VMEM((N_IMG, N_TILE * CAP), jnp.int32),
            pltpu.VMEM((16 * N_GRAD, 2 * N_TILE * CAP), bf16),
            pltpu.VMEM((N_IMG * 16 * N_GRAD, LANES), f32),
            pltpu.VMEM((24, OWNED), f32),
        ],
        9,
        smem=1,
    )(meta, returned, asked, conic, table, log_scales, quat_w, quat_v, cameras)
    return (rendered[None], param_grad, camera_grad)


def solution(mesh):
    own = P(None, ALL)
    return jax.shard_map(
        local,
        mesh=mesh,
        in_specs=(
            own,
            own,
            own,
            own,
            own,
            own,
            P(),
            P("img", "tile", None, None, None),
            P("img", "tile", None),
            P("img", "tile"),
            P("img", None, "tile", None),
        ),
        out_specs=(P("img", None, "tile", None), own, P()),
        check_vma=False,
    )
```

time: 101 us -> 95.4 us (0.945)
  blocking collectives: 21.2 us -> 72.3 us
  starting transfers between devices: 25.4 us -> 0 us
  waiting for transfers between devices: 21.1 us -> 0 us
  local copies, waits for them, and re-layouts: 6.15 us -> 1.67 us
  Pallas kernels: 23.2 us -> 19.7 us
  other arithmetic: 2.71 us -> 0.73 us
    all_to_all x1 -> x3, blocking collectives: 21.2 us -> 72.3 us  [exchange(): return lax.all_to_all(array, ORDER, split_axis=0, concat_axis=0, tiled=True)]
    all_to_all x2 -> x0, starting transfers between devices: 25.4 us -> none  [exchange(): return lax.all_to_all(array, ALL, split_axis=0, concat_axis=0, tiled=True)]
    all_to_all x2 -> x0, waiting for transfers between devices: 21.1 us -> none  [exchange(): return lax.all_to_all(array, ALL, split_axis=0, concat_axis=0, tiled=True)]
    pallas_call x1, Pallas kernels: 12.7 us -> 8.3 us  [local(): call(render_kernel, 'render', (jax.ShapeDtypeStruct((3, TILES_HERE, PIX),...]
    unnamed x25 -> x20, local copies, waits for them, and re-layouts: 4.67 us -> 1.67 us
    add_any x3 -> x0, other arithmetic: 2.64 us -> none  [the longest x1 0.94 us: harmonics_of(): sh_fourth[4] * x * (4.0 * zz - xx - yy)]
  transfers between devices with their start and end apart: 2 -> 0, of which waited for: 2 -> 0; matrix products, arithmetic and copies ran while one was open for 3% -> 0% of each run, Pallas kernels for 1% -> 0%
where the time goes in v2:
time: 95.4 us; the launch traced here: 95.1 us
  blocking collectives  72.3 us (76%)
  Pallas kernels  19.7 us (21%)
  local copies, waits for them, and re-layouts  1.67 us (2%)
    all_to_all x3, blocking collectives, exchange(): return lax.all_to_all(array, ORDER, split_axis=0, concat_axis=0, tiled=True)  72.3 us
    pallas_call x1, Pallas kernels, local(): call(render_kernel, 'render', (jax.ShapeDtypeStruct((3, TILES_HERE, PIX),...  8.3 us
    pallas_call x1, Pallas kernels, local(): call(pick_kernel, 'pick', (jax.ShapeDtypeStruct((FEAT_ROWS * devices, LAN...  6.02 us
    pallas_call x1, Pallas kernels, local(): call(pull_kernel, 'pull', (jax.ShapeDtypeStruct((59, OWNED), f32), jax.Sh...  5.28 us

profile of v2, /device:TPU:1, one launch (start us, length us, event | category | flops | bytes accessed | tf_op | source)
XLA Modules:
  0.0 95.1 jit_solution(723337686178016169)
XLA Ops:
  0.6 0.0 copy-start
  0.6 0.0 copy-start.3
  0.7 0.9 copy-done.3
  1.5 0.1 ask.1
  1.6 0.7 pad_add_fusion.meta
  2.4 0.0 copy-start.1
  2.4 0.0 copy-start.2
  2.4 0.0 copy-start.4
  2.4 0.0 copy-start.7
  2.4 0.0 copy-start.8
  2.4 28.5 %all_to_all.15 = s32[256,1,128]{2,1,0:T(1,128)S(1)} all-to-all(s32[256,1,128]{2,1,0:T(1,128)S(1)} %bitcast.23), channel_id=1, replica_groups=mesh['img'=8,'tile'=32] {'tile','img'}, dimensions={0} | all-to-all | bytes 262144 | tf_op jit(solution)/shard_map/all_to_all | solution.py:528
  30.8 0.0 copy-done
  30.8 0.0 copy-done.1
  30.8 0.0 copy-done.2
  30.8 0.0 copy-done.4
  30.9 0.0 copy-done.7
  30.9 0.0 copy-done.8
  30.9 0.0 copy-start.5
  30.9 0.7 copy-done.5
  31.6 6.0 %pick.1 = (f32[768,128]{1,0:T(8,128)S(1)}, f32[4,8,2048]{2,1,0:T(8,128)S(1)}, f32[8,128]{1,0:T(8,128)S(1)}) custom-call(s32[10]{0:T(128)S(1)} %pad_add_fusion.meta, s32[256,128]{1,0:T(8,128)S(1)} %bitcast.20, f32[3,2048]{1,0:T(4,128)S(1)} %copy-done.5, f32[3,2048]{1,0:T(4,128)S(1)} %copy-done.1, f32[1,2048]{1,0:T(1,128)S(1)} %copy-done.4, ...), custom_call_target="tpu_custom_call" | custom-call | tf_op jit(solution)/shard_map/pick/pallas_call | solution.py:547
  37.7 0.0 copy-start.6
  37.7 0.0 copy-start.9
  37.7 22.6 %all_to_all.16 = f32[256,1,384]{2,1,0:T(1,128)S(1)} all-to-all(f32[256,1,384]{2,1,0:T(1,128)S(1)} %bitcast.24), channel_id=1, replica_groups=mesh['img'=8,'tile'=32] {'tile','img'}, dimensions={0} | all-to-all | bytes 786432 | tf_op jit(solution)/shard_map/all_to_all | solution.py:528
  60.2 0.0 copy-done.6
  60.2 0.0 copy-done.9
  60.2 8.3 %render.1 = (f32[3,8,256]{2,1,0:T(8,128)}, f32[512,128]{1,0:T(8,128)S(1)}) custom-call(s32[10]{0:T(128)S(1)} %pad_add_fusion.meta, f32[768,128]{1,0:T(8,128)S(1)} %bitcast.19, s32[8,256]{1,0:T(8,128)S(1)} %bitcast.28, f32[3,8,256]{2,1,0:T(8,128)S(1)} %bitcast.27), custom_call_target="tpu_custom_call" | custom-call | tf_op jit(solution)/shard_map/render/pallas_call | solution.py:560
  68.5 21.3 %all_to_all.17 = f32[256,1,256]{2,1,0:T(1,128)S(1)} all-to-all(f32[256,1,256]{2,1,0:T(1,128)S(1)} %bitcast.25), channel_id=1, replica_groups=mesh['img'=8,'tile'=32] {'tile','img'}, dimensions={0} | all-to-all | bytes 524288 | tf_op jit(solution)/shard_map/all_to_all | solution.py:528
  89.8 5.3 %pull.1 = (f32[59,2048]{1,0:T(8,128)}, f32[8,10]{1,0:T(8,128)}) custom-call(s32[10]{0:T(128)S(1)} %pad_add_fusion.meta, f32[512,128]{1,0:T(8,128)S(1)} %bitcast.22, s32[256,128]{1,0:T(8,128)S(1)} %bitcast.21, f32[4,8,2048]{2,1,0:T(8,128)S(1)} %get-tuple-element.17.conic, f32[8,128]{1,0:T(8,128)S(1)} %get-tuple-element.18.table, f32[3,2048]{1,0:T(4,128)S(1)} %copy-done.1, ...), custom_call_target="tpu_custom_call" | custom-call | tf_op jit(solution)/shard_map/pull/pallas_call | solution.py:585
Async XLA Ops:
  0.6 30.2 %copy-start = (f32[48,2048]{1,0:T(8,128)S(1)}, f32[48,2048]{1,0:T(8,128)}, u32[]{:S(2)}) copy-start(f32[48,2048]{1,0:T(8,128)} %sh.1) | copy-start | bytes 1179652
  0.6 0.9 copy-start.3
  2.4 28.5 %copy-start.1 = (f32[3,2048]{1,0:T(4,128)S(1)}, f32[3,2048]{1,0:T(4,128)}, u32[]{:S(2)}) copy-start(f32[3,2048]{1,0:T(4,128)} %log_scales.3) | copy-start | bytes 73732
  2.4 28.5 %copy-start.2 = (f32[3,2048]{1,0:T(4,128)S(1)}, f32[3,2048]{1,0:T(4,128)}, u32[]{:S(2)}) copy-start(f32[3,2048]{1,0:T(4,128)} %quat_v.3) | copy-start | bytes 73732
  2.4 28.5 %copy-start.4 = (f32[1,2048]{1,0:T(1,128)S(1)}, f32[1,2048]{1,0:T(1,128)}, u32[]{:S(2)}) copy-start(f32[1,2048]{1,0:T(1,128)} %quat_w.3) | copy-start | bytes 24580
  2.4 28.5 %copy-start.7 = (f32[8,10]{1,0:T(8,128)S(1)}, f32[8,10]{1,0:T(8,128)}, u32[]{:S(2)}) copy-start(f32[8,10]{1,0:T(8,128)} %cam.3) | copy-start | bytes 964
  2.4 28.5 %copy-start.8 = (f32[1,2048]{1,0:T(1,128)S(1)}, f32[1,2048]{1,0:T(1,128)}, u32[]{:S(2)}) copy-start(f32[1,2048]{1,0:T(1,128)} %opacity.1) | copy-start | bytes 24580
  30.9 0.8 copy-start.5
  37.7 22.6 %copy-start.6 = (f32[1,3,8,256]{3,2,1,0:T(8,128)S(1)}, f32[1,3,8,256]{3,2,1,0:T(8,128)}, u32[]{:S(2)}) copy-start(f32[1,3,8,256]{3,2,1,0:T(8,128)} %param.21) | copy-start | bytes 73732
  37.7 22.6 %copy-start.9 = (s32[1,8,256]{2,1,0:T(8,128)S(1)}, s32[1,8,256]{2,1,0:T(8,128)}, u32[]{:S(2)}) copy-start(s32[1,8,256]{2,1,0:T(8,128)} %param.19) | copy-start | bytes 24580

commit v3 on v2

--- a/solution.py
+++ b/solution.py
@@ -86,18 +86,25 @@
     return [[rotation[r][c] * stretch[c] for c in range(3)] for r in range(3)]
 
 
-def swap_groups(vregs):
-    vregs = list(vregs)
+def turn_groups(vregs):
     group = lax.broadcasted_iota(jnp.int32, (8, LANES), 1) // CAP
+    work = [vregs[-k % 8] for k in range(8)]
     for bit in (1, 2, 4):
-        low = (group & bit) == 0
-        for i in range(8):
-            if i & bit:
-                continue
-            a, b = vregs[i], vregs[i + bit]
-            vregs[i] = jnp.where(low, a, pltpu.roll(b, CAP * bit, 1))
-            vregs[i + bit] = jnp.where(low, pltpu.roll(a, LANES - CAP * bit, 1), b)
-    return vregs
+        move = (group & bit) != 0
+        work = [jnp.where(move, work[(k - bit) % 8], work[k]) for k in range(8)]
+    return work
+
+
+def rotate(value, groups):
+    if isinstance(groups, int):
+        shift = CAP * groups % LANES
+        return value if shift == 0 else pltpu.roll(value, shift, 1)
+    return pltpu.roll(value, (CAP * groups) & (LANES - 1), 1)
+
+
+def swap_groups(vregs, turned=0, leave=False):
+    vregs = turn_groups([rotate(v, i + LANES // CAP - turned) for i, v in enumerate(vregs)])
+    return vregs if leave else [rotate(v, -g) for g, v in enumerate(vregs)]
 
 
 def lane_take(table, lanes):
@@ -186,9 +193,7 @@
     lax.fori_loop(0, OWNED // PROJECT_CHUNK, chunk, 0)
 
 
-def pick_kernel(
-    meta, asked, means, log_scales, quat_w, quat_v, opacity, sh, cam, out, conic, table, feats, harm
-):
+def project_kernel(means, log_scales, quat_w, quat_v, opacity, sh, cam, feats, table, harm):
     polar = jnp.broadcast_to(cam[:, 8:9], (N_IMG, LANES))
     azimuth = jnp.broadcast_to(cam[:, 9:10], (N_IMG, LANES))
     one, zero = jnp.ones_like(polar), jnp.zeros_like(polar)
@@ -203,23 +208,29 @@
         packed = jnp.where(lanes == b, values[b], packed)
     table[...] = packed
     project(means, log_scales, quat_w, quat_v, opacity, sh, cam, feats, harm)
-    for f in range(4):
-        conic[f] = feats[2 + f]
-    index = asked_lanes(asked, meta[TILES_HERE + 1])
-    low = [v & (LANES - 1) for v in index]
-    high = [v >> 7 for v in index]
-    for g in range(FEAT_ROWS):
-        for q in range(4):
-            picked = []
-            for f in range(8):
-                value = None
-                for h in range(OWNED // LANES):
-                    found = lane_take(feats[8 * g + f, :, h * LANES : (h + 1) * LANES], low[q])
-                    value = found if h == 0 else jnp.where(high[q] == h, found, value)
-                picked.append(value)
-            rows = swap_groups(picked)
-            for k in range(8):
-                out[pl.ds(FEAT_ROWS * 8 * (8 * q + k) + g, 8, stride=FEAT_ROWS), :] = rows[k]
+
+
+def pick_kernel(meta, asked, feats, out, index):
+    for q, value in enumerate(asked_lanes(asked, meta[TILES_HERE + 1])):
+        for f in range(8):
+            index[8 * q + f] = rotate(value, f)
+
+    def step(n, carry):
+        g, q = n >> 2, n & 3
+        picked = []
+        for f in range(8):
+            here = index[8 * q + f]
+            low, high = here & (LANES - 1), here >> 7
+            value = None
+            for h in range(OWNED // LANES):
+                found = lane_take(feats[8 * g + f, :, h * LANES : (h + 1) * LANES], low)
+                value = found if h == 0 else jnp.where(high == h, found, value)
+            picked.append(value)
+        for k, row in enumerate(turn_groups(picked)):
+            out[pl.ds(FEAT_ROWS * 8 * (8 * q + k) + g, 8, stride=FEAT_ROWS), :] = row
+        return carry
+
+    lax.fori_loop(0, 4 * FEAT_ROWS, step, 0, unroll=4)
 
 
 def render_kernel(
@@ -243,14 +254,19 @@
     sw_s,
 ):
     tile_base = meta[TILES_HERE] * TILES_HERE
-    for g in range(FEAT_ROWS):
-        for q in range(4):
-            pieces = [
-                rows[pl.ds(FEAT_ROWS * 8 * (8 * q + k) + g, 8, stride=FEAT_ROWS), :] for k in range(8)
-            ]
-            pieces = swap_groups(pieces)
-            for f in range(8):
-                tab[8 * g + f, 8 * q : 8 * q + 8, :] = pieces[f]
+    turned = meta[TILES_HERE] & 7
+
+    def sort_rows(n, carry):
+        g, q = n >> 2, n & 3
+        pieces = [
+            rows[pl.ds(FEAT_ROWS * 8 * (8 * q + k) + g, 8, stride=FEAT_ROWS), :] for k in range(8)
+        ]
+        pieces = swap_groups(pieces, turned)
+        for f in range(8):
+            tab[8 * g + f, pl.ds(pl.multiple_of(8 * q, 8), 8), :] = pieces[f]
+        return carry
+
+    lax.fori_loop(0, 4 * FEAT_ROWS, sort_rows, 0, unroll=4)
     entry_lane = [lists[:, h * LANES : (h + 1) * LANES] & (LANES - 1) for h in range(2)]
     entry_chunk = []
     for h in range(2):
@@ -402,14 +418,15 @@
     for m in range(10):
         total = jnp.sum(jnp.sum(terms[m], axis=0, keepdims=True), axis=1, keepdims=True)
         share = jnp.where(lanes == CAP + m, jnp.broadcast_to(total, (8, LANES)), share)
+    group = lanes // CAP
+    shares = [rotate(share, k) for k in range(8)]
     for q in range(4):
-        pieces = swap_groups([slot[32 * f + 8 * q : 32 * f + 8 * q + 8, :] for f in range(8)])
+        pieces = swap_groups([slot[32 * f + 8 * q : 32 * f + 8 * q + 8, :] for f in range(8)], leave=True)
         last = slot[32 * 8 + 8 * q : 32 * 8 + 8 * q + 8, :]
         for k in range(8):
             first_row = GRAD_ROWS * 8 * (8 * q + k)
             out[pl.ds(first_row, 8, stride=GRAD_ROWS), :] = pieces[k]
-            moved = last if k == 0 else pltpu.roll(last, LANES - CAP * k, 1)
-            out[pl.ds(first_row + 1, 8, stride=GRAD_ROWS), :] = jnp.where(lanes < CAP, moved, share)
+            out[pl.ds(first_row + 1, 8, stride=GRAD_ROWS), :] = jnp.where(group == k, last, shares[k])
 
 
 def conic_pull(ca, cb, cc, qxx, qxy, qyy):
@@ -418,29 +435,31 @@
     return 0.5 * (t00 * ca + t01 * cb), 0.5 * (t00 * cb + t01 * cc), 0.5 * (t10 * cb + t11 * cc)
 
 
-PULL_CHUNK = 128
+PULL_CHUNK = 512
 
 
 def pull_kernel(
-    meta, returned, asked, conic, table, log_scales, quat_w, quat_v, cam, out, cam_out, row_s, idx_s, lhs_s, sum_s, gc_s
+    meta, returned, asked, feats, table, log_scales, quat_w, quat_v, cam, out, cam_out, row_s, idx_s, lhs_s, sum_s, gc_s
 ):
     index = asked_lanes(asked, meta[TILES_HERE + 1])
     for q in range(4):
         idx_s[:, q * LANES : (q + 1) * LANES] = index[q]
     group = lax.broadcasted_iota(jnp.int32, (8, LANES), 1) // CAP
+    turned = meta[TILES_HERE] & 7
     camera = jnp.zeros((8, LANES), f32)
     for q in range(4):
         pieces = [returned[pl.ds(GRAD_ROWS * 8 * (8 * q + k), 8, stride=GRAD_ROWS), :] for k in range(8)]
-        pieces = swap_groups(pieces)
+        pieces = swap_groups(pieces, turned)
         for f in range(8):
             row_s[f, :, q * LANES : (q + 1) * LANES] = pieces[f]
         last = None
         for k in range(8):
             piece = returned[pl.ds(GRAD_ROWS * 8 * (8 * q + k) + 1, 8, stride=GRAD_ROWS), :]
             camera = camera + piece
-            last = piece if k == 0 else jnp.where(group == k, pltpu.roll(piece, CAP * k, 1), last)
+            moved = rotate(piece, k + 8 - turned)
+            last = moved if k == 0 else jnp.where(group == k, moved, last)
         row_s[8, :, q * LANES : (q + 1) * LANES] = last
-    cam_out[...] = pltpu.roll(camera, LANES - CAP, 1)[:, 0:10]
+    cam_out[...] = rotate(camera, 7 - turned)[:, 0:10]
 
     slots = N_TILE * CAP
     high_iota = lax.broadcasted_iota(jnp.int32, (16, slots), 0)
@@ -460,14 +479,21 @@
         )
         return carry
 
-    lax.fori_loop(0, N_IMG, image, 0)
+    lax.fori_loop(0, N_IMG, image, 0, unroll=8)
 
     column = [jnp.broadcast_to(cam[:, m : m + 1], (N_IMG, PULL_CHUNK)) for m in range(6)]
 
     def chunk(h, carry):
         at = pl.ds(pl.multiple_of(h * PULL_CHUNK, PULL_CHUNK), PULL_CHUNK)
-        gr = [sum_s[pl.ds(16 * f + h, 8, stride=16 * N_GRAD), :] for f in range(N_GRAD)]
-        ca, cb, cc = conic[0, :, at], conic[1, :, at], conic[2, :, at]
+        parts = PULL_CHUNK // LANES
+        gr = [
+            jnp.concatenate(
+                [sum_s[pl.ds(16 * f + h * parts + e, 8, stride=16 * N_GRAD), :] for e in range(parts)],
+                axis=1,
+            )
+            for f in range(N_GRAD)
+        ]
+        ca, cb, cc = feats[2, :, at], feats[3, :, at], feats[4, :, at]
         du = (ca * gr[1] + cb * gr[2], cb * gr[1] + cc * gr[2])
         h00, h01, h11 = conic_pull(ca, cb, cc, gr[3], gr[4], gr[5])
         a0, a1 = column[0:3], column[3:6]
@@ -492,7 +518,7 @@
             out[3 + c : 4 + c, at] = dls[c]
         for c in range(4):
             out[6 + c : 7 + c, at] = dquat[c]
-        base = conic[3, 0:1, at]
+        base = feats[5, 0:1, at]
         out[10:11, at] = over_images(gr[0]) * (1.0 - base)
         for k in range(3):
             gc_s[8 * k : 8 * k + 8, at] = gr[6 + k]
@@ -512,7 +538,7 @@
     return pl.BlockSpec(memory_space=memory)
 
 
-def call(kernel, name, out_shape, scratch, n_in, smem=0):
+def call(kernel, name, out_shape, scratch, n_in, smem=0, cost=None):
     return pl.pallas_call(
         kernel,
         name=name,
@@ -520,6 +546,7 @@
         in_specs=[whole(pltpu.SMEM)] * smem + [whole()] * (n_in - smem),
         out_specs=jax.tree.map(lambda _: whole(), out_shape),
         scratch_shapes=scratch,
+        cost_estimate=cost,
         compiler_params=pltpu.CompilerParams(vmem_limit_bytes=32 << 20),
     )
 
@@ -537,25 +564,29 @@
     means, log_scales, quat_w, quat_v, opacity, sh_coeffs, cameras, requests, lists, counts, image_cot
 ):
     devices = N_IMG * N_TILE
+    by_owner = jnp.transpose(requests.reshape(N_IMG, N_TILE, CAP), (0, 2, 1)).reshape(N_IMG * CAP, N_TILE)
+    wanted = call(ask_kernel, "ask", jax.ShapeDtypeStruct((devices, LANES), jnp.int32), [], 1)(by_owner)
+    asked = exchange_rows(wanted, 1)
     meta = jnp.concatenate(
         [counts[0], jnp.stack([lax.axis_index("tile"), lax.axis_index("img")]).astype(jnp.int32)]
     )
-    by_owner = jnp.transpose(requests.reshape(N_IMG, N_TILE, CAP), (0, 2, 1)).reshape(N_IMG * CAP, N_TILE)
-    wanted = call(ask_kernel, "ask", jax.ShapeDtypeStruct((devices, LANES), jnp.int32), [], 1)(by_owner)
-    wanted, meta = lax.optimization_barrier((wanted, meta))
-    asked = exchange_rows(wanted, 1)
-    packed, conic, table = call(
+    feats, table = call(
+        project_kernel,
+        "project",
+        (jax.ShapeDtypeStruct((N_FEAT, N_IMG, OWNED), f32), jax.ShapeDtypeStruct((N_IMG, LANES), f32)),
+        [pltpu.VMEM((48, N_IMG, LANES), f32)],
+        7,
+        cost=pl.CostEstimate(flops=20_000_000, transcendentals=0, bytes_accessed=1_000_000),
+    )(means, log_scales, quat_w, quat_v, opacity, sh_coeffs, cameras)
+    asked, feats, meta = lax.optimization_barrier((asked, feats, meta))
+    packed = call(
         pick_kernel,
         "pick",
-        (
-            jax.ShapeDtypeStruct((FEAT_ROWS * devices, LANES), f32),
-            jax.ShapeDtypeStruct((4, N_IMG, OWNED), f32),
-            jax.ShapeDtypeStruct((N_IMG, LANES), f32),
-        ),
-        [pltpu.VMEM((N_FEAT, N_IMG, OWNED), f32), pltpu.VMEM((48, N_IMG, LANES), f32)],
-        9,
+        jax.ShapeDtypeStruct((FEAT_ROWS * devices, LANES), f32),
+        [pltpu.VMEM((32, N_IMG, LANES), jnp.int32)],
+        3,
         smem=1,
-    )(meta, asked, means, log_scales, quat_w, quat_v, opacity, sh_coeffs, cameras)
+    )(meta, asked, feats)
     rows = exchange_rows(packed, FEAT_ROWS)
     rendered, slot_grads = call(
         render_kernel,
@@ -598,7 +629,7 @@
         ],
         9,
         smem=1,
-    )(meta, returned, asked, conic, table, log_scales, quat_w, quat_v, cameras)
+    )(meta, returned, asked, feats, table, log_scales, quat_w, quat_v, cameras)
     return (rendered[None], param_grad, camera_grad)
 
 

time: 95.4 us -> 92 us (0.964)
  blocking collectives: 72.3 us -> 46.4 us
  starting transfers between devices: 0 us -> 15.6 us
  waiting for transfers between devices: 0 us -> 5.55 us
  local copies, waits for them, and re-layouts: 1.67 us -> 6.2 us
  Pallas kernels: 19.7 us -> 16.1 us
    all_to_all x3 -> x2, blocking collectives: 72.3 us -> 46.4 us  [exchange(): return lax.all_to_all(array, ORDER, split_axis=0, concat_axis=0, tiled=True)]
    all_to_all x0 -> x1, starting transfers between devices: none -> 15.6 us  [exchange(): return lax.all_to_all(array, ORDER, split_axis=0, concat_axis=0, tiled=True)]
    all_to_all x0 -> x1, waiting for transfers between devices: none -> 5.55 us  [exchange(): return lax.all_to_all(array, ORDER, split_axis=0, concat_axis=0, tiled=True)]
    unnamed x20 -> x28, local copies, waits for them, and re-layouts: 1.67 us -> 6.2 us
    pallas_call x1 -> x2, Pallas kernels: 6.02 us -> 4.12 us  [the longest x1 2.87 us: local(): call(pick_kernel, 'pick', jax.ShapeDtypeStruct((FEAT_ROWS * devices, LANE...]
    pallas_call x1, Pallas kernels: 5.28 us -> 3.76 us  [local(): call(pull_kernel, 'pull', (jax.ShapeDtypeStruct((59, OWNED), f32), jax.Sh...]
  transfers between devices with their start and end apart: 0 -> 1, of which waited for: 0 -> 1; matrix products, arithmetic and copies ran while one was open for 0% -> 1% of each run, Pallas kernels for 0% -> 1%
where the time goes in v3:
time: 92 us; the launch traced here: 91.3 us
  blocking collectives  46.4 us (50%)
  Pallas kernels  16.1 us (18%)
  starting transfers between devices  15.6 us (17%)
  local copies, waits for them, and re-layouts  6.2 us (7%)
  waiting for transfers between devices  5.55 us (6%)
    all_to_all x2, blocking collectives, exchange(): return lax.all_to_all(array, ORDER, split_axis=0, concat_axis=0, tiled=True)  46.4 us
    all_to_all x1, starting transfers between devices, exchange(): return lax.all_to_all(array, ORDER, split_axis=0, concat_axis=0, tiled=True)  15.6 us
    pallas_call x1, Pallas kernels, local(): call(render_kernel, 'render', (jax.ShapeDtypeStruct((3, TILES_HERE, PIX),...  7.49 us
    unnamed x28, local copies, waits for them, and re-layouts  6.2 us
    all_to_all x1, waiting for transfers between devices, exchange(): return lax.all_to_all(array, ORDER, split_axis=0, concat_axis=0, tiled=True)  5.55 us
    pallas_call x1, Pallas kernels, local(): call(pull_kernel, 'pull', (jax.ShapeDtypeStruct((59, OWNED), f32), jax.Sh...  3.76 us
    pallas_call x1, Pallas kernels, local(): call(pick_kernel, 'pick', jax.ShapeDtypeStruct((FEAT_ROWS * devices, LANE...  2.87 us
  transfers between devices with their start and end apart: 1, of which 1 were waited for; matrix products, arithmetic and copies ran while one was open for 1% of the time, Pallas kernels for 1%

profile of v3, /device:TPU:1, one launch (start us, length us, event | category | flops | bytes accessed | tf_op | source)
XLA Modules:
  0.0 91.3 jit_solution(10743203194448159170)
XLA Ops:
  0.6 0.0 copy-start.5
  0.6 0.8 copy-done.5
  1.5 0.7 ask.1
  2.2 15.6 %all-to-all-start = ((s32[256,1,128]{2,1,0:T(1,128)}), s32[256,1,128]{2,1,0:T(1,128)S(1)}, u32[]{:S(2)}, u32[]{:S(2)}) async-start(s32[256,1,128]{2,1,0:T(1,128)} %bitcast.4), calls=%async_computation | async-start | bytes 262144 | tf_op jit(solution)/shard_map/all_to_all | solution.py:555
  17.9 0.0 copy-start
  17.9 1.0 %copy-done = f32[48,2048]{1,0:T(8,128)S(1)} copy-done((f32[48,2048]{1,0:T(8,128)S(1)}, f32[48,2048]{1,0:T(8,128)}, u32[]{:S(2)}) %copy-start) | copy-done | bytes 393240
  18.9 0.0 copy-start.1
  18.9 0.8 copy-done.1
  19.6 0.0 copy-start.3
  19.6 0.8 copy-done.3
  20.4 0.0 copy-start.6
  20.4 0.7 copy-done.6
  21.1 0.0 copy-start.8
  21.1 0.8 copy-done.8
  21.8 0.7 copy-done.10
  22.5 0.7 copy-done.12
  23.2 1.2 %project.1 = (f32[24,8,2048]{2,1,0:T(8,128)S(1)}, f32[8,128]{1,0:T(8,128)S(1)}) custom-call(f32[3,2048]{1,0:T(4,128)S(1)} %copy-done.8, f32[3,2048]{1,0:T(4,128)S(1)} %copy-done.1, f32[1,2048]{1,0:T(1,128)S(1)} %copy-done.6, f32[3,2048]{1,0:T(4,128)S(1)} %copy-done.3, f32[1,2048]{1,0:T(1,128)S(1)} %copy-done.12, f32[48,2048]{1,0:T(8,128)S(1)} %copy-done, ...), custom_call_target="tpu_custom_call" | custom-call | flops 20000000 | bytes 1000000 | tf_op jit(solution)/shard_map/project/pallas_call | solution.py:573
  24.5 0.0 copy-start.9
  24.5 0.0 copy-start.13
  24.5 0.7 pad_add_fusion.meta
  25.2 5.5 %all-to-all-done = s32[256,1,128]{2,1,0:T(1,128)S(1)} async-done(((s32[256,1,128]{2,1,0:T(1,128)}), s32[256,1,128]{2,1,0:T(1,128)S(1)}, u32[]{:S(2)}, u32[]{:S(2)}) %all-to-all-start) | async-done | bytes 131104 | tf_op jit(solution)/shard_map/all_to_all | solution.py:555
  30.8 2.9 %pick.1 = f32[768,128]{1,0:T(8,128)S(1)} custom-call(s32[10]{0:T(128)S(1)} %pad_add_fusion.meta, s32[256,128]{1,0:T(8,128)S(1)} %bitcast.21, f32[24,8,2048]{2,1,0:T(8,128)S(1)} %get-tuple-element.15.feats), custom_call_target="tpu_custom_call" | custom-call | tf_op jit(solution)/shard_map/pick/pallas_call | solution.py:582
  33.7 25.1 %all_to_all.15 = f32[256,1,384]{2,1,0:T(1,128)S(1)} all-to-all(f32[256,1,384]{2,1,0:T(1,128)S(1)} %bitcast.20), channel_id=1, replica_groups=mesh['img'=8,'tile'=32] {'tile','img'}, dimensions={0} | all-to-all | bytes 786432 | tf_op jit(solution)/shard_map/all_to_all | solution.py:555
  58.8 0.0 copy-done.9
  58.8 0.0 copy-done.13
  58.8 7.5 %render.1 = (f32[3,8,256]{2,1,0:T(8,128)}, f32[512,128]{1,0:T(8,128)S(1)}) custom-call(s32[10]{0:T(128)S(1)} %pad_add_fusion.meta, f32[768,128]{1,0:T(8,128)S(1)} %bitcast.19, s32[8,256]{1,0:T(8,128)S(1)} %bitcast.27, f32[3,8,256]{2,1,0:T(8,128)S(1)} %bitcast.26), custom_call_target="tpu_custom_call" | custom-call | tf_op jit(solution)/shard_map/render/pallas_call | solution.py:591
  66.3 21.3 %all_to_all.16 = f32[256,1,256]{2,1,0:T(1,128)S(1)} all-to-all(f32[256,1,256]{2,1,0:T(1,128)S(1)} %bitcast.24), channel_id=1, replica_groups=mesh['img'=8,'tile'=32] {'tile','img'}, dimensions={0} | all-to-all | bytes 524288 | tf_op jit(solution)/shard_map/all_to_all | solution.py:555
  87.5 0.0 copy-done.2
  87.5 0.0 copy-done.4
  87.5 0.0 copy-done.7
  87.6 0.0 copy-done.11
  87.6 3.8 %pull.1 = (f32[59,2048]{1,0:T(8,128)}, f32[8,10]{1,0:T(8,128)}) custom-call(s32[10]{0:T(128)S(1)} %pad_add_fusion.meta, f32[512,128]{1,0:T(8,128)S(1)} %bitcast.23, s32[256,128]{1,0:T(8,128)S(1)} %bitcast.22, f32[24,8,2048]{2,1,0:T(8,128)S(1)} %get-tuple-element.15.feats, f32[8,128]{1,0:T(8,128)S(1)} %get-tuple-element.18.table, f32[3,2048]{1,0:T(4,128)S(1)} %copy-done.2, ...), custom_call_target="tpu_custom_call" | custom-call | tf_op jit(solution)/shard_map/pull/pallas_call | solution.py:616
  (6 shorter events, 0.0 us)
Async XLA Ops:
  0.6 0.8 copy-start.5
  2.2 28.6 %all-to-all-start = ((s32[256,1,128]{2,1,0:T(1,128)}), s32[256,1,128]{2,1,0:T(1,128)S(1)}, u32[]{:S(2)}, u32[]{:S(2)}) async-start(s32[256,1,128]{2,1,0:T(1,128)} %bitcast.4), calls=%async_computation | async-start | bytes 262144 | tf_op jit(solution)/shard_map/all_to_all | solution.py:555
  17.9 1.0 %copy-start = (f32[48,2048]{1,0:T(8,128)S(1)}, f32[48,2048]{1,0:T(8,128)}, u32[]{:S(2)}) copy-start(f32[48,2048]{1,0:T(8,128)} %sh.1) | copy-start | bytes 1179652
  18.9 0.8 copy-start.1
  19.6 0.8 copy-start.3
  20.4 0.7 copy-start.6
  21.1 0.8 copy-start.8
  21.8 0.7 copy-start.10
  22.5 0.7 copy-start.12
  24.5 34.3 %copy-start.9 = (f32[1,3,8,256]{3,2,1,0:T(8,128)S(1)}, f32[1,3,8,256]{3,2,1,0:T(8,128)}, u32[]{:S(2)}) copy-start(f32[1,3,8,256]{3,2,1,0:T(8,128)} %param.21) | copy-start | bytes 73732
  24.5 34.3 %copy-start.13 = (s32[1,8,256]{2,1,0:T(8,128)S(1)}, s32[1,8,256]{2,1,0:T(8,128)}, u32[]{:S(2)}) copy-start(s32[1,8,256]{2,1,0:T(8,128)} %param.19) | copy-start | bytes 24580
  30.8 56.8 %copy-start.2 = (f32[3,2048]{1,0:T(4,128)S(1)}, f32[3,2048]{1,0:T(4,128)}, u32[]{:S(2)}) copy-start(f32[3,2048]{1,0:T(4,128)} %log_scales.3) | copy-start | bytes 73732
  30.8 56.8 %copy-start.4 = (f32[3,2048]{1,0:T(4,128)S(1)}, f32[3,2048]{1,0:T(4,128)}, u32[]{:S(2)}) copy-start(f32[3,2048]{1,0:T(4,128)} %quat_v.3) | copy-start | bytes 73732
  30.8 56.8 %copy-start.7 = (f32[1,2048]{1,0:T(1,128)S(1)}, f32[1,2048]{1,0:T(1,128)}, u32[]{:S(2)}) copy-start(f32[1,2048]{1,0:T(1,128)} %quat_w.3) | copy-start | bytes 24580
  30.8 56.8 %copy-start.11 = (f32[8,10]{1,0:T(8,128)S(1)}, f32[8,10]{1,0:T(8,128)}, u32[]{:S(2)}) copy-start(f32[8,10]{1,0:T(8,128)} %cam.3) | copy-start | bytes 964

commit v4 on v3

--- a/solution.py
+++ b/solution.py
@@ -193,7 +193,15 @@
     lax.fori_loop(0, OWNED // PROJECT_CHUNK, chunk, 0)
 
 
-def project_kernel(means, log_scales, quat_w, quat_v, opacity, sh, cam, feats, table, harm):
+def project_kernel(*refs):
+    sources, (feats, table), rest = refs[:7], refs[7:9], refs[9:]
+    harm, held, sems = rest[0], rest[1:8], rest[8]
+    copies = [pltpu.make_async_copy(a, b, sems.at[n]) for n, (a, b) in enumerate(zip(sources, held))]
+    for copy in reversed(copies):
+        copy.start()
+    for copy in reversed(copies):
+        copy.wait()
+    means, log_scales, quat_w, quat_v, opacity, sh, cam = held
     polar = jnp.broadcast_to(cam[:, 8:9], (N_IMG, LANES))
     azimuth = jnp.broadcast_to(cam[:, 9:10], (N_IMG, LANES))
     one, zero = jnp.ones_like(polar), jnp.zeros_like(polar)
@@ -538,12 +546,12 @@
     return pl.BlockSpec(memory_space=memory)
 
 
-def call(kernel, name, out_shape, scratch, n_in, smem=0, cost=None):
+def call(kernel, name, out_shape, scratch, n_in, smem=0, memory=pltpu.VMEM, cost=None):
     return pl.pallas_call(
         kernel,
         name=name,
         out_shape=out_shape,
-        in_specs=[whole(pltpu.SMEM)] * smem + [whole()] * (n_in - smem),
+        in_specs=[whole(pltpu.SMEM)] * smem + [whole(memory)] * (n_in - smem),
         out_specs=jax.tree.map(lambda _: whole(), out_shape),
         scratch_shapes=scratch,
         cost_estimate=cost,
@@ -570,14 +578,21 @@
     meta = jnp.concatenate(
         [counts[0], jnp.stack([lax.axis_index("tile"), lax.axis_index("img")]).astype(jnp.int32)]
     )
+    owned = [
+        pltpu.with_memory_space_constraint(a, pltpu.HBM)
+        for a in (means, log_scales, quat_w, quat_v, opacity, sh_coeffs, cameras)
+    ]
     feats, table = call(
         project_kernel,
         "project",
         (jax.ShapeDtypeStruct((N_FEAT, N_IMG, OWNED), f32), jax.ShapeDtypeStruct((N_IMG, LANES), f32)),
-        [pltpu.VMEM((48, N_IMG, LANES), f32)],
+        [pltpu.VMEM((48, N_IMG, LANES), f32)]
+        + [pltpu.VMEM(a.shape, f32) for a in owned]
+        + [pltpu.SemaphoreType.DMA((7,))],
         7,
+        memory=pltpu.HBM,
         cost=pl.CostEstimate(flops=20_000_000, transcendentals=0, bytes_accessed=1_000_000),
-    )(means, log_scales, quat_w, quat_v, opacity, sh_coeffs, cameras)
+    )(*owned)
     asked, feats, meta = lax.optimization_barrier((asked, feats, meta))
     packed = call(
         pick_kernel,

time: 92 us -> 88.9 us (0.966)
  local copies, waits for them, and re-layouts: 6.2 us -> 0.86 us
  waiting for transfers between devices: 5.55 us -> 9.83 us
  blocking collectives: 46.4 us -> 43.7 us
  Pallas kernels: 16.1 us -> 17.2 us
    unnamed x28 -> x14, local copies, waits for them, and re-layouts: 6.2 us -> 0.86 us
    all_to_all x1, waiting for transfers between devices: 5.55 us -> 9.83 us  [exchange(): return lax.all_to_all(array, ORDER, split_axis=0, concat_axis=0, tiled=True)]
    all_to_all x2, blocking collectives: 46.4 us -> 43.7 us  [exchange(): return lax.all_to_all(array, ORDER, split_axis=0, concat_axis=0, tiled=True)]
    pallas_call x1, Pallas kernels: 1.25 us -> 2.32 us  [local(): call(project_kernel, 'project', (jax.ShapeDtypeStruct((N_FEAT, N_IMG, OWN...]
  transfers between devices with their start and end apart: 1 -> 1, of which waited for: 1 -> 1; matrix products, arithmetic and copies ran while one was open for 1% -> 1% of each run, Pallas kernels for 1% -> 3%
where the time goes in v4:
time: 88.9 us; the launch traced here: 88.7 us
  blocking collectives  43.7 us (49%)
  Pallas kernels  17.2 us (19%)
  starting transfers between devices  15.6 us (18%)
  waiting for transfers between devices  9.83 us (11%)
    all_to_all x2, blocking collectives, exchange(): return lax.all_to_all(array, ORDER, split_axis=0, concat_axis=0, tiled=True)  43.7 us
    all_to_all x1, starting transfers between devices, exchange(): return lax.all_to_all(array, ORDER, split_axis=0, concat_axis=0, tiled=True)  15.6 us
    all_to_all x1, waiting for transfers between devices, exchange(): return lax.all_to_all(array, ORDER, split_axis=0, concat_axis=0, tiled=True)  9.83 us
    pallas_call x1, Pallas kernels, local(): call(render_kernel, 'render', (jax.ShapeDtypeStruct((3, TILES_HERE, PIX),...  7.49 us
    pallas_call x1, Pallas kernels, local(): call(pull_kernel, 'pull', (jax.ShapeDtypeStruct((59, OWNED), f32), jax.Sh...  3.76 us
    pallas_call x1, Pallas kernels, local(): call(pick_kernel, 'pick', jax.ShapeDtypeStruct((FEAT_ROWS * devices, LANE...  2.87 us
    pallas_call x1, Pallas kernels, local(): call(project_kernel, 'project', (jax.ShapeDtypeStruct((N_FEAT, N_IMG, OWN...  2.32 us
  transfers between devices with their start and end apart: 1, of which 1 were waited for; matrix products, arithmetic and copies ran while one was open for 1% of the time, Pallas kernels for 3%

profile of v4, /device:TPU:1, one launch (start us, length us, event | category | flops | bytes accessed | tf_op | source)
XLA Modules:
  0.0 88.7 jit_solution(2537425164229890256)
XLA Ops:
  0.6 0.0 copy-start.2
  0.6 0.8 copy-done.2
  1.5 0.7 ask.1
  2.2 15.6 %all-to-all-start = ((s32[256,1,128]{2,1,0:T(1,128)}), s32[256,1,128]{2,1,0:T(1,128)S(1)}, u32[]{:S(2)}, u32[]{:S(2)}) async-start(s32[256,1,128]{2,1,0:T(1,128)} %bitcast.4), calls=%async_computation | async-start | bytes 262144 | tf_op jit(solution)/shard_map/all_to_all | solution.py:563
  17.9 2.3 %project.1 = (f32[24,8,2048]{2,1,0:T(8,128)S(1)}, f32[8,128]{1,0:T(8,128)S(1)}) custom-call(f32[3,2048]{1,0:T(4,128)} %refs_0_.1, f32[3,2048]{1,0:T(4,128)} %log_scales.1, f32[1,2048]{1,0:T(1,128)} %quat_w.1, f32[3,2048]{1,0:T(4,128)} %quat_v.1, f32[1,2048]{1,0:T(1,128)} %refs_4_.1, f32[48,2048]{1,0:T(8,128)} %refs_5_.1, f32[8,10]{1,0:T(8,128)} %cam.1), custom_call_target="tpu_custom_call" | custom-call | flops 20000000 | bytes 1000000 | tf_op jit(solution)/shard_map/project/pallas_call | solution.py:585
  20.2 0.0 copy-start.4
  20.2 0.0 copy-start.6
  20.2 0.7 pad_add_fusion.meta
  21.0 9.8 %all-to-all-done = s32[256,1,128]{2,1,0:T(1,128)S(1)} async-done(((s32[256,1,128]{2,1,0:T(1,128)}), s32[256,1,128]{2,1,0:T(1,128)S(1)}, u32[]{:S(2)}, u32[]{:S(2)}) %all-to-all-start) | async-done | bytes 131104 | tf_op jit(solution)/shard_map/all_to_all | solution.py:563
  30.8 0.0 copy-start
  30.8 0.0 copy-start.1
  30.8 0.0 copy-start.3
  30.8 0.0 copy-start.5
  30.8 2.9 %pick.1 = f32[768,128]{1,0:T(8,128)S(1)} custom-call(s32[10]{0:T(128)S(1)} %pad_add_fusion.meta, s32[256,128]{1,0:T(8,128)S(1)} %bitcast.21, f32[24,8,2048]{2,1,0:T(8,128)S(1)} %get-tuple-element.15.feats), custom_call_target="tpu_custom_call" | custom-call | tf_op jit(solution)/shard_map/pick/pallas_call | solution.py:597
  33.7 22.4 %all_to_all.15 = f32[256,1,384]{2,1,0:T(1,128)S(1)} all-to-all(f32[256,1,384]{2,1,0:T(1,128)S(1)} %bitcast.20), channel_id=1, replica_groups=mesh['img'=8,'tile'=32] {'tile','img'}, dimensions={0} | all-to-all | bytes 786432 | tf_op jit(solution)/shard_map/all_to_all | solution.py:563
  56.1 0.0 copy-done.4
  56.1 0.0 copy-done.6
  56.1 7.5 %render.1 = (f32[3,8,256]{2,1,0:T(8,128)}, f32[512,128]{1,0:T(8,128)S(1)}) custom-call(s32[10]{0:T(128)S(1)} %pad_add_fusion.meta, f32[768,128]{1,0:T(8,128)S(1)} %bitcast.19, s32[8,256]{1,0:T(8,128)S(1)} %bitcast.27, f32[3,8,256]{2,1,0:T(8,128)S(1)} %bitcast.26), custom_call_target="tpu_custom_call" | custom-call | tf_op jit(solution)/shard_map/render/pallas_call | solution.py:606
  63.6 21.3 %all_to_all.16 = f32[256,1,256]{2,1,0:T(1,128)S(1)} all-to-all(f32[256,1,256]{2,1,0:T(1,128)S(1)} %bitcast.24), channel_id=1, replica_groups=mesh['img'=8,'tile'=32] {'tile','img'}, dimensions={0} | all-to-all | bytes 524288 | tf_op jit(solution)/shard_map/all_to_all | solution.py:563
  84.9 0.0 copy-done
  84.9 0.0 copy-done.1
  84.9 0.0 copy-done.3
  84.9 0.0 copy-done.5
  84.9 3.8 %pull.1 = (f32[59,2048]{1,0:T(8,128)}, f32[8,10]{1,0:T(8,128)}) custom-call(s32[10]{0:T(128)S(1)} %pad_add_fusion.meta, f32[512,128]{1,0:T(8,128)S(1)} %bitcast.23, s32[256,128]{1,0:T(8,128)S(1)} %bitcast.22, f32[24,8,2048]{2,1,0:T(8,128)S(1)} %get-tuple-element.15.feats, f32[8,128]{1,0:T(8,128)S(1)} %get-tuple-element.18.table, f32[3,2048]{1,0:T(4,128)S(1)} %copy-done, ...), custom_call_target="tpu_custom_call" | custom-call | tf_op jit(solution)/shard_map/pull/pallas_call | solution.py:631
Async XLA Ops:
  0.6 0.8 copy-start.2
  2.2 28.6 %all-to-all-start = ((s32[256,1,128]{2,1,0:T(1,128)}), s32[256,1,128]{2,1,0:T(1,128)S(1)}, u32[]{:S(2)}, u32[]{:S(2)}) async-start(s32[256,1,128]{2,1,0:T(1,128)} %bitcast.4), calls=%async_computation | async-start | bytes 262144 | tf_op jit(solution)/shard_map/all_to_all | solution.py:563
  20.2 35.9 %copy-start.4 = (f32[1,3,8,256]{3,2,1,0:T(8,128)S(1)}, f32[1,3,8,256]{3,2,1,0:T(8,128)}, u32[]{:S(2)}) copy-start(f32[1,3,8,256]{3,2,1,0:T(8,128)} %param.21) | copy-start | bytes 73732
  20.2 35.9 %copy-start.6 = (s32[1,8,256]{2,1,0:T(8,128)S(1)}, s32[1,8,256]{2,1,0:T(8,128)}, u32[]{:S(2)}) copy-start(s32[1,8,256]{2,1,0:T(8,128)} %param.19) | copy-start | bytes 24580
  30.8 54.1 %copy-start = (f32[3,2048]{1,0:T(4,128)S(1)}, f32[3,2048]{1,0:T(4,128)}, u32[]{:S(2)}) copy-start(f32[3,2048]{1,0:T(4,128)} %log_scales.1) | copy-start | bytes 73732
  30.8 54.1 %copy-start.1 = (f32[3,2048]{1,0:T(4,128)S(1)}, f32[3,2048]{1,0:T(4,128)}, u32[]{:S(2)}) copy-start(f32[3,2048]{1,0:T(4,128)} %quat_v.1) | copy-start | bytes 73732
  30.8 54.1 %copy-start.3 = (f32[1,2048]{1,0:T(1,128)S(1)}, f32[1,2048]{1,0:T(1,128)}, u32[]{:S(2)}) copy-start(f32[1,2048]{1,0:T(1,128)} %quat_w.1) | copy-start | bytes 24580
  30.8 54.1 %copy-start.5 = (f32[8,10]{1,0:T(8,128)S(1)}, f32[8,10]{1,0:T(8,128)}, u32[]{:S(2)}) copy-start(f32[8,10]{1,0:T(8,128)} %cam.1) | copy-start | bytes 964

commit v5 on v4

--- a/solution.py
+++ b/solution.py
@@ -114,6 +114,10 @@
 def halves(value):
     high = value.astype(bf16)
     return high, (value - high.astype(f32)).astype(bf16)
+
+
+def row_parts(row):
+    return halves(jnp.broadcast_to(row, (16, row.shape[1])))
 
 
 def dot(a, b):
@@ -347,8 +351,9 @@
                 hi, low = halves(jnp.log2(1.0 - alpha))
                 lk_s[p, r, 0:LIST] = hi
                 lk_s[p, r, LIST : 2 * LIST] = low
+            state.append((at, uy, dx, col_h, col_l, cot_h, cot_l))
+        for p in range(2):
             lb_s[p] = dot(lk_s[p], upper[...])
-            state.append((at, uy, dx, col_h, col_l, cot_h, cot_l))
         for p in range(2):
             for py in range(TILE_SIDE):
                 r = slice(TILE_SIDE * py, TILE_SIDE * (py + 1))
@@ -361,6 +366,7 @@
                 hi, low = halves(sw)
                 sw_s[p, r, 0:LIST] = hi
                 sw_s[p, r, LIST : 2 * LIST] = low
+        for p in range(2):
             lb_s[p] = dot(sw_s[p], lower[...])
         for p in range(2):
             at, uy, dx, col_h, col_l, cot_h, cot_l = state[p]
@@ -395,11 +401,13 @@
                 down(acc[2][0], acc[2][1]),
             ] + [gcol[k : k + 1, :] + gcol[3 + k : 4 + k, :] for k in range(3)]
             s = lists[at, :]
-            chunk_hit = ch_iota == (((s >> 7) & 3) * 8 + (s >> 9))
+            chunk_hit = (ch_iota == (((s >> 7) & 3) * 8 + (s >> 9))).astype(f32).astype(bf16)
             for f in range(N_GRAD):
-                hi, low = halves(jnp.where(chunk_hit, grad[f], 0.0))
-                grads[p, 32 * f : 32 * (f + 1), 0:LIST] = hi
-                grads[p, 32 * f : 32 * (f + 1), LIST : 2 * LIST] = low
+                for n, part in enumerate(row_parts(grad[f])):
+                    for r in range(0, 32, 16):
+                        grads[p, 32 * f + r : 32 * f + r + 16, n * LIST : (n + 1) * LIST] = (
+                            chunk_hit[r : r + 16, :] * part
+                        )
             lane_hit = (lane_iota == (s & (LANES - 1))).astype(f32).astype(bf16)
             slot[...] += dot_t(grads[p], jnp.concatenate([lane_hit, lane_hit], axis=1))
         return carry
@@ -447,8 +455,9 @@
 
 
 def pull_kernel(
-    meta, returned, asked, feats, table, log_scales, quat_w, quat_v, cam, out, cam_out, row_s, idx_s, lhs_s, sum_s, gc_s
+    meta, returned, asked, feats, table, log_scales, quat_w, quat_v, cam, image, out, cam_out, image_out, row_s, idx_s, lhs_s, sum_s, gc_s
 ):
+    image_out[...] = image[...]
     index = asked_lanes(asked, meta[TILES_HERE + 1])
     for q in range(4):
         idx_s[:, q * LANES : (q + 1) * LANES] = index[q]
@@ -476,12 +485,11 @@
     def image(i, carry):
         at = pl.ds(i, 1)
         s = idx_s[at, :]
-        high_hit = high_iota == (s >> 7)
+        high_hit = (high_iota == (s >> 7)).astype(f32).astype(bf16)
         lane_hit = (lane_iota == (s & (LANES - 1))).astype(f32).astype(bf16)
         for f in range(N_GRAD):
-            hi, low = halves(jnp.where(high_hit, row_s[f, at, :], 0.0))
-            lhs_s[16 * f : 16 * (f + 1), 0:slots] = hi
-            lhs_s[16 * f : 16 * (f + 1), slots : 2 * slots] = low
+            for n, part in enumerate(row_parts(row_s[f, at, :])):
+                lhs_s[16 * f : 16 * (f + 1), n * slots : (n + 1) * slots] = high_hit * part
         sum_s[pl.ds(pl.multiple_of(i * (16 * N_GRAD), 16), 16 * N_GRAD), :] = dot_t(
             lhs_s[...], jnp.concatenate([lane_hit, lane_hit], axis=1)
         )
@@ -628,12 +636,13 @@
         smem=1,
     )(meta, rows, lists[0], image_cot[0])
     returned = exchange_rows(slot_grads, GRAD_ROWS)
-    param_grad, camera_grad = call(
+    param_grad, camera_grad, rendered = call(
         pull_kernel,
         "pull",
         (
             jax.ShapeDtypeStruct((59, OWNED), f32),
             jax.ShapeDtypeStruct((N_IMG, 10), f32),
+            jax.ShapeDtypeStruct((3, TILES_HERE, PIX), f32),
         ),
         [
             pltpu.VMEM((N_GRAD, N_IMG, N_TILE * CAP), f32),
@@ -642,9 +651,9 @@
             pltpu.VMEM((N_IMG * 16 * N_GRAD, LANES), f32),
             pltpu.VMEM((24, OWNED), f32),
         ],
-        9,
+        10,
         smem=1,
-    )(meta, returned, asked, feats, table, log_scales, quat_w, quat_v, cameras)
+    )(meta, returned, asked, feats, table, log_scales, quat_w, quat_v, cameras, rendered)
     return (rendered[None], param_grad, camera_grad)
 
 

time: 88.9 us -> 88.5 us (level)
  no operation moved by 1% of the time
where the time goes in v5:
time: 88.5 us; the launch traced here: 88.2 us
  blocking collectives  43.7 us (49%)
  Pallas kernels  16.7 us (19%)
  starting transfers between devices  15.6 us (18%)
  waiting for transfers between devices  9.83 us (11%)
    all_to_all x2, blocking collectives, exchange(): return lax.all_to_all(array, ORDER, split_axis=0, concat_axis=0, tiled=True)  43.7 us
    all_to_all x1, starting transfers between devices, exchange(): return lax.all_to_all(array, ORDER, split_axis=0, concat_axis=0, tiled=True)  15.6 us
    all_to_all x1, waiting for transfers between devices, exchange(): return lax.all_to_all(array, ORDER, split_axis=0, concat_axis=0, tiled=True)  9.83 us
    pallas_call x1, Pallas kernels, local(): call(render_kernel, 'render', (jax.ShapeDtypeStruct((3, TILES_HERE, PIX),...  7.11 us
    pallas_call x1, Pallas kernels, local(): call(pull_kernel, 'pull', (jax.ShapeDtypeStruct((59, OWNED), f32), jax.Sh...  3.65 us
    pallas_call x1, Pallas kernels, local(): call(pick_kernel, 'pick', jax.ShapeDtypeStruct((FEAT_ROWS * devices, LANE...  2.87 us
    pallas_call x1, Pallas kernels, local(): call(project_kernel, 'project', (jax.ShapeDtypeStruct((N_FEAT, N_IMG, OWN...  2.32 us
  transfers between devices with their start and end apart: 1, of which 1 were waited for; matrix products, arithmetic and copies ran while one was open for 1% of the time, Pallas kernels for 3%

profile of v5, /device:TPU:1, one launch (start us, length us, event | category | flops | bytes accessed | tf_op | source)
XLA Modules:
  0.0 88.2 jit_solution(3658042251267891283)
XLA Ops:
  0.6 0.0 copy-start.2
  0.6 0.8 copy-done.2
  1.5 0.7 ask.1
  2.2 15.6 %all-to-all-start = ((s32[256,1,128]{2,1,0:T(1,128)}), s32[256,1,128]{2,1,0:T(1,128)S(1)}, u32[]{:S(2)}, u32[]{:S(2)}) async-start(s32[256,1,128]{2,1,0:T(1,128)} %bitcast.4), calls=%async_computation | async-start | bytes 262144 | tf_op jit(solution)/shard_map/all_to_all | solution.py:571
  17.9 2.3 %project.1 = (f32[24,8,2048]{2,1,0:T(8,128)S(1)}, f32[8,128]{1,0:T(8,128)S(1)}) custom-call(f32[3,2048]{1,0:T(4,128)} %refs_0_.1, f32[3,2048]{1,0:T(4,128)} %log_scales.1, f32[1,2048]{1,0:T(1,128)} %quat_w.1, f32[3,2048]{1,0:T(4,128)} %quat_v.1, f32[1,2048]{1,0:T(1,128)} %refs_4_.1, f32[48,2048]{1,0:T(8,128)} %refs_5_.1, f32[8,10]{1,0:T(8,128)} %cam.1), custom_call_target="tpu_custom_call" | custom-call | flops 20000000 | bytes 1000000 | tf_op jit(solution)/shard_map/project/pallas_call | solution.py:593
  20.2 0.0 copy-start.4
  20.2 0.0 copy-start.6
  20.2 0.7 pad_add_fusion.meta
  21.0 9.8 %all-to-all-done = s32[256,1,128]{2,1,0:T(1,128)S(1)} async-done(((s32[256,1,128]{2,1,0:T(1,128)}), s32[256,1,128]{2,1,0:T(1,128)S(1)}, u32[]{:S(2)}, u32[]{:S(2)}) %all-to-all-start) | async-done | bytes 131104 | tf_op jit(solution)/shard_map/all_to_all | solution.py:571
  30.8 0.0 copy-start
  30.8 0.0 copy-start.1
  30.8 0.0 copy-start.3
  30.8 0.0 copy-start.5
  30.8 2.9 %pick.1 = f32[768,128]{1,0:T(8,128)S(1)} custom-call(s32[10]{0:T(128)S(1)} %pad_add_fusion.meta, s32[256,128]{1,0:T(8,128)S(1)} %bitcast.21, f32[24,8,2048]{2,1,0:T(8,128)S(1)} %get-tuple-element.16.feats), custom_call_target="tpu_custom_call" | custom-call | tf_op jit(solution)/shard_map/pick/pallas_call | solution.py:605
  33.7 22.4 %all_to_all.15 = f32[256,1,384]{2,1,0:T(1,128)S(1)} all-to-all(f32[256,1,384]{2,1,0:T(1,128)S(1)} %bitcast.20), channel_id=1, replica_groups=mesh['img'=8,'tile'=32] {'tile','img'}, dimensions={0} | all-to-all | bytes 786432 | tf_op jit(solution)/shard_map/all_to_all | solution.py:571
  56.1 0.0 copy-done.4
  56.1 0.0 copy-done.6
  56.1 7.1 %render.1 = (f32[3,8,256]{2,1,0:T(8,128)S(1)}, f32[512,128]{1,0:T(8,128)S(1)}) custom-call(s32[10]{0:T(128)S(1)} %pad_add_fusion.meta, f32[768,128]{1,0:T(8,128)S(1)} %bitcast.19, s32[8,256]{1,0:T(8,128)S(1)} %bitcast.27, f32[3,8,256]{2,1,0:T(8,128)S(1)} %bitcast.26), custom_call_target="tpu_custom_call" | custom-call | tf_op jit(solution)/shard_map/render/pallas_call | solution.py:614
  63.2 21.3 %all_to_all.16 = f32[256,1,256]{2,1,0:T(1,128)S(1)} all-to-all(f32[256,1,256]{2,1,0:T(1,128)S(1)} %bitcast.24), channel_id=1, replica_groups=mesh['img'=8,'tile'=32] {'tile','img'}, dimensions={0} | all-to-all | bytes 524288 | tf_op jit(solution)/shard_map/all_to_all | solution.py:571
  84.5 0.0 copy-done
  84.5 0.0 copy-done.1
  84.5 0.0 copy-done.3
  84.5 0.0 copy-done.5
  84.5 3.6 %pull.1 = (f32[59,2048]{1,0:T(8,128)}, f32[8,10]{1,0:T(8,128)}, f32[3,8,256]{2,1,0:T(8,128)}) custom-call(s32[10]{0:T(128)S(1)} %pad_add_fusion.meta, f32[512,128]{1,0:T(8,128)S(1)} %bitcast.23, s32[256,128]{1,0:T(8,128)S(1)} %bitcast.22, f32[24,8,2048]{2,1,0:T(8,128)S(1)} %get-tuple-element.16.feats, f32[8,128]{1,0:T(8,128)S(1)} %get-tuple-element.18.table, ...), custom_call_target="tpu_custom_call" | custom-call | tf_op jit(solution)/shard_map/pull/pallas_call | solution.py:639
Async XLA Ops:
  0.6 0.8 copy-start.2
  2.2 28.6 %all-to-all-start = ((s32[256,1,128]{2,1,0:T(1,128)}), s32[256,1,128]{2,1,0:T(1,128)S(1)}, u32[]{:S(2)}, u32[]{:S(2)}) async-start(s32[256,1,128]{2,1,0:T(1,128)} %bitcast.4), calls=%async_computation | async-start | bytes 262144 | tf_op jit(solution)/shard_map/all_to_all | solution.py:571
  20.2 35.9 %copy-start.4 = (f32[1,3,8,256]{3,2,1,0:T(8,128)S(1)}, f32[1,3,8,256]{3,2,1,0:T(8,128)}, u32[]{:S(2)}) copy-start(f32[1,3,8,256]{3,2,1,0:T(8,128)} %param.21) | copy-start | bytes 73732
  20.2 35.9 %copy-start.6 = (s32[1,8,256]{2,1,0:T(8,128)S(1)}, s32[1,8,256]{2,1,0:T(8,128)}, u32[]{:S(2)}) copy-start(s32[1,8,256]{2,1,0:T(8,128)} %param.19) | copy-start | bytes 24580
  30.8 53.7 %copy-start = (f32[3,2048]{1,0:T(4,128)S(1)}, f32[3,2048]{1,0:T(4,128)}, u32[]{:S(2)}) copy-start(f32[3,2048]{1,0:T(4,128)} %log_scales.1) | copy-start | bytes 73732
  30.8 53.7 %copy-start.1 = (f32[3,2048]{1,0:T(4,128)S(1)}, f32[3,2048]{1,0:T(4,128)}, u32[]{:S(2)}) copy-start(f32[3,2048]{1,0:T(4,128)} %quat_v.1) | copy-start | bytes 73732
  30.8 53.7 %copy-start.3 = (f32[1,2048]{1,0:T(1,128)S(1)}, f32[1,2048]{1,0:T(1,128)}, u32[]{:S(2)}) copy-start(f32[1,2048]{1,0:T(1,128)} %quat_w.1) | copy-start | bytes 24580
  30.8 53.7 %copy-start.5 = (f32[8,10]{1,0:T(8,128)S(1)}, f32[8,10]{1,0:T(8,128)}, u32[]{:S(2)}) copy-start(f32[8,10]{1,0:T(8,128)} %cam.1) | copy-start | bytes 964

commit v6 on v5

--- a/solution.py
+++ b/solution.py
@@ -222,8 +222,9 @@
     project(means, log_scales, quat_w, quat_v, opacity, sh, cam, feats, harm)
 
 
-def pick_kernel(meta, asked, feats, out, index):
+def pick_kernel(meta, asked, feats, out, idx_out, index):
     for q, value in enumerate(asked_lanes(asked, meta[TILES_HERE + 1])):
+        idx_out[:, q * LANES : (q + 1) * LANES] = value
         for f in range(8):
             index[8 * q + f] = rotate(value, f)
 
@@ -264,6 +265,7 @@
     s_s,
     w_s,
     sw_s,
+    later,
 ):
     tile_base = meta[TILES_HERE] * TILES_HERE
     turned = meta[TILES_HERE] & 7
@@ -279,26 +281,35 @@
         return carry
 
     lax.fori_loop(0, 4 * FEAT_ROWS, sort_rows, 0, unroll=4)
-    entry_lane = [lists[:, h * LANES : (h + 1) * LANES] & (LANES - 1) for h in range(2)]
-    entry_chunk = []
-    for h in range(2):
-        s = lists[:, h * LANES : (h + 1) * LANES]
-        entry_chunk.append(((s >> 7) & 3) * 8 + (s >> 9))
-
-    def gather(ch, carry):
-        new = list(carry)
-        for h in range(2):
-            hit = entry_chunk[h] == ch
-            for f in range(N_USED):
-                row = jnp.broadcast_to(tab[f, pl.ds(ch, 1), :], (8, LANES))
-                new[2 * f + h] = jnp.where(hit, lane_take(row, entry_lane[h]), carry[2 * f + h])
-        return tuple(new)
+
+    def entries(quad):
+        s = jnp.concatenate(
+            [lists[4 * quad : 4 * quad + 4, h * LANES : (h + 1) * LANES] for h in range(2)], axis=0
+        )
+        return s & (LANES - 1), ((s >> 7) & 3) * 8 + (s >> 9)
+
+    def gather(ch, carry, lane, chunk):
+        hit = chunk == ch
+        return tuple(
+            jnp.where(hit, lane_take(jnp.broadcast_to(tab[f, pl.ds(ch, 1), :], (8, LANES)), lane), carry[f])
+            for f in range(N_USED)
+        )
+
+    def keep(found, quad):
+        for f in range(N_USED):
+            for h in range(2):
+                feat[f, 4 * quad : 4 * quad + 4, h * LANES : (h + 1) * LANES] = found[f][4 * h : 4 * h + 4, :]
 
     zero = jnp.zeros((8, LANES), f32)
-    found = lax.fori_loop(0, 32, gather, tuple([zero] * (2 * N_USED)), unroll=8)
+    first_lane, first_chunk = entries(0)
+    keep(
+        lax.fori_loop(
+            0, 32, lambda ch, c: gather(ch, c, first_lane, first_chunk), tuple([zero] * N_USED), unroll=8
+        ),
+        0,
+    )
     for f in range(N_USED):
-        for h in range(2):
-            feat[f, :, h * LANES : (h + 1) * LANES] = found[2 * f + h]
+        later[f] = zero
     ri = lax.broadcasted_iota(jnp.int32, (LIST, LIST), 0)
     ci = lax.broadcasted_iota(jnp.int32, (LIST, LIST), 1)
     up = (ri < ci).astype(f32).astype(bf16)
@@ -410,6 +421,13 @@
                         )
             lane_hit = (lane_iota == (s & (LANES - 1))).astype(f32).astype(bf16)
             slot[...] += dot_t(grads[p], jnp.concatenate([lane_hit, lane_hit], axis=1))
+        lane_at, chunk_at = entries(1)
+        found = tuple(later[f] for f in range(N_USED))
+        for n in range(16):
+            found = gather(16 * (pair_index & 1) + n, found, lane_at, chunk_at)
+        for f in range(N_USED):
+            later[f] = found[f]
+        keep(found, 1)
         return carry
 
     lax.fori_loop(0, TILES_HERE // 2, pair, 0)
@@ -455,12 +473,9 @@
 
 
 def pull_kernel(
-    meta, returned, asked, feats, table, log_scales, quat_w, quat_v, cam, image, out, cam_out, image_out, row_s, idx_s, lhs_s, sum_s, gc_s
+    meta, returned, idx_s, feats, table, log_scales, quat_w, quat_v, cam, image, out, cam_out, image_out, row_s, lhs_s, sum_s, gc_s
 ):
     image_out[...] = image[...]
-    index = asked_lanes(asked, meta[TILES_HERE + 1])
-    for q in range(4):
-        idx_s[:, q * LANES : (q + 1) * LANES] = index[q]
     group = lax.broadcasted_iota(jnp.int32, (8, LANES), 1) // CAP
     turned = meta[TILES_HERE] & 7
     camera = jnp.zeros((8, LANES), f32)
@@ -602,10 +617,13 @@
         cost=pl.CostEstimate(flops=20_000_000, transcendentals=0, bytes_accessed=1_000_000),
     )(*owned)
     asked, feats, meta = lax.optimization_barrier((asked, feats, meta))
-    packed = call(
+    packed, index = call(
         pick_kernel,
         "pick",
-        jax.ShapeDtypeStruct((FEAT_ROWS * devices, LANES), f32),
+        (
+            jax.ShapeDtypeStruct((FEAT_ROWS * devices, LANES), f32),
+            jax.ShapeDtypeStruct((N_IMG, N_TILE * CAP), jnp.int32),
+        ),
         [pltpu.VMEM((32, N_IMG, LANES), jnp.int32)],
         3,
         smem=1,
@@ -631,6 +649,7 @@
             pltpu.VMEM((2, PIX, LIST), f32),
             pltpu.VMEM((2, 2 * PIX, LIST), bf16),
             pltpu.VMEM((2, PIX, 2 * LIST), bf16),
+            pltpu.VMEM((N_USED, 8, LANES), f32),
         ],
         4,
         smem=1,
@@ -646,14 +665,13 @@
         ),
         [
             pltpu.VMEM((N_GRAD, N_IMG, N_TILE * CAP), f32),
-            pltpu.VMEM((N_IMG, N_TILE * CAP), jnp.int32),
             pltpu.VMEM((16 * N_GRAD, 2 * N_TILE * CAP), bf16),
             pltpu.VMEM((N_IMG * 16 * N_GRAD, LANES), f32),
             pltpu.VMEM((24, OWNED), f32),
         ],
         10,
         smem=1,
-    )(meta, returned, asked, feats, table, log_scales, quat_w, quat_v, cameras, rendered)
+    )(meta, returned, index, feats, table, log_scales, quat_w, quat_v, cameras, rendered)
     return (rendered[None], param_grad, camera_grad)
 
 

time: 88.5 us -> 87.9 us (level)
  no operation moved by 1% of the time
where the time goes in v6:
time: 87.9 us; the launch traced here: 87.6 us
  blocking collectives  43.7 us (50%)
  Pallas kernels  16.1 us (18%)
  starting transfers between devices  15.6 us (18%)
  waiting for transfers between devices  9.84 us (11%)
    all_to_all x2, blocking collectives, exchange(): return lax.all_to_all(array, ORDER, split_axis=0, concat_axis=0, tiled=True)  43.7 us
    all_to_all x1, starting transfers between devices, exchange(): return lax.all_to_all(array, ORDER, split_axis=0, concat_axis=0, tiled=True)  15.6 us
    all_to_all x1, waiting for transfers between devices, exchange(): return lax.all_to_all(array, ORDER, split_axis=0, concat_axis=0, tiled=True)  9.84 us
    pallas_call x1, Pallas kernels, local(): call(render_kernel, 'render', (jax.ShapeDtypeStruct((3, TILES_HERE, PIX),...  6.6 us
    pallas_call x1, Pallas kernels, local(): call(pull_kernel, 'pull', (jax.ShapeDtypeStruct((59, OWNED), f32), jax.Sh...  3.6 us
    pallas_call x1, Pallas kernels, local(): call(pick_kernel, 'pick', (jax.ShapeDtypeStruct((FEAT_ROWS * devices, LAN...  2.87 us
    pallas_call x1, Pallas kernels, local(): call(project_kernel, 'project', (jax.ShapeDtypeStruct((N_FEAT, N_IMG, OWN...  2.32 us
  transfers between devices with their start and end apart: 1, of which 1 were waited for; matrix products, arithmetic and copies ran while one was open for 1% of the time, Pallas kernels for 3%

profile of v6, /device:TPU:1, one launch (start us, length us, event | category | flops | bytes accessed | tf_op | source)
XLA Modules:
  0.0 87.6 jit_solution(10318179331112112767)
XLA Ops:
  0.6 0.0 copy-start.2
  0.6 0.8 copy-done.2
  1.5 0.7 ask.1
  2.2 15.6 %all-to-all-start = ((s32[256,1,128]{2,1,0:T(1,128)}), s32[256,1,128]{2,1,0:T(1,128)S(1)}, u32[]{:S(2)}, u32[]{:S(2)}) async-start(s32[256,1,128]{2,1,0:T(1,128)} %bitcast.4), calls=%async_computation | async-start | bytes 262144 | tf_op jit(solution)/shard_map/all_to_all | solution.py:586
  17.9 0.0 copy-start.4
  17.9 0.0 copy-start.6
  17.9 2.3 %project.1 = (f32[24,8,2048]{2,1,0:T(8,128)S(1)}, f32[8,128]{1,0:T(8,128)S(1)}) custom-call(f32[3,2048]{1,0:T(4,128)} %refs_0_.1, f32[3,2048]{1,0:T(4,128)} %log_scales.1, f32[1,2048]{1,0:T(1,128)} %quat_w.1, f32[3,2048]{1,0:T(4,128)} %quat_v.1, f32[1,2048]{1,0:T(1,128)} %refs_4_.1, f32[48,2048]{1,0:T(8,128)} %refs_5_.1, f32[8,10]{1,0:T(8,128)} %cam.1), custom_call_target="tpu_custom_call" | custom-call | flops 20000000 | bytes 1000000 | tf_op jit(solution)/shard_map/project/pallas_call | solution.py:608
  20.2 0.7 pad_add_fusion.meta
  20.9 9.8 %all-to-all-done = s32[256,1,128]{2,1,0:T(1,128)S(1)} async-done(((s32[256,1,128]{2,1,0:T(1,128)}), s32[256,1,128]{2,1,0:T(1,128)S(1)}, u32[]{:S(2)}, u32[]{:S(2)}) %all-to-all-start) | async-done | bytes 131104 | tf_op jit(solution)/shard_map/all_to_all | solution.py:586
  30.8 0.0 copy-start
  30.8 0.0 copy-start.1
  30.8 0.0 copy-start.3
  30.8 0.0 copy-start.5
  30.8 2.9 %pick.1 = (f32[768,128]{1,0:T(8,128)S(1)}, s32[8,512]{1,0:T(8,128)S(1)}) custom-call(s32[10]{0:T(128)S(1)} %pad_add_fusion.meta, s32[256,128]{1,0:T(8,128)S(1)} %bitcast.21, f32[24,8,2048]{2,1,0:T(8,128)S(1)} %get-tuple-element.18.feats), custom_call_target="tpu_custom_call" | custom-call | tf_op jit(solution)/shard_map/pick/pallas_call | solution.py:620
  33.7 22.4 %all_to_all.15 = f32[256,1,384]{2,1,0:T(1,128)S(1)} all-to-all(f32[256,1,384]{2,1,0:T(1,128)S(1)} %bitcast.22), channel_id=1, replica_groups=mesh['img'=8,'tile'=32] {'tile','img'}, dimensions={0} | all-to-all | bytes 786432 | tf_op jit(solution)/shard_map/all_to_all | solution.py:586
  56.1 0.0 copy-done.4
  56.1 0.0 copy-done.6
  56.1 6.6 %render.1 = (f32[3,8,256]{2,1,0:T(8,128)S(1)}, f32[512,128]{1,0:T(8,128)S(1)}) custom-call(s32[10]{0:T(128)S(1)} %pad_add_fusion.meta, f32[768,128]{1,0:T(8,128)S(1)} %bitcast.19, s32[8,256]{1,0:T(8,128)S(1)} %bitcast.26, f32[3,8,256]{2,1,0:T(8,128)S(1)} %bitcast.25), custom_call_target="tpu_custom_call" | custom-call | tf_op jit(solution)/shard_map/render/pallas_call | solution.py:632
  62.7 21.3 %all_to_all.16 = f32[256,1,256]{2,1,0:T(1,128)S(1)} all-to-all(f32[256,1,256]{2,1,0:T(1,128)S(1)} %bitcast.23), channel_id=1, replica_groups=mesh['img'=8,'tile'=32] {'tile','img'}, dimensions={0} | all-to-all | bytes 524288 | tf_op jit(solution)/shard_map/all_to_all | solution.py:586
  84.0 0.0 copy-done
  84.0 0.0 copy-done.1
  84.0 0.0 copy-done.3
  84.0 0.0 copy-done.5
  84.0 3.6 %pull.1 = (f32[59,2048]{1,0:T(8,128)}, f32[8,10]{1,0:T(8,128)}, f32[3,8,256]{2,1,0:T(8,128)}) custom-call(s32[10]{0:T(128)S(1)} %pad_add_fusion.meta, f32[512,128]{1,0:T(8,128)S(1)} %bitcast.20, s32[8,512]{1,0:T(8,128)S(1)} %get-tuple-element.21.idx_s, f32[24,8,2048]{2,1,0:T(8,128)S(1)} %get-tuple-element.18.feats, f32[8,128]{1,0:T(8,128)S(1)} %get-tuple-element.22.table, ...), custom_call_target="tpu_custom_call" | custom-call | tf_op jit(solution)/shard_map/pull/pallas_call | solution.py:658
Async XLA Ops:
  0.6 0.8 copy-start.2
  2.2 28.6 %all-to-all-start = ((s32[256,1,128]{2,1,0:T(1,128)}), s32[256,1,128]{2,1,0:T(1,128)S(1)}, u32[]{:S(2)}, u32[]{:S(2)}) async-start(s32[256,1,128]{2,1,0:T(1,128)} %bitcast.4), calls=%async_computation | async-start | bytes 262144 | tf_op jit(solution)/shard_map/all_to_all | solution.py:586
  17.9 38.2 %copy-start.4 = (f32[1,3,8,256]{3,2,1,0:T(8,128)S(1)}, f32[1,3,8,256]{3,2,1,0:T(8,128)}, u32[]{:S(2)}) copy-start(f32[1,3,8,256]{3,2,1,0:T(8,128)} %param.21) | copy-start | bytes 73732
  17.9 38.2 %copy-start.6 = (s32[1,8,256]{2,1,0:T(8,128)S(1)}, s32[1,8,256]{2,1,0:T(8,128)}, u32[]{:S(2)}) copy-start(s32[1,8,256]{2,1,0:T(8,128)} %param.19) | copy-start | bytes 24580
  30.8 53.2 %copy-start = (f32[3,2048]{1,0:T(4,128)S(1)}, f32[3,2048]{1,0:T(4,128)}, u32[]{:S(2)}) copy-start(f32[3,2048]{1,0:T(4,128)} %log_scales.1) | copy-start | bytes 73732
  30.8 53.2 %copy-start.1 = (f32[3,2048]{1,0:T(4,128)S(1)}, f32[3,2048]{1,0:T(4,128)}, u32[]{:S(2)}) copy-start(f32[3,2048]{1,0:T(4,128)} %quat_v.1) | copy-start | bytes 73732
  30.8 53.2 %copy-start.3 = (f32[1,2048]{1,0:T(1,128)S(1)}, f32[1,2048]{1,0:T(1,128)}, u32[]{:S(2)}) copy-start(f32[1,2048]{1,0:T(1,128)} %quat_w.1) | copy-start | bytes 24580
  30.8 53.2 %copy-start.5 = (f32[8,10]{1,0:T(8,128)S(1)}, f32[8,10]{1,0:T(8,128)}, u32[]{:S(2)}) copy-start(f32[8,10]{1,0:T(8,128)} %cam.1) | copy-start | bytes 964

commit v7 on v6

--- a/solution.py
+++ b/solution.py
@@ -243,7 +243,7 @@
             out[pl.ds(FEAT_ROWS * 8 * (8 * q + k) + g, 8, stride=FEAT_ROWS), :] = row
         return carry
 
-    lax.fori_loop(0, 4 * FEAT_ROWS, step, 0, unroll=4)
+    lax.fori_loop(0, 4 * FEAT_ROWS, step, 0, unroll=6)
 
 
 def render_kernel(
@@ -304,7 +304,7 @@
     first_lane, first_chunk = entries(0)
     keep(
         lax.fori_loop(
-            0, 32, lambda ch, c: gather(ch, c, first_lane, first_chunk), tuple([zero] * N_USED), unroll=8
+            0, 32, lambda ch, c: gather(ch, c, first_lane, first_chunk), tuple([zero] * N_USED), unroll=16
         ),
         0,
     )
@@ -473,7 +473,7 @@
 
 
 def pull_kernel(
-    meta, returned, idx_s, feats, table, log_scales, quat_w, quat_v, cam, image, out, cam_out, image_out, row_s, lhs_s, sum_s, gc_s
+    meta, returned, idx_s, feats, table, log_scales, quat_w, quat_v, cam, image, out, cam_out, image_out, row_s, lhs_s, sum_s
 ):
     image_out[...] = image[...]
     group = lax.broadcasted_iota(jnp.int32, (8, LANES), 1) // CAP
@@ -513,6 +513,9 @@
     lax.fori_loop(0, N_IMG, image, 0, unroll=8)
 
     column = [jnp.broadcast_to(cam[:, m : m + 1], (N_IMG, PULL_CHUNK)) for m in range(6)]
+
+    y_h, y_l = [v.astype(f32) for v in halves(jnp.transpose(table[...])[0:16, :])]
+    y_all = jnp.concatenate([y_h, y_h, y_l, y_l], axis=1).astype(bf16)
 
     def chunk(h, carry):
         at = pl.ds(pl.multiple_of(h * PULL_CHUNK, PULL_CHUNK), PULL_CHUNK)
@@ -552,17 +555,12 @@
         base = feats[5, 0:1, at]
         out[10:11, at] = over_images(gr[0]) * (1.0 - base)
         for k in range(3):
-            gc_s[8 * k : 8 * k + 8, at] = gr[6 + k]
+            g_h, g_l = [v.astype(f32) for v in halves(gr[6 + k])]
+            g_all = jnp.concatenate([g_h, g_l, g_h, g_l], axis=0).astype(bf16)
+            out[11 + 16 * k : 27 + 16 * k, at] = dot(y_all, g_all)
         return carry
 
-    lax.fori_loop(0, OWNED // PULL_CHUNK, chunk, 0)
-
-    y_h, y_l = halves(jnp.transpose(table[...])[0:16, :])
-    y_all = jnp.concatenate([y_h.astype(f32), y_h.astype(f32), y_l.astype(f32), y_l.astype(f32)], axis=1).astype(bf16)
-    for k in range(3):
-        g_h, g_l = halves(gc_s[8 * k : 8 * k + 8, :])
-        g_all = jnp.concatenate([g_h.astype(f32), g_l.astype(f32), g_h.astype(f32), g_l.astype(f32)], axis=0).astype(bf16)
-        out[11 + 16 * k : 27 + 16 * k, :] = dot(y_all, g_all)
+    lax.fori_loop(0, OWNED // PULL_CHUNK, chunk, 0, unroll=2)
 
 
 def whole(memory=pltpu.VMEM):
@@ -667,7 +665,6 @@
             pltpu.VMEM((N_GRAD, N_IMG, N_TILE * CAP), f32),
             pltpu.VMEM((16 * N_GRAD, 2 * N_TILE * CAP), bf16),
             pltpu.VMEM((N_IMG * 16 * N_GRAD, LANES), f32),
-            pltpu.VMEM((24, OWNED), f32),
         ],
         10,
         smem=1,

time: 87.9 us -> 87.4 us (level)
  no operation moved by 1% of the time
where the time goes in v7:
time: 87.4 us; the launch traced here: 87.1 us
  blocking collectives  43.7 us (50%)
  Pallas kernels  15.7 us (18%)
  starting transfers between devices  15.6 us (18%)
  waiting for transfers between devices  9.84 us (11%)
    all_to_all x2, blocking collectives, exchange(): return lax.all_to_all(array, ORDER, split_axis=0, concat_axis=0, tiled=True)  43.7 us
    all_to_all x1, starting transfers between devices, exchange(): return lax.all_to_all(array, ORDER, split_axis=0, concat_axis=0, tiled=True)  15.6 us
    all_to_all x1, waiting for transfers between devices, exchange(): return lax.all_to_all(array, ORDER, split_axis=0, concat_axis=0, tiled=True)  9.84 us
    pallas_call x1, Pallas kernels, local(): call(render_kernel, 'render', (jax.ShapeDtypeStruct((3, TILES_HERE, PIX),...  6.46 us
    pallas_call x1, Pallas kernels, local(): call(pull_kernel, 'pull', (jax.ShapeDtypeStruct((59, OWNED), f32), jax.Sh...  3.35 us
    pallas_call x1, Pallas kernels, local(): call(pick_kernel, 'pick', (jax.ShapeDtypeStruct((FEAT_ROWS * devices, LAN...  2.8 us
    pallas_call x1, Pallas kernels, local(): call(project_kernel, 'project', (jax.ShapeDtypeStruct((N_FEAT, N_IMG, OWN...  2.32 us
  transfers between devices with their start and end apart: 1, of which 1 were waited for; matrix products, arithmetic and copies ran while one was open for 1% of the time, Pallas kernels for 3%

profile of v7, /device:TPU:1, one launch (start us, length us, event | category | flops | bytes accessed | tf_op | source)
XLA Modules:
  0.0 87.1 jit_solution(17360330437395843056)
XLA Ops:
  0.6 0.0 copy-start.2
  0.6 0.8 copy-done.2
  1.5 0.7 ask.1
  2.2 15.6 %all-to-all-start = ((s32[256,1,128]{2,1,0:T(1,128)}), s32[256,1,128]{2,1,0:T(1,128)S(1)}, u32[]{:S(2)}, u32[]{:S(2)}) async-start(s32[256,1,128]{2,1,0:T(1,128)} %bitcast.4), calls=%async_computation | async-start | bytes 262144 | tf_op jit(solution)/shard_map/all_to_all | solution.py:584
  17.9 0.0 copy-start.4
  17.9 0.0 copy-start.6
  17.9 2.3 %project.1 = (f32[24,8,2048]{2,1,0:T(8,128)S(1)}, f32[8,128]{1,0:T(8,128)S(1)}) custom-call(f32[3,2048]{1,0:T(4,128)} %refs_0_.1, f32[3,2048]{1,0:T(4,128)} %log_scales.1, f32[1,2048]{1,0:T(1,128)} %quat_w.1, f32[3,2048]{1,0:T(4,128)} %quat_v.1, f32[1,2048]{1,0:T(1,128)} %refs_4_.1, f32[48,2048]{1,0:T(8,128)} %refs_5_.1, f32[8,10]{1,0:T(8,128)} %cam.1), custom_call_target="tpu_custom_call" | custom-call | flops 20000000 | bytes 1000000 | tf_op jit(solution)/shard_map/project/pallas_call | solution.py:606
  20.2 0.7 pad_add_fusion.meta
  20.9 9.8 %all-to-all-done = s32[256,1,128]{2,1,0:T(1,128)S(1)} async-done(((s32[256,1,128]{2,1,0:T(1,128)}), s32[256,1,128]{2,1,0:T(1,128)S(1)}, u32[]{:S(2)}, u32[]{:S(2)}) %all-to-all-start) | async-done | bytes 131104 | tf_op jit(solution)/shard_map/all_to_all | solution.py:584
  30.8 0.0 copy-start
  30.8 0.0 copy-start.1
  30.8 0.0 copy-start.3
  30.8 0.0 copy-start.5
  30.8 2.8 %pick.1 = (f32[768,128]{1,0:T(8,128)S(1)}, s32[8,512]{1,0:T(8,128)S(1)}) custom-call(s32[10]{0:T(128)S(1)} %pad_add_fusion.meta, s32[256,128]{1,0:T(8,128)S(1)} %bitcast.21, f32[24,8,2048]{2,1,0:T(8,128)S(1)} %get-tuple-element.18.feats), custom_call_target="tpu_custom_call" | custom-call | tf_op jit(solution)/shard_map/pick/pallas_call | solution.py:618
  33.6 22.4 %all_to_all.15 = f32[256,1,384]{2,1,0:T(1,128)S(1)} all-to-all(f32[256,1,384]{2,1,0:T(1,128)S(1)} %bitcast.22), channel_id=1, replica_groups=mesh['img'=8,'tile'=32] {'tile','img'}, dimensions={0} | all-to-all | bytes 786432 | tf_op jit(solution)/shard_map/all_to_all | solution.py:584
  56.0 0.0 copy-done.4
  56.0 0.0 copy-done.6
  56.0 6.5 %render.1 = (f32[3,8,256]{2,1,0:T(8,128)S(1)}, f32[512,128]{1,0:T(8,128)S(1)}) custom-call(s32[10]{0:T(128)S(1)} %pad_add_fusion.meta, f32[768,128]{1,0:T(8,128)S(1)} %bitcast.19, s32[8,256]{1,0:T(8,128)S(1)} %bitcast.26, f32[3,8,256]{2,1,0:T(8,128)S(1)} %bitcast.25), custom_call_target="tpu_custom_call" | custom-call | tf_op jit(solution)/shard_map/render/pallas_call | solution.py:630
  62.5 21.3 %all_to_all.16 = f32[256,1,256]{2,1,0:T(1,128)S(1)} all-to-all(f32[256,1,256]{2,1,0:T(1,128)S(1)} %bitcast.23), channel_id=1, replica_groups=mesh['img'=8,'tile'=32] {'tile','img'}, dimensions={0} | all-to-all | bytes 524288 | tf_op jit(solution)/shard_map/all_to_all | solution.py:584
  83.8 0.0 copy-done
  83.8 0.0 copy-done.1
  83.8 0.0 copy-done.3
  83.8 0.0 copy-done.5
  83.8 3.3 %pull.1 = (f32[59,2048]{1,0:T(8,128)}, f32[8,10]{1,0:T(8,128)}, f32[3,8,256]{2,1,0:T(8,128)}) custom-call(s32[10]{0:T(128)S(1)} %pad_add_fusion.meta, f32[512,128]{1,0:T(8,128)S(1)} %bitcast.20, s32[8,512]{1,0:T(8,128)S(1)} %get-tuple-element.21.idx_s, f32[24,8,2048]{2,1,0:T(8,128)S(1)} %get-tuple-element.18.feats, f32[8,128]{1,0:T(8,128)S(1)} %get-tuple-element.22.table, ...), custom_call_target="tpu_custom_call" | custom-call | tf_op jit(solution)/shard_map/pull/pallas_call | solution.py:656
Async XLA Ops:
  0.6 0.8 copy-start.2
  2.2 28.6 %all-to-all-start = ((s32[256,1,128]{2,1,0:T(1,128)}), s32[256,1,128]{2,1,0:T(1,128)S(1)}, u32[]{:S(2)}, u32[]{:S(2)}) async-start(s32[256,1,128]{2,1,0:T(1,128)} %bitcast.4), calls=%async_computation | async-start | bytes 262144 | tf_op jit(solution)/shard_map/all_to_all | solution.py:584
  17.9 38.2 %copy-start.4 = (f32[1,3,8,256]{3,2,1,0:T(8,128)S(1)}, f32[1,3,8,256]{3,2,1,0:T(8,128)}, u32[]{:S(2)}) copy-start(f32[1,3,8,256]{3,2,1,0:T(8,128)} %param.21) | copy-start | bytes 73732
  17.9 38.2 %copy-start.6 = (s32[1,8,256]{2,1,0:T(8,128)S(1)}, s32[1,8,256]{2,1,0:T(8,128)}, u32[]{:S(2)}) copy-start(s32[1,8,256]{2,1,0:T(8,128)} %param.19) | copy-start | bytes 24580
  30.8 53.0 %copy-start = (f32[3,2048]{1,0:T(4,128)S(1)}, f32[3,2048]{1,0:T(4,128)}, u32[]{:S(2)}) copy-start(f32[3,2048]{1,0:T(4,128)} %log_scales.1) | copy-start | bytes 73732
  30.8 53.0 %copy-start.1 = (f32[3,2048]{1,0:T(4,128)S(1)}, f32[3,2048]{1,0:T(4,128)}, u32[]{:S(2)}) copy-start(f32[3,2048]{1,0:T(4,128)} %quat_v.1) | copy-start | bytes 73732
  30.8 53.0 %copy-start.3 = (f32[1,2048]{1,0:T(1,128)S(1)}, f32[1,2048]{1,0:T(1,128)}, u32[]{:S(2)}) copy-start(f32[1,2048]{1,0:T(1,128)} %quat_w.1) | copy-start | bytes 24580
  30.8 53.0 %copy-start.5 = (f32[8,10]{1,0:T(8,128)S(1)}, f32[8,10]{1,0:T(8,128)}, u32[]{:S(2)}) copy-start(f32[8,10]{1,0:T(8,128)} %cam.1) | copy-start | bytes 964

commit v8 on v7

--- a/solution.py
+++ b/solution.py
@@ -594,7 +594,9 @@
 ):
     devices = N_IMG * N_TILE
     by_owner = jnp.transpose(requests.reshape(N_IMG, N_TILE, CAP), (0, 2, 1)).reshape(N_IMG * CAP, N_TILE)
-    wanted = call(ask_kernel, "ask", jax.ShapeDtypeStruct((devices, LANES), jnp.int32), [], 1)(by_owner)
+    wanted = call(ask_kernel, "ask", jax.ShapeDtypeStruct((devices, LANES), jnp.int32), [], 1)(
+        pltpu.with_memory_space_constraint(by_owner, pltpu.HBM)
+    )
     asked = exchange_rows(wanted, 1)
     meta = jnp.concatenate(
         [counts[0], jnp.stack([lax.axis_index("tile"), lax.axis_index("img")]).astype(jnp.int32)]

time: 87.4 us -> 87.4 us (level)
  no operation moved by 1% of the time
where the time goes in v8:
time: 87.4 us; the launch traced here: 87.1 us
  blocking collectives  43.7 us (50%)
  Pallas kernels  16.5 us (19%)
  starting transfers between devices  15.6 us (18%)
  waiting for transfers between devices  9.84 us (11%)
    all_to_all x2, blocking collectives, exchange(): return lax.all_to_all(array, ORDER, split_axis=0, concat_axis=0, tiled=True)  43.7 us
    all_to_all x1, starting transfers between devices, exchange(): return lax.all_to_all(array, ORDER, split_axis=0, concat_axis=0, tiled=True)  15.6 us
    all_to_all x1, waiting for transfers between devices, exchange(): return lax.all_to_all(array, ORDER, split_axis=0, concat_axis=0, tiled=True)  9.84 us
    pallas_call x1, Pallas kernels, local(): call(render_kernel, 'render', (jax.ShapeDtypeStruct((3, TILES_HERE, PIX),...  6.47 us
    pallas_call x1, Pallas kernels, local(): call(pull_kernel, 'pull', (jax.ShapeDtypeStruct((59, OWNED), f32), jax.Sh...  3.34 us
    pallas_call x1, Pallas kernels, local(): call(pick_kernel, 'pick', (jax.ShapeDtypeStruct((FEAT_ROWS * devices, LAN...  2.8 us
    pallas_call x1, Pallas kernels, local(): call(project_kernel, 'project', (jax.ShapeDtypeStruct((N_FEAT, N_IMG, OWN...  2.32 us
  transfers between devices with their start and end apart: 1, of which 1 were waited for; matrix products, arithmetic and copies ran while one was open for 1% of the time, Pallas kernels for 3%

profile of v8, /device:TPU:1, one launch (start us, length us, event | category | flops | bytes accessed | tf_op | source)
XLA Modules:
  0.0 87.1 jit_solution(2721705678878234459)
XLA Ops:
  0.6 1.6 %ask.1 = s32[256,128]{1,0:T(8,128)} custom-call(s32[128,32]{1,0:T(8,128)} %bitcast.26), custom_call_target="tpu_custom_call" | custom-call | tf_op jit(solution)/shard_map/ask/pallas_call | solution.py:597
  2.2 15.6 %all-to-all-start = ((s32[256,1,128]{2,1,0:T(1,128)}), s32[256,1,128]{2,1,0:T(1,128)S(1)}, u32[]{:S(2)}, u32[]{:S(2)}) async-start(s32[256,1,128]{2,1,0:T(1,128)} %bitcast.4), calls=%async_computation | async-start | bytes 262144 | tf_op jit(solution)/shard_map/all_to_all | solution.py:584
  17.9 0.0 copy-start.3
  17.9 0.0 copy-start.5
  17.9 2.3 %project.1 = (f32[24,8,2048]{2,1,0:T(8,128)S(1)}, f32[8,128]{1,0:T(8,128)S(1)}) custom-call(f32[3,2048]{1,0:T(4,128)} %refs_0_.1, f32[3,2048]{1,0:T(4,128)} %log_scales.1, f32[1,2048]{1,0:T(1,128)} %quat_w.1, f32[3,2048]{1,0:T(4,128)} %quat_v.1, f32[1,2048]{1,0:T(1,128)} %refs_4_.1, f32[48,2048]{1,0:T(8,128)} %refs_5_.1, f32[8,10]{1,0:T(8,128)} %cam.1), custom_call_target="tpu_custom_call" | custom-call | flops 20000000 | bytes 1000000 | tf_op jit(solution)/shard_map/project/pallas_call | solution.py:608
  20.2 0.7 pad_add_fusion.meta
  20.9 9.8 %all-to-all-done = s32[256,1,128]{2,1,0:T(1,128)S(1)} async-done(((s32[256,1,128]{2,1,0:T(1,128)}), s32[256,1,128]{2,1,0:T(1,128)S(1)}, u32[]{:S(2)}, u32[]{:S(2)}) %all-to-all-start) | async-done | bytes 131104 | tf_op jit(solution)/shard_map/all_to_all | solution.py:584
  30.8 0.0 copy-start
  30.8 0.0 copy-start.1
  30.8 0.0 copy-start.2
  30.8 0.0 copy-start.4
  30.8 2.8 %pick.1 = (f32[768,128]{1,0:T(8,128)S(1)}, s32[8,512]{1,0:T(8,128)S(1)}) custom-call(s32[10]{0:T(128)S(1)} %pad_add_fusion.meta, s32[256,128]{1,0:T(8,128)S(1)} %bitcast.21, f32[24,8,2048]{2,1,0:T(8,128)S(1)} %get-tuple-element.18.feats), custom_call_target="tpu_custom_call" | custom-call | tf_op jit(solution)/shard_map/pick/pallas_call | solution.py:620
  33.6 22.4 %all_to_all.15 = f32[256,1,384]{2,1,0:T(1,128)S(1)} all-to-all(f32[256,1,384]{2,1,0:T(1,128)S(1)} %bitcast.22), channel_id=1, replica_groups=mesh['img'=8,'tile'=32] {'tile','img'}, dimensions={0} | all-to-all | bytes 786432 | tf_op jit(solution)/shard_map/all_to_all | solution.py:584
  56.0 0.0 copy-done.3
  56.0 0.0 copy-done.5
  56.0 6.5 %render.1 = (f32[3,8,256]{2,1,0:T(8,128)S(1)}, f32[512,128]{1,0:T(8,128)S(1)}) custom-call(s32[10]{0:T(128)S(1)} %pad_add_fusion.meta, f32[768,128]{1,0:T(8,128)S(1)} %bitcast.19, s32[8,256]{1,0:T(8,128)S(1)} %bitcast.25, f32[3,8,256]{2,1,0:T(8,128)S(1)} %bitcast.24), custom_call_target="tpu_custom_call" | custom-call | tf_op jit(solution)/shard_map/render/pallas_call | solution.py:632
  62.5 21.3 %all_to_all.16 = f32[256,1,256]{2,1,0:T(1,128)S(1)} all-to-all(f32[256,1,256]{2,1,0:T(1,128)S(1)} %bitcast.23), channel_id=1, replica_groups=mesh['img'=8,'tile'=32] {'tile','img'}, dimensions={0} | all-to-all | bytes 524288 | tf_op jit(solution)/shard_map/all_to_all | solution.py:584
  83.8 0.0 copy-done
  83.8 0.0 copy-done.1
  83.8 0.0 copy-done.2
  83.8 0.0 copy-done.4
  83.8 3.3 %pull.1 = (f32[59,2048]{1,0:T(8,128)}, f32[8,10]{1,0:T(8,128)}, f32[3,8,256]{2,1,0:T(8,128)}) custom-call(s32[10]{0:T(128)S(1)} %pad_add_fusion.meta, f32[512,128]{1,0:T(8,128)S(1)} %bitcast.20, s32[8,512]{1,0:T(8,128)S(1)} %get-tuple-element.21.idx_s, f32[24,8,2048]{2,1,0:T(8,128)S(1)} %get-tuple-element.18.feats, f32[8,128]{1,0:T(8,128)S(1)} %get-tuple-element.22.table, ...), custom_call_target="tpu_custom_call" | custom-call | tf_op jit(solution)/shard_map/pull/pallas_call | solution.py:658
Async XLA Ops:
  2.2 28.6 %all-to-all-start = ((s32[256,1,128]{2,1,0:T(1,128)}), s32[256,1,128]{2,1,0:T(1,128)S(1)}, u32[]{:S(2)}, u32[]{:S(2)}) async-start(s32[256,1,128]{2,1,0:T(1,128)} %bitcast.4), calls=%async_computation | async-start | bytes 262144 | tf_op jit(solution)/shard_map/all_to_all | solution.py:584
  17.9 38.2 %copy-start.3 = (f32[1,3,8,256]{3,2,1,0:T(8,128)S(1)}, f32[1,3,8,256]{3,2,1,0:T(8,128)}, u32[]{:S(2)}) copy-start(f32[1,3,8,256]{3,2,1,0:T(8,128)} %param.21) | copy-start | bytes 73732
  17.9 38.2 %copy-start.5 = (s32[1,8,256]{2,1,0:T(8,128)S(1)}, s32[1,8,256]{2,1,0:T(8,128)}, u32[]{:S(2)}) copy-start(s32[1,8,256]{2,1,0:T(8,128)} %param.19) | copy-start | bytes 24580
  30.8 53.0 %copy-start = (f32[3,2048]{1,0:T(4,128)S(1)}, f32[3,2048]{1,0:T(4,128)}, u32[]{:S(2)}) copy-start(f32[3,2048]{1,0:T(4,128)} %log_scales.1) | copy-start | bytes 73732
  30.8 53.0 %copy-start.1 = (f32[3,2048]{1,0:T(4,128)S(1)}, f32[3,2048]{1,0:T(4,128)}, u32[]{:S(2)}) copy-start(f32[3,2048]{1,0:T(4,128)} %quat_v.1) | copy-start | bytes 73732
  30.8 53.0 %copy-start.2 = (f32[1,2048]{1,0:T(1,128)S(1)}, f32[1,2048]{1,0:T(1,128)}, u32[]{:S(2)}) copy-start(f32[1,2048]{1,0:T(1,128)} %quat_w.1) | copy-start | bytes 24580
  30.8 53.0 %copy-start.4 = (f32[8,10]{1,0:T(8,128)S(1)}, f32[8,10]{1,0:T(8,128)}, u32[]{:S(2)}) copy-start(f32[8,10]{1,0:T(8,128)} %cam.1) | copy-start | bytes 964
